TPU v7x, 128 devices: a whole 4x4x4 slice. The times are simulated.
128 devices in a mesh: grp: 8 (over x, core), row: 16 (over z, y).
Axes of the slice: x: 4, y: 4, z: 4, core: 2. Of those that a mesh axis runs over, the one named last changes fastest.
Arguments:
- iterate: bfloat16 [64, 1048576], P(None, ('grp', 'row')), may hold values from -6 to 6
- near_tiles: bfloat16 [8192, 128, 128], P(('grp', 'row')), may hold values from -0.125 to 0.125
- near_rows: int32 [8192], P(('grp', 'row')), may hold values from 0 to 63
- near_cols: int32 [8192], P(('grp', 'row')), may hold values from 0 to 63
- near_count: int32 [128], P(('grp', 'row')), may hold values from 32 to 64, as said below
- cross_tiles: bfloat16 [8192, 128, 128], P(('grp', 'row')), may hold values from -0.125 to 0.125
- cross_rows: int32 [8192], P(('grp', 'row')), may hold values from 0 to 63
- cross_cols: int32 [8192], P(('grp', 'row')), may hold values from 0 to 63
- cross_count: int32 [128], P(('grp', 'row')), may hold values from 0 to 64, as said below
Outputs:
- basis: float32 [64, 1048576], P(None, ('grp', 'row'))
- rayleigh: float32 [64, 64], replicated
Inputs may be any that keep to these rules, and one draw needn't show every extreme that they name: `near_count`: slots at or past a device's count hold no part of the matrix. Some device uses all 64 near slots. `cross_count`: the last device's count is 0; some other device uses all 64 cross slots. `near_rows`: positions may repeat; repeated tiles add.
All inputs are finite; a program needn't handle non-finite values.
Results may differ from a plain program's by a relative error of at most 0.003.
Values may be sent and summed in bfloat16 or wider, within the bound.
No kernel may reach another device: no remote copies, remote signals or barrier semaphores. Data moves between devices by JAX's collectives and lax.ppermute only.
A program may use at most 128 MiB of HBM per device.

v0:
```python
import jax
import jax.numpy as jnp
from jax import lax
from jax.sharding import Mesh
from jax.sharding import PartitionSpec as P

EIGS = 64
TILE = 128
BR_DEV = 64
GRP_ROW = ("grp_0", "grp_1", "row_0", "row_1")


def from_behind(array, axis, by):
    devices = lax.axis_size(axis)
    pairs = [(i, i + by) for i in range(devices) if 0 <= i + by < devices]
    return lax.ppermute(array, axis, pairs)


def extended(array, sides, width):
    edges = {}
    for axis, dim in sides:
        devices, length = (lax.axis_size(axis), array.shape[dim])
        up = [(i, (i + 1) % devices) for i in range(devices - 1)]
        last = lax.slice_in_dim(array, length - width, length, axis=dim)
        leading = lax.slice_in_dim(array, 0, width, axis=dim)
        edges[dim] = (
            lax.ppermute(last, axis, up),
            lax.ppermute(leading, axis, [(b, a) for a, b in up]),
        )
    done = []
    for _, dim in sides:
        low, high = edges[dim]
        around = [(width, width) if d in done else (0, 0) for d in range(array.ndim)]
        array = jnp.concatenate([jnp.pad(low, around), array, jnp.pad(high, around)], axis=dim)
        done.append(dim)
    return array


def over_axes(array, axes):
    for axis in axes:
        array = lax.psum(array, axis)
    return array


def tile_terms(blocks, index, tiles, flipped):
    picked = jnp.take(blocks, index, axis=1)
    if flipped:
        return jnp.einsum("ktr,trc->tkc", picked, tiles, preferred_element_type=jnp.float32)
    return jnp.einsum("ktc,trc->tkr", picked, tiles, preferred_element_type=jnp.float32)


def place(terms, index, weight):
    selector = jax.nn.one_hot(index, BR_DEV, dtype=jnp.float32) * weight[:, None]
    placed = jnp.einsum(
        "ts,tkc->ksc",
        selector,
        terms,
        precision=lax.Precision.HIGHEST,
        preferred_element_type=jnp.float32,
    )
    return placed.reshape(EIGS, BR_DEV * TILE)


def shards(
    iterate,
    near_tiles,
    near_rows,
    near_cols,
    near_count,
    cross_tiles,
    cross_rows,
    cross_cols,
    cross_count,
):
    width = BR_DEV * TILE
    near_mask = (jnp.arange(near_tiles.shape[0], dtype=jnp.int32) < near_count[0]).astype(
        jnp.float32
    )
    cross_mask = (jnp.arange(cross_tiles.shape[0], dtype=jnp.int32) < cross_count[0]).astype(
        jnp.float32
    )
    lent_tiles, lent_rows, lent_cols, lent_count = from_behind(
        (cross_tiles, cross_rows, cross_cols, cross_count), GRP_ROW, 1
    )
    lent_mask = (jnp.arange(lent_tiles.shape[0], dtype=jnp.int32) < lent_count[0]).astype(
        jnp.float32
    )

    def apply_s(vector_b):
        blocks = vector_b.reshape(EIGS, BR_DEV, TILE)
        padded = extended(vector_b, ((GRP_ROW, 1),), width)
        behind = padded[:, :width].reshape(EIGS, BR_DEV, TILE)
        ahead = padded[:, 2 * width :].reshape(EIGS, BR_DEV, TILE)
        total = place(tile_terms(blocks, near_cols, near_tiles, False), near_rows, near_mask)
        total = total + place(tile_terms(blocks, near_rows, near_tiles, True), near_cols, near_mask)
        total = total + place(
            tile_terms(ahead, cross_cols, cross_tiles, False), cross_rows, cross_mask
        )
        total = total + place(tile_terms(behind, lent_rows, lent_tiles, True), lent_cols, lent_mask)
        return total

    def mapped(current):
        return (-0.25 * current - apply_s(current.astype(jnp.bfloat16))) / 0.75

    before = iterate.astype(jnp.float32)
    current = mapped(before)
    for step in range(3):
        following = 2.0 * mapped(current) - before
        before, current = (current, following)
    rounded = current.astype(jnp.bfloat16)
    rounded_f = rounded.astype(jnp.float32)
    count_rows = float(width * lax.axis_size(GRP_ROW))
    local_gram = jnp.dot(
        current, current.T, precision=lax.Precision.HIGHEST, preferred_element_type=jnp.float32
    )
    image = rounded_f - apply_s(rounded)
    local_proj = jnp.dot(
        rounded_f, image.T, precision=lax.Precision.HIGHEST, preferred_element_type=jnp.float32
    )
    gram, projected = (over_axes(local_gram, GRP_ROW), over_axes(local_proj, GRP_ROW))
    lower = jnp.linalg.cholesky(gram / count_rows)
    basis = jax.scipy.linalg.solve_triangular(lower, current, lower=True)
    halfway = jax.scipy.linalg.solve_triangular(lower, projected / count_rows, lower=True)
    rayleigh = jax.scipy.linalg.solve_triangular(lower, halfway.T, lower=True)
    return (basis, rayleigh)


def solution(mesh):
    finer = Mesh(mesh.devices.reshape(4, 2, 4, 4), ("grp_0", "grp_1", "row_0", "row_1"))
    in_specs = (
        P(None, GRP_ROW),
        P(GRP_ROW, None, None),
        P(GRP_ROW),
        P(GRP_ROW),
        P(GRP_ROW),
        P(GRP_ROW, None, None),
        P(GRP_ROW),
        P(GRP_ROW),
        P(GRP_ROW),
    )
    out_specs = (P(None, GRP_ROW), P())
    return jax.shard_map(
        shards, mesh=finer, in_specs=in_specs, out_specs=out_specs, check_vma=False
    )
```

profile of v0, /device:TPU:0, one launch (start us, length us, event | category | flops | bytes accessed | tf_op | source)
XLA Modules:
  0.0 438.3 jit_solution(2132862414698501512)
XLA Ops:
  2.1 5.6 %collective-permute-start.1 = (bf16[64,8192]{1,0:T(8,128)(2,1)}, bf16[64,8192]{1,0:T(8,128)(2,1)}, u32[]{:S(2)}, u32[]{:S(2)}) collective-permute-start(bf16[64,8192]{1,0:T(8,128)(2,1)} %param.13), channel_id=1, source_target_pairs={{0,1},{1,2},{2,3},{3,4},{4,5},{5,6},{6,7},{7,8},{8,9},{9,10},{10,1... | collective-permute-start | bytes 3145736 | tf_op jit(solution)/shard_map/ppermute | solution.py:27
  14.3 4.7 %collective-permute-start.4 = (s32[64]{0:T(128)}, s32[64]{0:T(128)S(1)}, u32[]{:S(2)}, u32[]{:S(2)}) collective-permute-start(s32[64]{0:T(128)} %param.20), channel_id=1, source_target_pairs={{0,1},{1,2},{2,3},{3,4},{4,5},{5,6},{6,7},{7,8},{8,9},{9,10},{10,1... | collective-permute-start | bytes 776 | tf_op jit(solution)/shard_map/ppermute | solution.py:16
  34.2 4.6 %fusion.44 = f32[64,128,64]{1,2,0:T(8,128)} fusion(f32[64,64,128]{2,1,0:T(8,128)S(1)} %fusion.95, s32[64]{0:T(128)S(1)} %copy-done.29, f32[64]{0:T(128)S(1)} %compare_convert_fusion.2), kind=kOutput, calls=%fused_computation.70 | convolution fusion | flops 402661376 | bytes 4194816 | tf_op jit(solution)/shard_map/ts,tkc->ksc/dot_general | solution.py:54
  38.8 32.6 %collective-permute-done.5 = s32[1]{0:T(128)} collective-permute-done((s32[1]{0:T(128)}, s32[1]{0:T(128)}, u32[]{:S(2)}, u32[]{:S(2)}) %collective-permute-start.5) | collective-permute-done | bytes 36 | tf_op jit(solution)/shard_map/ppermute | solution.py:16
  71.4 6.4 %collective-permute-start.2 = (s32[64]{0:T(128)S(1)}, s32[64]{0:T(128)S(1)}, u32[]{:S(2)}, u32[]{:S(2)}) collective-permute-start(s32[64]{0:T(128)S(1)} %copy-done.30), channel_id=1, source_target_pairs={{0,1},{1,2},{2,3},{3,4},{4,5},{5,6},{6,7},{7,8},{8,9},{9,10},{10,1... | collective-permute-start | bytes 776 | tf_op jit(solution)/shard_map/ppermute | solution.py:16
  111.0 6.4 %collective-permute-start.7 = (bf16[64,8192]{1,0:T(8,128)(2,1)}, bf16[64,8192]{1,0:T(8,128)(2,1)}, u32[]{:S(2)}, u32[]{:S(2)}) collective-permute-start(bf16[64,8192]{1,0:T(8,128)(2,1)} %multiply_convert_fusion), channel_id=1, source_target_pairs={{0,1},{1,2},{2,3},{3,4},{4,5},{5,6},{6,7},{7,8},{8,9},{9,10},{10,1... | collective-permute-start | bytes 3145736 | tf_op jit(solution)/shard_map/ppermute | solution.py:27
  125.6 4.7 %fusion.36 = f32[64,128,64]{1,2,0:T(8,128)} fusion(f32[64,64,128]{2,1,0:T(8,128)S(1)} %fusion.87, s32[64]{0:T(128)S(1)} %copy-done.29, f32[64]{0:T(128)S(1)} %compare_convert_fusion.2), kind=kOutput, calls=%fused_computation.62 | convolution fusion | flops 402661376 | bytes 4194816 | tf_op jit(solution)/shard_map/ts,tkc->ksc/dot_general | solution.py:54
  139.2 4.9 %fusion.34 = f32[64,128,64]{1,2,0:T(8,128)} fusion(f32[64,64,128]{2,1,0:T(8,128)S(1)} %fusion.85, f32[64]{0:T(128)S(1)} %compare_convert_fusion.1, s32[64]{0:T(128)S(1)} %copy-done.30), kind=kOutput, calls=%fused_computation.60 | convolution fusion | flops 402661376 | bytes 4194816 | tf_op jit(solution)/shard_map/ts,tkc->ksc/dot_general | solution.py:54
  152.7 5.5 %add_add_fusion.3 = f32[64,128,64]{1,2,0:T(8,128)S(1)} fusion(f32[64,128,64]{1,2,0:T(8,128)} %fusion.34, f32[64,128,64]{1,2,0:T(8,128)S(1)} %copy-done.16, f32[64,128,64]{1,2,0:T(8,128)S(1)} %copy-done.19, f32[64,64,128]{2,1,0:T(8,128)S(1)} %fusion.83, f32[64]{0:T(128)S(1)} %compare_convert_fusion, s32[64]{0:T(128)S(1)} %collective-permute-done.4), kind=kOutput, calls=%fused_computation.78 | convolution fusion | flops 404234240 | bytes 10486272 | tf_op jit(solution)/shard_map/ts,tkc->ksc/dot_general | solution.py:54
  172.4 5.7 %collective-permute-start.9 = (bf16[64,8192]{1,0:T(8,128)(2,1)}, bf16[64,8192]{1,0:T(8,128)(2,1)}, u32[]{:S(2)}, u32[]{:S(2)}) collective-permute-start(bf16[64,8192]{1,0:T(8,128)(2,1)} %fusion.310), channel_id=1, source_target_pairs={{0,1},{1,2},{2,3},{3,4},{4,5},{5,6},{6,7},{7,8},{8,9},{9,10},{10,1... | collective-permute-start | bytes 3145736 | tf_op jit(solution)/shard_map/ppermute | solution.py:27
  180.9 4.7 %fusion.30 = f32[64,128,64]{1,2,0:T(8,128)} fusion(f32[64,64,128]{2,1,0:T(8,128)S(1)} %fusion.81, f32[64]{0:T(128)S(1)} %compare_convert_fusion.2, s32[64]{0:T(128)S(1)} %copy-done.28), kind=kOutput, calls=%fused_computation.56 | convolution fusion | flops 402661376 | bytes 4194816 | tf_op jit(solution)/shard_map/ts,tkc->ksc/dot_general | solution.py:54
  186.3 4.7 %fusion.28 = f32[64,128,64]{1,2,0:T(8,128)} fusion(f32[64,64,128]{2,1,0:T(8,128)S(1)} %fusion.79, s32[64]{0:T(128)S(1)} %copy-done.29, f32[64]{0:T(128)S(1)} %compare_convert_fusion.2), kind=kOutput, calls=%fused_computation.54 | convolution fusion | flops 402661376 | bytes 4194816 | tf_op jit(solution)/shard_map/ts,tkc->ksc/dot_general | solution.py:54
  200.0 5.1 %fusion.26 = f32[64,128,64]{1,2,0:T(8,128)} fusion(f32[64,64,128]{2,1,0:T(8,128)S(1)} %fusion.77, f32[64]{0:T(128)S(1)} %compare_convert_fusion.1, s32[64]{0:T(128)S(1)} %copy-done.30), kind=kOutput, calls=%fused_computation.52 | convolution fusion | flops 402661376 | bytes 4194816 | tf_op jit(solution)/shard_map/ts,tkc->ksc/dot_general | solution.py:54
  213.7 5.5 %add_add_fusion.2 = f32[64,128,64]{1,2,0:T(8,128)S(1)} fusion(f32[64,128,64]{1,2,0:T(8,128)} %fusion.26, f32[64,128,64]{1,2,0:T(8,128)S(1)} %copy-done.17, f32[64,128,64]{1,2,0:T(8,128)S(1)} %copy-done.20, f32[64,64,128]{2,1,0:T(8,128)S(1)} %fusion.75, f32[64]{0:T(128)S(1)} %compare_convert_fusion, s32[64]{0:T(128)S(1)} %collective-permute-done.4), kind=kOutput, calls=%fused_computation.77 | convolution fusion | flops 404234240 | bytes 10486272 | tf_op jit(solution)/shard_map/ts,tkc->ksc/dot_general | solution.py:54
  219.2 6.0 %fusion.309 = bf16[64,8192]{1,0:T(8,128)(2,1)} fusion(f32[8,8,64,128]{3,2,1,0:T(8,128)S(1)} %bitcast.309, bf16[64,8192]{1,0:T(8,128)(2,1)S(1)} %copy-done.9, f32[8,8,64,128]{3,2,1,0:T(8,128)S(1)} %bitcast.314, f32[8,8,64,128]{3,2,1,0:T(8,128)S(1)} %bitcast.312), kind=kLoop, calls=%fused_computation.373 | loop fusion | flops 6815744 | bytes 8388608 | tf_op jit(solution)/shard_map/convert_element_type | solution.py:103
  234.9 7.1 %collective-permute-start.11 = (bf16[64,8192]{1,0:T(8,128)(2,1)}, bf16[64,8192]{1,0:T(8,128)(2,1)}, u32[]{:S(2)}, u32[]{:S(2)}) collective-permute-start(bf16[64,8192]{1,0:T(8,128)(2,1)} %fusion.309), channel_id=1, source_target_pairs={{0,1},{1,2},{2,3},{3,4},{4,5},{5,6},{6,7},{7,8},{8,9},{9,10},{10,1... | collective-permute-start | bytes 3145736 | tf_op jit(solution)/shard_map/ppermute | solution.py:27
  244.7 4.7 %fusion.22 = f32[64,128,64]{1,2,0:T(8,128)} fusion(f32[64,64,128]{2,1,0:T(8,128)S(1)} %fusion.73, f32[64]{0:T(128)S(1)} %compare_convert_fusion.2, s32[64]{0:T(128)S(1)} %copy-done.28), kind=kOutput, calls=%fused_computation.48 | convolution fusion | flops 402661376 | bytes 4194816 | tf_op jit(solution)/shard_map/ts,tkc->ksc/dot_general | solution.py:54
  250.2 4.7 %fusion.20 = f32[64,128,64]{1,2,0:T(8,128)} fusion(f32[64,64,128]{2,1,0:T(8,128)S(1)} %fusion.71, s32[64]{0:T(128)S(1)} %copy-done.29, f32[64]{0:T(128)S(1)} %compare_convert_fusion.2), kind=kOutput, calls=%fused_computation.46 | convolution fusion | flops 402661376 | bytes 4194816 | tf_op jit(solution)/shard_map/ts,tkc->ksc/dot_general | solution.py:54
  263.8 5.1 %fusion.18 = f32[64,128,64]{1,2,0:T(8,128)} fusion(f32[64,64,128]{2,1,0:T(8,128)S(1)} %fusion.69, f32[64]{0:T(128)S(1)} %compare_convert_fusion.1, s32[64]{0:T(128)S(1)} %copy-done.30), kind=kOutput, calls=%fused_computation.44 | convolution fusion | flops 402661376 | bytes 4194816 | tf_op jit(solution)/shard_map/ts,tkc->ksc/dot_general | solution.py:54
  277.4 5.5 %add_add_fusion.1 = f32[64,128,64]{1,2,0:T(8,128)S(1)} fusion(f32[64,128,64]{1,2,0:T(8,128)} %fusion.18, f32[64,128,64]{1,2,0:T(8,128)S(1)} %copy-done.18, f32[64,128,64]{1,2,0:T(8,128)S(1)} %copy-done.21, f32[64,64,128]{2,1,0:T(8,128)S(1)} %fusion.67, f32[64]{0:T(128)S(1)} %compare_convert_fusion, s32[64]{0:T(128)S(1)} %collective-permute-done.4), kind=kOutput, calls=%fused_computation.76 | convolution fusion | flops 404234240 | bytes 10486272 | tf_op jit(solution)/shard_map/ts,tkc->ksc/dot_general | solution.py:54
  283.0 10.0 %fusion.311 = (bf16[64,8192]{1,0:T(8,128)(2,1)}, f32[64,8192]{1,0:T(8,128)}) fusion(f32[8,8,64,128]{3,2,1,0:T(8,128)S(1)} %bitcast.317, f32[8,8,64,128]{3,2,1,0:T(8,128)S(1)} %bitcast.315, f32[8,8,64,128]{3,2,1,0:T(8,128)S(1)} %bitcast.313, f32[8,8,64,128]{3,2,1,0:T(8,128)S(1)} %bitcast.310, bf16[64,8192]{1,0:T(8,128)(2,1)S(1)} %copy-done.9), kind=kLoop, calls=%fused_computation.375 | loop fusion | flops 8912896 | bytes 12582912 | tf_op jit(solution)/shard_map/convert_element_type | solution.py:110
  299.1 6.7 %collective-permute-start.13 = (bf16[64,8192]{1,0:T(8,128)(2,1)}, bf16[64,8192]{1,0:T(8,128)(2,1)}, u32[]{:S(2)}, u32[]{:S(2)}) collective-permute-start(bf16[64,8192]{1,0:T(8,128)(2,1)} %get-tuple-element.12), channel_id=1, source_target_pairs={{0,1},{1,2},{2,3},{3,4},{4,5},{5,6},{6,7},{7,8},{8,9},{9,10},{10,1... | collective-permute-start | bytes 3145736 | tf_op jit(solution)/shard_map/ppermute | solution.py:27
  308.5 4.7 %fusion.14 = f32[64,128,64]{1,2,0:T(8,128)} fusion(f32[64,64,128]{2,1,0:T(8,128)S(1)} %fusion.65, f32[64]{0:T(128)S(1)} %compare_convert_fusion.2, s32[64]{0:T(128)S(1)} %copy-done.28), kind=kOutput, calls=%fused_computation.40 | convolution fusion | flops 402661376 | bytes 4194816 | tf_op jit(solution)/shard_map/ts,tkc->ksc/dot_general | solution.py:54
  315.8 4.7 %fusion.12 = f32[64,128,64]{1,2,0:T(8,128)} fusion(f32[64,64,128]{2,1,0:T(8,128)S(1)} %fusion.63, s32[64]{0:T(128)S(1)} %copy-done.29, f32[64]{0:T(128)S(1)} %compare_convert_fusion.2), kind=kOutput, calls=%fused_computation.38 | convolution fusion | flops 402661376 | bytes 4194816 | tf_op jit(solution)/shard_map/ts,tkc->ksc/dot_general | solution.py:54
  327.1 4.8 %fusion.10 = f32[64,128,64]{1,2,0:T(8,128)} fusion(f32[64,64,128]{2,1,0:T(8,128)S(1)} %fusion.61, f32[64]{0:T(128)S(1)} %compare_convert_fusion.1, s32[64]{0:T(128)S(1)} %copy-done.30), kind=kOutput, calls=%fused_computation.36 | convolution fusion | flops 402661376 | bytes 4194816 | tf_op jit(solution)/shard_map/ts,tkc->ksc/dot_general | solution.py:54
  338.4 5.4 %add_add_fusion = f32[64,128,64]{1,2,0:T(8,128)S(1)} fusion(f32[64,128,64]{1,2,0:T(8,128)} %fusion.10, f32[64,128,64]{1,2,0:T(8,128)S(1)} %copy-done.14, f32[64,128,64]{1,2,0:T(8,128)S(1)} %copy-done.15, f32[64,64,128]{2,1,0:T(8,128)S(1)} %fusion.59, f32[64]{0:T(128)S(1)} %compare_convert_fusion, s32[64]{0:T(128)S(1)} %collective-permute-done.4), kind=kOutput, calls=%fused_computation.74 | convolution fusion | flops 404234240 | bytes 10486272 | tf_op jit(solution)/shard_map/ts,tkc->ksc/dot_general | solution.py:54
  347.8 30.2 %all-reduce.2 = (f32[64,64]{0,1:T(8,128)S(1)}, f32[64,64]{0,1:T(8,128)S(1)}) all-reduce(f32[64,64]{0,1:T(8,128)S(1)} %fusion.313, f32[64,64]{0,1:T(8,128)S(1)} %fusion.1), channel_id=1, replica_groups=mesh['grp_0'=4,'grp_1'=2,'row_0'=4,'row_1'=4] {'grp_0'}, use_global_device_ids=true, to_apply=%region_0.2 | all-reduce | flops 8192 | bytes 65536 | tf_op jit(solution)/shard_map/psum | solution.py:41
  381.6 14.9 %all-reduce.1 = (f32[64,64]{0,1:T(8,128)S(1)}, f32[64,64]{0,1:T(8,128)S(1)}) all-reduce(f32[64,64]{0,1:T(8,128)S(1)} %get-tuple-element.10, f32[64,64]{0,1:T(8,128)S(1)} %get-tuple-element.11), channel_id=1, replica_groups=mesh['grp_0'=4,'grp_1'=2,'row_0'=4,'row_1'=4] {'row_0'}, use_global_device_ids=true, to_apply=%region_2.4 | all-reduce | flops 8192 | bytes 65536 | tf_op jit(solution)/shard_map/psum | solution.py:41
  396.5 23.3 %all-reduce = (f32[64,64]{0,1:T(8,128)S(1)}, f32[64,64]{0,1:T(8,128)S(1)}) all-reduce(f32[64,64]{0,1:T(8,128)S(1)} %get-tuple-element.6, f32[64,64]{0,1:T(8,128)S(1)} %get-tuple-element.7), channel_id=1, replica_groups=mesh['grp_0'=4,'grp_1'=2,'row_0'=4,'row_1'=4] {'row_1'}, use_global_device_ids=true, to_apply=%region_3.5 | all-reduce | flops 8192 | bytes 65536 | tf_op jit(solution)/shard_map/psum | solution.py:41
  419.9 5.8 %cholesky.15 = f32[64,64]{1,0:T(8,128)S(1)} custom-call(f32[64,64]{1,0:T(8,128)S(1)} %fusion.165), custom_call_target="Cholesky" | custom-call | tf_op jit(solution)/shard_map/jit(cholesky)/cholesky | solution.py:121
  427.1 4.9 %custom-call.10 = f32[1,64,64]{1,2,0:T(8,128)S(1)} custom-call(f32[1,64,64]{2,1,0:T(8,128)S(1)} %fusion.159), custom_call_target="InvertDiagBlocksLowerTriangular" | custom-call | tf_op jit(solution)/shard_map/jit(_solve_triangular)/triangular_solve | solution.py:122
  432.0 4.8 %fusion.163 = f32[64,8192]{1,0:T(8,128)} fusion(f32[64,8192]{1,0:T(8,128)} %get-tuple-element.13, f32[1,64,64]{1,2,0:T(8,128)S(1)} %custom-call.10), kind=kOutput, calls=%fused_computation.202 | convolution fusion | flops 402653184 | bytes 4210688 | tf_op jit(solution)/shard_map/jit(_solve_triangular)/triangular_solve | solution.py:122
  (171 shorter events, 180.6 us)
Async XLA Ops:
  0.6 25.4 %copy-start = (bf16[64,128,128]{2,1,0:T(8,128)(2,1)S(1)}, bf16[64,128,128]{2,1,0:T(8,128)(2,1)}, u32[]{:S(2)}) copy-start(bf16[64,128,128]{2,1,0:T(8,128)(2,1)} %param.14) | copy-start | bytes 6291460
  0.6 21.3 %copy-start.29 = (s32[64]{0:T(128)S(1)}, s32[64]{0:T(128)}, u32[]{:S(2)}) copy-start(s32[64]{0:T(128)} %param.16) | copy-start | bytes 772
  0.7 21.3 %copy-start.28 = (s32[64]{0:T(128)S(1)}, s32[64]{0:T(128)}, u32[]{:S(2)}) copy-start(s32[64]{0:T(128)} %param.15) | copy-start | bytes 772
  0.7 78.3 %collective-permute-start = (bf16[64,8192]{1,0:T(8,128)(2,1)}, bf16[64,8192]{1,0:T(8,128)(2,1)}, u32[]{:S(2)}, u32[]{:S(2)}) collective-permute-start(bf16[64,8192]{1,0:T(8,128)(2,1)} %param.13), channel_id=1, source_target_pairs={{1,0},{2,1},{3,2},{4,3},{5,4},{6,5},{7,6},{8,7},{9,8},{10,9},{11,1... | collective-permute-start | bytes 3145736 | tf_op jit(solution)/shard_map/ppermute | solution.py:28
  2.1 80.1 %collective-permute-start.1 = (bf16[64,8192]{1,0:T(8,128)(2,1)}, bf16[64,8192]{1,0:T(8,128)(2,1)}, u32[]{:S(2)}, u32[]{:S(2)}) collective-permute-start(bf16[64,8192]{1,0:T(8,128)(2,1)} %param.13), channel_id=1, source_target_pairs={{0,1},{1,2},{2,3},{3,4},{4,5},{5,6},{6,7},{7,8},{8,9},{9,10},{10,1... | collective-permute-start | bytes 3145736 | tf_op jit(solution)/shard_map/ppermute | solution.py:27
  7.7 84.5 %collective-permute-start.3 = (bf16[64,128,128]{2,1,0:T(8,128)(2,1)}, bf16[64,128,128]{2,1,0:T(8,128)(2,1)}, u32[]{:S(2)}, u32[]{:S(2)}) collective-permute-start(bf16[64,128,128]{2,1,0:T(8,128)(2,1)} %param.18), channel_id=1, source_target_pairs={{0,1},{1,2},{2,3},{3,4},{4,5},{5,6},{6,7},{7,8},{8,9},{9,10},{10,1... | collective-permute-start | bytes 6291464 | tf_op jit(solution)/shard_map/ppermute | solution.py:16
  11.6 59.8 %collective-permute-start.5 = (s32[1]{0:T(128)}, s32[1]{0:T(128)}, u32[]{:S(2)}, u32[]{:S(2)}) collective-permute-start(s32[1]{0:T(128)} %param.21), channel_id=1, source_target_pairs={{0,1},{1,2},{2,3},{3,4},{4,5},{5,6},{6,7},{7,8},{8,9},{9,10},{10,1... | collective-permute-start | bytes 20 | tf_op jit(solution)/shard_map/ppermute | solution.py:16
  14.3 80.4 %collective-permute-start.4 = (s32[64]{0:T(128)}, s32[64]{0:T(128)S(1)}, u32[]{:S(2)}, u32[]{:S(2)}) collective-permute-start(s32[64]{0:T(128)} %param.20), channel_id=1, source_target_pairs={{0,1},{1,2},{2,3},{3,4},{4,5},{5,6},{6,7},{7,8},{8,9},{9,10},{10,1... | collective-permute-start | bytes 776 | tf_op jit(solution)/shard_map/ppermute | solution.py:16
  28.8 4.7 %copy-start.27 = (bf16[64,64,128]{2,1,0:T(8,128)(2,1)S(1)}, bf16[64,64,128]{2,1,0:T(8,128)(2,1)}, u32[]{:S(2)}) copy-start(bf16[64,64,128]{2,1,0:T(8,128)(2,1)} %gather_fusion.1) | copy-start | bytes 3145732
  34.1 4.7 %copy-start.31 = (s32[64]{0:T(128)S(1)}, s32[64]{0:T(128)}, u32[]{:S(2)}) copy-start(s32[64]{0:T(128)} %param.20) | copy-start | bytes 772
  34.2 37.3 %copy-start.30 = (s32[64]{0:T(128)S(1)}, s32[64]{0:T(128)}, u32[]{:S(2)}) copy-start(s32[64]{0:T(128)} %param.19) | copy-start | bytes 772
  71.4 7.5 %collective-permute-start.2 = (s32[64]{0:T(128)S(1)}, s32[64]{0:T(128)S(1)}, u32[]{:S(2)}, u32[]{:S(2)}) collective-permute-start(s32[64]{0:T(128)S(1)} %copy-done.30), channel_id=1, source_target_pairs={{0,1},{1,2},{2,3},{3,4},{4,5},{5,6},{6,7},{7,8},{8,9},{9,10},{10,1... | collective-permute-start | bytes 776 | tf_op jit(solution)/shard_map/ppermute | solution.py:16
  101.3 28.9 %collective-permute-start.6 = (bf16[64,8192]{1,0:T(8,128)(2,1)}, bf16[64,8192]{1,0:T(8,128)(2,1)}, u32[]{:S(2)}, u32[]{:S(2)}) collective-permute-start(bf16[64,8192]{1,0:T(8,128)(2,1)} %multiply_convert_fusion), channel_id=1, source_target_pairs={{1,0},{2,1},{3,2},{4,3},{5,4},{6,5},{7,6},{8,7},{9,8},{10,9},{11,1... | collective-permute-start | bytes 3145736 | tf_op jit(solution)/shard_map/ppermute | solution.py:28
  111.0 33.1 %collective-permute-start.7 = (bf16[64,8192]{1,0:T(8,128)(2,1)}, bf16[64,8192]{1,0:T(8,128)(2,1)}, u32[]{:S(2)}, u32[]{:S(2)}) collective-permute-start(bf16[64,8192]{1,0:T(8,128)(2,1)} %multiply_convert_fusion), channel_id=1, source_target_pairs={{0,1},{1,2},{2,3},{3,4},{4,5},{5,6},{6,7},{7,8},{8,9},{9,10},{10,1... | collective-permute-start | bytes 3145736 | tf_op jit(solution)/shard_map/ppermute | solution.py:27
  120.2 4.7 %copy-start.23 = (bf16[64,64,128]{2,1,0:T(8,128)(2,1)S(1)}, bf16[64,64,128]{2,1,0:T(8,128)(2,1)}, u32[]{:S(2)}) copy-start(bf16[64,64,128]{2,1,0:T(8,128)(2,1)} %gather_fusion.5) | copy-start | bytes 3145732
  152.7 5.6 %copy-start.2 = (f32[64,128,64]{1,2,0:T(8,128)S(1)}, f32[64,128,64]{1,2,0:T(8,128)}, u32[]{:S(2)}) copy-start(f32[64,128,64]{1,2,0:T(8,128)} %copy-done.1) | copy-start | bytes 6291460
  158.3 4.4 %copy-start.6 = (f32[64,128,64]{1,2,0:T(8,128)}, f32[64,128,64]{1,2,0:T(8,128)S(1)}, u32[]{:S(2)}) copy-start(f32[64,128,64]{1,2,0:T(8,128)S(1)} %add_add_fusion.3) | copy-start | bytes 6291460
  162.7 28.4 %collective-permute-start.8 = (bf16[64,8192]{1,0:T(8,128)(2,1)}, bf16[64,8192]{1,0:T(8,128)(2,1)}, u32[]{:S(2)}, u32[]{:S(2)}) collective-permute-start(bf16[64,8192]{1,0:T(8,128)(2,1)} %fusion.310), channel_id=1, source_target_pairs={{1,0},{2,1},{3,2},{4,3},{5,4},{6,5},{7,6},{8,7},{9,8},{10,9},{11,1... | collective-permute-start | bytes 3145736 | tf_op jit(solution)/shard_map/ppermute | solution.py:28
  172.4 32.7 %collective-permute-start.9 = (bf16[64,8192]{1,0:T(8,128)(2,1)}, bf16[64,8192]{1,0:T(8,128)(2,1)}, u32[]{:S(2)}, u32[]{:S(2)}) collective-permute-start(bf16[64,8192]{1,0:T(8,128)(2,1)} %fusion.310), channel_id=1, source_target_pairs={{0,1},{1,2},{2,3},{3,4},{4,5},{5,6},{6,7},{7,8},{8,9},{9,10},{10,1... | collective-permute-start | bytes 3145736 | tf_op jit(solution)/shard_map/ppermute | solution.py:27
  180.9 4.7 %copy-start.24 = (bf16[64,64,128]{2,1,0:T(8,128)(2,1)S(1)}, bf16[64,64,128]{2,1,0:T(8,128)(2,1)}, u32[]{:S(2)}) copy-start(bf16[64,64,128]{2,1,0:T(8,128)(2,1)} %gather_fusion.9) | copy-start | bytes 3145732
  213.7 5.5 %copy-start.3 = (f32[64,128,64]{1,2,0:T(8,128)S(1)}, f32[64,128,64]{1,2,0:T(8,128)}, u32[]{:S(2)}) copy-start(f32[64,128,64]{1,2,0:T(8,128)} %copy-done.1) | copy-start | bytes 6291460
  213.7 5.5 %copy-start.7 = (f32[64,128,64]{1,2,0:T(8,128)S(1)}, f32[64,128,64]{1,2,0:T(8,128)}, u32[]{:S(2)}) copy-start(f32[64,128,64]{1,2,0:T(8,128)} %copy-done.6) | copy-start | bytes 6291460
  219.2 6.0 %copy-start.10 = (f32[64,128,64]{1,2,0:T(8,128)}, f32[64,128,64]{1,2,0:T(8,128)S(1)}, u32[]{:S(2)}) copy-start(f32[64,128,64]{1,2,0:T(8,128)S(1)} %add_add_fusion.2) | copy-start | bytes 6291460
  225.2 29.6 %collective-permute-start.10 = (bf16[64,8192]{1,0:T(8,128)(2,1)}, bf16[64,8192]{1,0:T(8,128)(2,1)}, u32[]{:S(2)}, u32[]{:S(2)}) collective-permute-start(bf16[64,8192]{1,0:T(8,128)(2,1)} %fusion.309), channel_id=1, source_target_pairs={{1,0},{2,1},{3,2},{4,3},{5,4},{6,5},{7,6},{8,7},{9,8},{10,9},{11,1... | collective-permute-start | bytes 3145736 | tf_op jit(solution)/shard_map/ppermute | solution.py:28
  234.9 34.0 %collective-permute-start.11 = (bf16[64,8192]{1,0:T(8,128)(2,1)}, bf16[64,8192]{1,0:T(8,128)(2,1)}, u32[]{:S(2)}, u32[]{:S(2)}) collective-permute-start(bf16[64,8192]{1,0:T(8,128)(2,1)} %fusion.309), channel_id=1, source_target_pairs={{0,1},{1,2},{2,3},{3,4},{4,5},{5,6},{6,7},{7,8},{8,9},{9,10},{10,1... | collective-permute-start | bytes 3145736 | tf_op jit(solution)/shard_map/ppermute | solution.py:27
  244.7 4.7 %copy-start.25 = (bf16[64,64,128]{2,1,0:T(8,128)(2,1)S(1)}, bf16[64,64,128]{2,1,0:T(8,128)(2,1)}, u32[]{:S(2)}) copy-start(bf16[64,64,128]{2,1,0:T(8,128)(2,1)} %gather_fusion.13) | copy-start | bytes 3145732
  277.4 5.5 %copy-start.4 = (f32[64,128,64]{1,2,0:T(8,128)S(1)}, f32[64,128,64]{1,2,0:T(8,128)}, u32[]{:S(2)}) copy-start(f32[64,128,64]{1,2,0:T(8,128)} %copy-done.1) | copy-start | bytes 6291460
  277.4 5.5 %copy-start.8 = (f32[64,128,64]{1,2,0:T(8,128)S(1)}, f32[64,128,64]{1,2,0:T(8,128)}, u32[]{:S(2)}) copy-start(f32[64,128,64]{1,2,0:T(8,128)} %copy-done.6) | copy-start | bytes 6291460
  277.4 5.5 %copy-start.11 = (f32[64,128,64]{1,2,0:T(8,128)S(1)}, f32[64,128,64]{1,2,0:T(8,128)}, u32[]{:S(2)}) copy-start(f32[64,128,64]{1,2,0:T(8,128)} %copy-done.10) | copy-start | bytes 6291460
  293.0 27.5 %collective-permute-start.12 = (bf16[64,8192]{1,0:T(8,128)(2,1)}, bf16[64,8192]{1,0:T(8,128)(2,1)}, u32[]{:S(2)}, u32[]{:S(2)}) collective-permute-start(bf16[64,8192]{1,0:T(8,128)(2,1)} %get-tuple-element.12), channel_id=1, source_target_pairs={{1,0},{2,1},{3,2},{4,3},{5,4},{6,5},{7,6},{8,7},{9,8},{10,9},{11,1... | collective-permute-start | bytes 3145736 | tf_op jit(solution)/shard_map/ppermute | solution.py:28
  299.1 32.9 %collective-permute-start.13 = (bf16[64,8192]{1,0:T(8,128)(2,1)}, bf16[64,8192]{1,0:T(8,128)(2,1)}, u32[]{:S(2)}, u32[]{:S(2)}) collective-permute-start(bf16[64,8192]{1,0:T(8,128)(2,1)} %get-tuple-element.12), channel_id=1, source_target_pairs={{0,1},{1,2},{2,3},{3,4},{4,5},{5,6},{6,7},{7,8},{8,9},{9,10},{10,1... | collective-permute-start | bytes 3145736 | tf_op jit(solution)/shard_map/ppermute | solution.py:27
  308.5 4.7 %copy-start.5 = (f32[64,8192]{1,0:T(8,128)S(1)}, f32[64,8192]{1,0:T(8,128)}, u32[]{:S(2)}) copy-start(f32[64,8192]{1,0:T(8,128)} %get-tuple-element.13) | copy-start | bytes 6291460
  (14 other events, 41.0 us)
where the time goes:
time: 447 us; the launch traced here: 438 us
  matrix products  156 us (35%)
  local copies, waits for them, and re-layouts  82.1 us (18%)
  blocking collectives  72 us (16%)
  starting transfers between devices  55.8 us (12%)
  other arithmetic  36.3 us (8%)
  waiting for transfers between devices  33.1 us (7%)
    dot_general x20, matrix products, place(): jnp.einsum('ts,tkc->ksc', selector, terms, precision=lax.Precision.HIGHES...  95.9 us
    psum x4, blocking collectives, over_axes(): array = lax.psum(array, axis)  72 us
    gather x20, local copies, waits for them, and re-layouts, tile_terms(): picked = jnp.take(blocks, index, axis=1)  48.2 us
    ppermute x4, waiting for transfers between devices, from_behind(): return lax.ppermute(array, axis, pairs)  33 us
    ppermute x5, starting transfers between devices, extended(): lax.ppermute(last, axis, up)  31.5 us
    dot_general x10, matrix products, tile_terms(): jnp.einsum('ktc,trc->tkr', picked, tiles, preferred_element_type=jnp.floa...  31.1 us
    ppermute x4, starting transfers between devices, from_behind(): return lax.ppermute(array, axis, pairs)  17.8 us
    dot_general x10, matrix products, tile_terms(): jnp.einsum('ktr,trc->tkc', picked, tiles, preferred_element_type=jnp.floa...  17.3 us
  transfers between devices with their start and end apart: 14, of which 2 were waited for; matrix products, arithmetic and copies ran while one was open for 39% of the time, Pallas kernels for 0%

commit v1 on v0

v1 whole, which is shorter than its diff:
```python
import jax
import jax.numpy as jnp
from jax import lax
from jax.experimental import pallas as pl
from jax.experimental.pallas import tpu as pltpu
from jax.sharding import Mesh
from jax.sharding import PartitionSpec as P

EIGS = 64
TILE = 128
BR_DEV = 64
SLOTS = 64
HALF = 32
CHUNK = 16
PANEL = 1024
AXES = ("grp_0", "grp_1", "row_0", "row_1")
F32 = jnp.float32
BF16 = jnp.bfloat16
VM = pl.BlockSpec(memory_space=pltpu.VMEM)
SM = pl.BlockSpec(memory_space=pltpu.SMEM)
PARAMS = pltpu.CompilerParams(vmem_limit_bytes=16 * 1024 * 1024)
NEAR_ROW, NEAR_COL, CROSS_ROW, CROSS_COL, COUNTS = 0, 1, 2, 3, 4


def call(body, shapes, inputs, scratch=()):
    specs = [SM] + [VM] * (len(inputs) - 1)
    return pl.pallas_call(
        body,
        out_shape=[jax.ShapeDtypeStruct(s, d) for s, d in shapes],
        in_specs=specs,
        out_specs=[VM] * len(shapes),
        scratch_shapes=[pltpu.VMEM(s, d) for s, d in scratch],
        compiler_params=PARAMS,
        name=body.__name__,
    )(*inputs)


def block(i):
    return pl.ds(pl.multiple_of(i * TILE, TILE), TILE)


def dot(a, b):
    return jnp.dot(a, b, preferred_element_type=F32)


def dot_t(a, b):
    return lax.dot_general(a, b, (((1,), (1,)), ((), ())), preferred_element_type=F32)


def over_slots(count, body):
    def chunk(i, carry):
        for u in range(CHUNK):
            body(i * CHUNK + u)
        return carry

    lax.fori_loop(0, (count + CHUNK - 1) // CHUNK, chunk, 0)


def over_panels(body):
    def panel(i, carry):
        body(pl.ds(pl.multiple_of(i * PANEL, PANEL), PANEL))
        return carry

    lax.fori_loop(0, BR_DEV * TILE // PANEL, panel, 0)


def lent(idx, tiles, source, acc, out):
    count = idx[COUNTS, 1]
    acc[...] = jnp.zeros_like(acc)

    def slot(t):
        left = source[:, block(idx[CROSS_ROW, t])]
        acc[:, block(idx[CROSS_COL, t])] += dot(left, tiles[t])

    over_slots(count, slot)

    def close(s):
        out[:, s] = acc[:, s].astype(BF16)

    over_panels(close)


def first_lent(idx, cross, source, out_a, out_b, acc):
    count = idx[COUNTS, 1]
    acc[...] = jnp.zeros_like(acc)

    def slot(t):
        left = source[:, block(idx[CROSS_ROW, t])]
        left = jnp.where(t < count, left, jnp.zeros_like(left))
        acc[:, block(idx[CROSS_COL, t])] += dot(left, cross[t])

    over_slots(count, slot)

    def close(s):
        out_a[:, s] = acc[:HALF, s].astype(BF16)
        out_b[:, s] = acc[HALF:, s].astype(BF16)

    over_panels(close)


def prepare(idx, near, cross, near_m, near_t, cross_m, cross_t):
    def one(t, carry):
        for which, src, plain, flipped in ((0, near, near_m, near_t), (1, cross, cross_m, cross_t)):
            tile = src[t]
            tile = jnp.where(t < idx[COUNTS, which], tile, jnp.zeros_like(tile))
            plain[t] = tile
            flipped[t] = tile.T
        return carry

    lax.fori_loop(0, SLOTS, one, 0)


def products(idx, near_m, near_t, cross_t, own, ahead, to_row, to_col, from_ahead):
    to_row[...] = jnp.zeros_like(to_row)
    to_col[...] = jnp.zeros_like(to_col)
    from_ahead[...] = jnp.zeros_like(from_ahead)
    most = jnp.maximum(idx[COUNTS, 0], idx[COUNTS, 1])

    def slot(t):
        row, col = idx[NEAR_ROW, t], idx[NEAR_COL, t]
        to_row[:, block(row)] += dot(own[:, block(col)], near_t[t])
        to_col[:, block(col)] += dot(own[:, block(row)], near_m[t])
        from_ahead[:, block(idx[CROSS_ROW, t])] += dot(
            ahead[:, block(idx[CROSS_COL, t])], cross_t[t]
        )

    over_slots(most, slot)


def first_step(
    idx, near_m, near_t, cross_m, cross_t, own, ahead, behind, new, new_b, new_w, s0, s1, s2
):
    products(idx, near_m, near_t, cross_t, own, ahead, s0, s1, s2)

    def update(s):
        image = s0[:, s] + s1[:, s] + s2[:, s] + behind[:, s].astype(F32)
        following = (-0.25 * own[:, s].astype(F32) - image) * (1.0 / 0.75)
        new[:, s] = following
        new_b[:, s] = following.astype(BF16)

    over_panels(update)
    lent(idx, cross_m, new_b, s0, new_w)


def middle_step(
    idx, near_m, near_t, cross_m, cross_t, own, ahead, behind, current, before,
    new, new_b, new_w, s0, s1, s2,
):
    products(idx, near_m, near_t, cross_t, own, ahead, s0, s1, s2)

    def update(s):
        image = s0[:, s] + s1[:, s] + s2[:, s] + behind[:, s].astype(F32)
        following = (-0.25 * current[:, s] - image) * (2.0 / 0.75) - before[:, s].astype(F32)
        new[:, s] = following
        new_b[:, s] = following.astype(BF16)

    over_panels(update)
    lent(idx, cross_m, new_b, s0, new_w)


def last_step(
    idx, near_m, near_t, cross_m, cross_t, own, ahead, behind, current, before,
    rest, new_b, new_w, s0, s1, s2,
):
    products(idx, near_m, near_t, cross_t, own, ahead, s0, s1, s2)

    def update(s):
        image = s0[:, s] + s1[:, s] + s2[:, s] + behind[:, s].astype(F32)
        following = (-0.25 * current[:, s] - image) * (2.0 / 0.75) - before[:, s].astype(F32)
        rounded = following.astype(BF16)
        new_b[:, s] = rounded
        rest[:, s] = (following - rounded.astype(F32)).astype(BF16)

    over_panels(update)
    lent(idx, cross_m, new_b, s0, new_w)


def local_sums(idx, near_m, own_a, own_b, rest_a, rest_b, out, acc):
    acc[...] = jnp.zeros_like(acc)

    def slot(t):
        row, col = idx[NEAR_ROW, t], idx[NEAR_COL, t]
        left = jnp.concatenate([own_a[:, block(row)], own_b[:, block(row)]], axis=0)
        acc[:, block(col)] += dot(left, near_m[t])

    over_slots(idx[COUNTS, 0], slot)
    total = jnp.zeros((3 * EIGS, EIGS), F32)
    for k in range(0, BR_DEV * TILE, PANEL):
        s = slice(k, k + PANEL)
        own = jnp.concatenate([own_a[:, s], own_b[:, s]], axis=0)
        left = jnp.concatenate(
            [own, rest_a[:, s], rest_b[:, s], acc[:, s].astype(BF16)], axis=0
        )
        total = total + dot_t(left, own)
    half = 0.5 * total[:EIGS]
    out[:, :EIGS] = half + total[EIGS : 2 * EIGS]
    out[:, EIGS:] = half - total[2 * EIGS :]


def crossing_sums(
    idx, sums, own_a, own_b, lent_a, lent_b, ahead_a, ahead_b, behind_a, behind_b, out
):
    middle = BR_DEV * TILE // 2
    total = jnp.zeros((EIGS, EIGS), F32)
    for k in range(0, middle, PANEL):
        s = slice(k, k + PANEL)
        left = jnp.concatenate([behind_a[:, s], behind_b[:, s]], axis=0)
        total = total + dot_t(left, jnp.concatenate([own_a[:, s], own_b[:, s]], axis=0))
        u = slice(middle + k, middle + k + PANEL)
        left = jnp.concatenate([lent_a[:, u], lent_b[:, u]], axis=0)
        total = total + dot_t(left, jnp.concatenate([ahead_a[:, s], ahead_b[:, s]], axis=0))
    gram = sums[:, :EIGS]
    inner = sums[:, EIGS:] - total
    out[:, :EIGS] = gram + gram.T
    out[:, EIGS:] = inner + inner.T


def split(x):
    high = x.astype(BF16)
    return high, (x - high.astype(F32)).astype(BF16)


def finish(idx, sums, own_a, own_b, rest_a, rest_b, basis, rayleigh):
    count = 1.0 / float(128 * BR_DEV * TILE)
    rows = lax.broadcasted_iota(jnp.int32, (EIGS, 2 * EIGS), 0)
    lanes = lax.broadcasted_iota(jnp.int32, (EIGS, 2 * EIGS), 1)
    work = jnp.where(lanes < EIGS, sums[...] * count, (lanes - EIGS == rows).astype(F32))
    for j in range(EIGS - 1):
        pivot_row = work[j : j + 1, :] / work[j : j + 1, j : j + 1]
        column = jnp.where(rows[:, :1] > j, work[:, j : j + 1], 0.0)
        work = work - column * pivot_row
    pivots = jnp.sum(jnp.where(lanes == rows, work, 0.0), axis=1, keepdims=True)
    inverse = (work / jnp.sqrt(pivots))[:, EIGS:]
    high, low = split(inverse)
    left = jnp.concatenate([high, high, low], axis=1)
    for k in range(0, BR_DEV * TILE, PANEL):
        s = slice(k, k + PANEL)
        own = [own_a[:, s], own_b[:, s]]
        right = jnp.concatenate(own + [rest_a[:, s], rest_b[:, s]] + own, axis=0)
        basis[:, s] = dot(left, right)
    inner = sums[:, EIGS:] * count
    halfway = jnp.dot(
        inverse, inner, precision=lax.Precision.HIGHEST, preferred_element_type=F32
    )
    rayleigh[...] = lax.dot_general(
        inverse,
        halfway,
        (((1,), (1,)), ((), ())),
        precision=lax.Precision.HIGHEST,
        preferred_element_type=F32,
    )


def shards(
    iterate, near, near_rows, near_cols, near_count, cross, cross_rows, cross_cols, cross_count
):
    devices = lax.axis_size(AXES)
    width = BR_DEV * TILE
    onward = [(i, i + 1) for i in range(devices - 1)]
    back = [(b, a) for a, b in onward]

    def to_next(x):
        return lax.ppermute(x, AXES, onward)

    def to_last(x):
        return lax.ppermute(x, AXES, back)

    counts = jnp.concatenate([near_count, cross_count, jnp.zeros((SLOTS - 2,), jnp.int32)])
    idx = jnp.stack([near_rows, near_cols, cross_rows, cross_cols, counts])

    half = ((HALF, width), BF16)
    full = ((HALF, width), F32)
    tiles = ((SLOTS, TILE, TILE), BF16)

    own = [iterate[:HALF], iterate[HALF:]]
    ahead = [to_last(x) for x in own]
    give = call(first_lent, [half, half], (idx, cross, iterate), [((EIGS, width), F32)])
    behind = [to_next(x) for x in give]
    near_m, near_t, cross_m, cross_t = call(prepare, [tiles] * 4, (idx, near, cross))
    operands = (idx, near_m, near_t, cross_m, cross_t)

    before, current = [None, None], [x for x in own]
    lend = [None, None]
    rest = [None, None]
    for step in range(4):
        for h in range(2):
            args = operands + (own[h], ahead[h], behind[h])
            if step == 0:
                new, new_b, new_w = call(first_step, [full, half, half], args, [full] * 3)
                before[h], current[h] = own[h], new
            elif step < 3:
                args = args + (current[h], before[h])
                new, new_b, new_w = call(middle_step, [full, half, half], args, [full] * 3)
                before[h], current[h] = current[h], new
            else:
                args = args + (current[h], before[h])
                rest[h], new_b, new_w = call(last_step, [half, half, half], args, [full] * 3)
            own[h], lend[h] = new_b, new_w
            if step < 3:
                ahead[h], behind[h] = to_last(new_b), to_next(new_w)
            else:
                ahead[h] = to_last(new_b[:, width // 2 :])
                behind[h] = to_next(new_w[:, : width // 2])

    sums = call(
        local_sums,
        [((EIGS, 2 * EIGS), F32)],
        (idx, near_m, *own, *rest),
        [((EIGS, width), F32)],
    )[0]
    sums = call(
        crossing_sums,
        [((EIGS, 2 * EIGS), F32)],
        (idx, sums, *own, *lend, *ahead, *behind),
    )[0]
    reach = 1
    while reach < devices:
        sums = sums + lax.ppermute(sums, AXES, [(i, i ^ reach) for i in range(devices)])
        reach *= 2
    basis, rayleigh = call(
        finish,
        [((EIGS, width), F32), ((EIGS, EIGS), F32)],
        (idx, sums, *own, *rest),
    )
    return basis, rayleigh


def solution(mesh):
    finer = Mesh(mesh.devices.reshape(4, 2, 4, 4), AXES)
    in_specs = (
        P(None, AXES),
        P(AXES, None, None),
        P(AXES),
        P(AXES),
        P(AXES),
        P(AXES, None, None),
        P(AXES),
        P(AXES),
        P(AXES),
    )
    return jax.shard_map(
        shards, mesh=finer, in_specs=in_specs, out_specs=(P(None, AXES), P()), check_vma=False
    )
```

time: 447 us -> 193 us (0.43); the launches traced: 438 us -> 190 us
  matrix products: 156 us -> 0 us
  local copies, waits for them, and re-layouts: 82.1 us -> 2.77 us
  blocking collectives: 72 us -> 0 us
  Pallas kernels: 0 us -> 55.1 us
  starting transfers between devices: 55.8 us -> 107 us
  other arithmetic: 36.3 us -> 0.11 us
  waiting for transfers between devices: 33.1 us -> 23 us
    dot_general x42 -> x0, matrix products: 150 us -> none  [the longest x20 95.9 us: place(): jnp.einsum('ts,tkc->ksc', selector, terms, precision=lax.Precision.HIGHES...]
    psum x4 -> x0, blocking collectives: 72 us -> none  [over_axes(): array = lax.psum(array, axis)]
    pallas_call x0 -> x13, Pallas kernels: none -> 55.1 us  [call(): pl.pallas_call(body, out_shape=[jax.ShapeDtypeStruct(s, d) for s, d in sh...]
    ppermute x14 -> x27, starting transfers between devices: 55.8 us -> 107 us  [the longest x10 58.8 us: to_next(): return lax.ppermute(x, AXES, onward)]
    gather x20 -> x0, local copies, waits for them, and re-layouts: 48.2 us -> none  [tile_terms(): picked = jnp.take(blocks, index, axis=1)]
    reshape x15 -> x0, local copies, waits for them, and re-layouts: 31.9 us -> none  [the longest x5 10.7 us: apply_s(): ahead = padded[:, 2 * width:].reshape(EIGS, BR_DEV, TILE)]
    convert_element_type x7 -> x0, other arithmetic: 23.5 us -> none  [the longest x3 12.9 us: mapped(): return (-0.25 * current - apply_s(current.astype(jnp.bfloat16))) / 0.75]
    another operation x5 -> x1, other arithmetic: 12.1 us -> 0.08 us  [shards(): idx = jnp.stack([near_rows, near_cols, cross_rows, cross_cols, counts])]
  transfers between devices with their start and end apart: 14 -> 27, of which waited for: 2 -> 10; matrix products, arithmetic and copies ran while one was open for 39% -> 0% of each run, Pallas kernels for 0% -> 24%
where the time goes in v1:
time: 193 us; the launch traced here: 190 us
  starting transfers between devices  107 us (55%)
  Pallas kernels  55.1 us (29%)
  waiting for transfers between devices  23 us (12%)
  local copies, waits for them, and re-layouts  2.77 us (1%)
  between operations  2.45 us (1%)
    ppermute x10, starting transfers between devices, to_next(): return lax.ppermute(x, AXES, onward)  58.8 us
    pallas_call x13, Pallas kernels, call(): pl.pallas_call(body, out_shape=[jax.ShapeDtypeStruct(s, d) for s, d in sh...  55.1 us
    ppermute x7, starting transfers between devices, shards(): lax.ppermute(sums, AXES, [(i, i ^ reach) for i in range(devices)])  35.1 us
    ppermute x7, waiting for transfers between devices, shards(): lax.ppermute(sums, AXES, [(i, i ^ reach) for i in range(devices)])  16.1 us
    ppermute x10, starting transfers between devices, to_last(): return lax.ppermute(x, AXES, back)  12.9 us
    ppermute x10, waiting for transfers between devices, to_next(): return lax.ppermute(x, AXES, onward)  4.71 us
  transfers between devices with their start and end apart: 27, of which 10 were waited for; matrix products, arithmetic and copies ran while one was open for 0% of the time, Pallas kernels for 24%

profile of v1, /device:TPU:0, one launch (start us, length us, event | category | flops | bytes accessed | tf_op | source)
XLA Modules:
  0.0 190.2 jit_solution(11743924376446956095)
XLA Ops:
  7.8 4.6 %collective-permute-start.1 = (bf16[32,8192]{1,0:T(8,128)(2,1)S(1)}, bf16[32,8192]{1,0:T(8,128)(2,1)S(1)}, u32[]{:S(2)}, u32[]{:S(2)}) collective-permute-start(bf16[32,8192]{1,0:T(8,128)(2,1)S(1)} %get-tuple-element.36), channel_id=1, source_target_pairs={{0,1},{1,2},{2,3},{3,4},{4,5},{5,6},{6,7},{7,8},{8,9},{9,10},{10,1... | collective-permute-start | bytes 1572872 | tf_op jit(solution)/shard_map/ppermute | solution.py:263
  13.7 4.6 %collective-permute-start.9 = (bf16[32,8192]{1,0:T(8,128)(2,1)S(1)}, bf16[32,8192]{1,0:T(8,128)(2,1)S(1)}, u32[]{:S(2)}, u32[]{:S(2)}) collective-permute-start(bf16[32,8192]{1,0:T(8,128)(2,1)S(1)} %get-tuple-element.47), channel_id=1, source_target_pairs={{0,1},{1,2},{2,3},{3,4},{4,5},{5,6},{6,7},{7,8},{8,9},{9,10},{10,1... | collective-permute-start | bytes 1572872 | tf_op jit(solution)/shard_map/ppermute | solution.py:263
  18.3 5.7 %prepare.1 = (bf16[64,128,128]{2,1,0:T(8,128)(2,1)S(1)}, bf16[64,128,128]{2,1,0:T(8,128)(2,1)S(1)}, bf16[64,128,128]{2,1,0:T(8,128)(2,1)S(1)}, bf16[64,128,128]{2,1,0:T(8,128)(2,1)S(1)}) custom-call(s32[5,64]{1,0:T(8,128)S(1)} %stack.23.idx, bf16[64,128,128]{2,1,0:T(8,128)(2,1)S(1)} %copy-done.2, bf16[64,128,128]{2,1,0:T(8,128)(2,1)S(1)} %copy-done), custom_call_target="tpu_custom_call" | custom-call | tf_op jit(solution)/shard_map/prepare/pallas_call | solution.py:27
  24.0 4.7 %first_step.2 = (f32[32,8192]{1,0:T(8,128)S(1)}, bf16[32,8192]{1,0:T(8,128)(2,1)S(1)}, bf16[32,8192]{1,0:T(8,128)(2,1)S(1)}) custom-call(s32[5,64]{1,0:T(8,128)S(1)} %stack.23.idx, bf16[64,128,128]{2,1,0:T(8,128)(2,1)S(1)} %get-tuple-element.32.near_m, bf16[64,128,128]{2,1,0:T(8,128)(2,1)S(1)} %get-tuple-element.33.near_t, ...), custom_call_target="tpu_custom_call" | custom-call | tf_op jit(solution)/shard_map/first_step/pallas_call | solution.py:27
  30.0 4.9 %collective-permute-start.3 = (bf16[32,8192]{1,0:T(8,128)(2,1)S(1)}, bf16[32,8192]{1,0:T(8,128)(2,1)S(1)}, u32[]{:S(2)}, u32[]{:S(2)}) collective-permute-start(bf16[32,8192]{1,0:T(8,128)(2,1)S(1)} %get-tuple-element.38), channel_id=1, source_target_pairs={{0,1},{1,2},{2,3},{3,4},{4,5},{5,6},{6,7},{7,8},{8,9},{9,10},{10,1... | collective-permute-start | bytes 1572872 | tf_op jit(solution)/shard_map/ppermute | solution.py:263
  34.9 4.3 %first_step.3 = (f32[32,8192]{1,0:T(8,128)S(1)}, bf16[32,8192]{1,0:T(8,128)(2,1)S(1)}, bf16[32,8192]{1,0:T(8,128)(2,1)S(1)}) custom-call(s32[5,64]{1,0:T(8,128)S(1)} %stack.23.idx, bf16[64,128,128]{2,1,0:T(8,128)(2,1)S(1)} %get-tuple-element.32.near_m, bf16[64,128,128]{2,1,0:T(8,128)(2,1)S(1)} %get-tuple-element.33.near_t, ...), custom_call_target="tpu_custom_call" | custom-call | tf_op jit(solution)/shard_map/first_step/pallas_call | solution.py:27
  40.5 4.6 %collective-permute-start.11 = (bf16[32,8192]{1,0:T(8,128)(2,1)S(1)}, bf16[32,8192]{1,0:T(8,128)(2,1)S(1)}, u32[]{:S(2)}, u32[]{:S(2)}) collective-permute-start(bf16[32,8192]{1,0:T(8,128)(2,1)S(1)} %get-tuple-element.49), channel_id=1, source_target_pairs={{0,1},{1,2},{2,3},{3,4},{4,5},{5,6},{6,7},{7,8},{8,9},{9,10},{10,1... | collective-permute-start | bytes 1572872 | tf_op jit(solution)/shard_map/ppermute | solution.py:263
  45.1 4.4 %middle_step.4 = (f32[32,8192]{1,0:T(8,128)S(1)}, bf16[32,8192]{1,0:T(8,128)(2,1)S(1)}, bf16[32,8192]{1,0:T(8,128)(2,1)S(1)}) custom-call(s32[5,64]{1,0:T(8,128)S(1)} %stack.23.idx, bf16[64,128,128]{2,1,0:T(8,128)(2,1)S(1)} %get-tuple-element.32.near_m, bf16[64,128,128]{2,1,0:T(8,128)(2,1)S(1)} %get-tuple-element.33.near_t, ...), custom_call_target="tpu_custom_call" | custom-call | tf_op jit(solution)/shard_map/middle_step/pallas_call | solution.py:27
  50.8 6.9 %collective-permute-start.5 = (bf16[32,8192]{1,0:T(8,128)(2,1)S(1)}, bf16[32,8192]{1,0:T(8,128)(2,1)S(1)}, u32[]{:S(2)}, u32[]{:S(2)}) collective-permute-start(bf16[32,8192]{1,0:T(8,128)(2,1)S(1)} %get-tuple-element.41), channel_id=1, source_target_pairs={{0,1},{1,2},{2,3},{3,4},{4,5},{5,6},{6,7},{7,8},{8,9},{9,10},{10,1... | collective-permute-start | bytes 1572872 | tf_op jit(solution)/shard_map/ppermute | solution.py:263
  57.7 4.4 %middle_step.6 = (f32[32,8192]{1,0:T(8,128)S(1)}, bf16[32,8192]{1,0:T(8,128)(2,1)S(1)}, bf16[32,8192]{1,0:T(8,128)(2,1)S(1)}) custom-call(s32[5,64]{1,0:T(8,128)S(1)} %stack.23.idx, bf16[64,128,128]{2,1,0:T(8,128)(2,1)S(1)} %get-tuple-element.32.near_m, bf16[64,128,128]{2,1,0:T(8,128)(2,1)S(1)} %get-tuple-element.33.near_t, ...), custom_call_target="tpu_custom_call" | custom-call | tf_op jit(solution)/shard_map/middle_step/pallas_call | solution.py:27
  63.4 6.9 %collective-permute-start.13 = (bf16[32,8192]{1,0:T(8,128)(2,1)S(1)}, bf16[32,8192]{1,0:T(8,128)(2,1)S(1)}, u32[]{:S(2)}, u32[]{:S(2)}) collective-permute-start(bf16[32,8192]{1,0:T(8,128)(2,1)S(1)} %get-tuple-element.52), channel_id=1, source_target_pairs={{0,1},{1,2},{2,3},{3,4},{4,5},{5,6},{6,7},{7,8},{8,9},{9,10},{10,1... | collective-permute-start | bytes 1572872 | tf_op jit(solution)/shard_map/ppermute | solution.py:263
  70.3 4.3 %middle_step.5 = (f32[32,8192]{1,0:T(8,128)S(1)}, bf16[32,8192]{1,0:T(8,128)(2,1)S(1)}, bf16[32,8192]{1,0:T(8,128)(2,1)S(1)}) custom-call(s32[5,64]{1,0:T(8,128)S(1)} %stack.23.idx, bf16[64,128,128]{2,1,0:T(8,128)(2,1)S(1)} %get-tuple-element.32.near_m, bf16[64,128,128]{2,1,0:T(8,128)(2,1)S(1)} %get-tuple-element.33.near_t, ...), custom_call_target="tpu_custom_call" | custom-call | tf_op jit(solution)/shard_map/middle_step/pallas_call | solution.py:27
  76.0 6.9 %collective-permute-start.7 = (bf16[32,8192]{1,0:T(8,128)(2,1)S(1)}, bf16[32,8192]{1,0:T(8,128)(2,1)S(1)}, u32[]{:S(2)}, u32[]{:S(2)}) collective-permute-start(bf16[32,8192]{1,0:T(8,128)(2,1)S(1)} %get-tuple-element.44), channel_id=1, source_target_pairs={{0,1},{1,2},{2,3},{3,4},{4,5},{5,6},{6,7},{7,8},{8,9},{9,10},{10,1... | collective-permute-start | bytes 1572872 | tf_op jit(solution)/shard_map/ppermute | solution.py:263
  82.9 4.3 %middle_step.7 = (f32[32,8192]{1,0:T(8,128)S(1)}, bf16[32,8192]{1,0:T(8,128)(2,1)S(1)}, bf16[32,8192]{1,0:T(8,128)(2,1)S(1)}) custom-call(s32[5,64]{1,0:T(8,128)S(1)} %stack.23.idx, bf16[64,128,128]{2,1,0:T(8,128)(2,1)S(1)} %get-tuple-element.32.near_m, bf16[64,128,128]{2,1,0:T(8,128)(2,1)S(1)} %get-tuple-element.33.near_t, ...), custom_call_target="tpu_custom_call" | custom-call | tf_op jit(solution)/shard_map/middle_step/pallas_call | solution.py:27
  88.6 6.9 %collective-permute-start.15 = (bf16[32,8192]{1,0:T(8,128)(2,1)S(1)}, bf16[32,8192]{1,0:T(8,128)(2,1)S(1)}, u32[]{:S(2)}, u32[]{:S(2)}) collective-permute-start(bf16[32,8192]{1,0:T(8,128)(2,1)S(1)} %get-tuple-element.55), channel_id=1, source_target_pairs={{0,1},{1,2},{2,3},{3,4},{4,5},{5,6},{6,7},{7,8},{8,9},{9,10},{10,1... | collective-permute-start | bytes 1572872 | tf_op jit(solution)/shard_map/ppermute | solution.py:263
  95.5 4.4 %last_step.2 = (bf16[32,8192]{1,0:T(8,128)(2,1)S(1)}, bf16[32,8192]{1,0:T(8,128)(2,1)S(1)}, bf16[32,8192]{1,0:T(8,128)(2,1)S(1)}) custom-call(s32[5,64]{1,0:T(8,128)S(1)} %stack.23.idx, bf16[64,128,128]{2,1,0:T(8,128)(2,1)S(1)} %get-tuple-element.32.near_m, bf16[64,128,128]{2,1,0:T(8,128)(2,1)S(1)} %get-tuple-element.33.near_t, ...), custom_call_target="tpu_custom_call" | custom-call | tf_op jit(solution)/shard_map/last_step/pallas_call | solution.py:27
  101.3 2.2 %collective-permute-done.14.ahead = bf16[32,8192]{1,0:T(8,128)(2,1)S(1)} collective-permute-done((bf16[32,8192]{1,0:T(8,128)(2,1)S(1)}, bf16[32,8192]{1,0:T(8,128)(2,1)S(1)}, u32[]{:S(2)}, u32[]{:S(2)}) %collective-permute-start.14) | collective-permute-done | bytes 524320 | tf_op jit(solution)/shard_map/ppermute | solution.py:266
  103.5 4.0 %collective-permute-done.15.behind = bf16[32,8192]{1,0:T(8,128)(2,1)S(1)} collective-permute-done((bf16[32,8192]{1,0:T(8,128)(2,1)S(1)}, bf16[32,8192]{1,0:T(8,128)(2,1)S(1)}, u32[]{:S(2)}, u32[]{:S(2)}) %collective-permute-start.15) | collective-permute-done | bytes 524320 | tf_op jit(solution)/shard_map/ppermute | solution.py:263
  107.5 4.4 %last_step.3 = (bf16[32,8192]{1,0:T(8,128)(2,1)S(1)}, bf16[32,8192]{1,0:T(8,128)(2,1)S(1)}, bf16[32,8192]{1,0:T(8,128)(2,1)S(1)}) custom-call(s32[5,64]{1,0:T(8,128)S(1)} %stack.23.idx, bf16[64,128,128]{2,1,0:T(8,128)(2,1)S(1)} %get-tuple-element.32.near_m, bf16[64,128,128]{2,1,0:T(8,128)(2,1)S(1)} %get-tuple-element.33.near_t, ...), custom_call_target="tpu_custom_call" | custom-call | tf_op jit(solution)/shard_map/last_step/pallas_call | solution.py:27
  113.3 5.0 %collective-permute-start.18 = (bf16[32,4096]{1,0:T(8,128)(2,1)S(1)}, bf16[32,4096]{1,0:T(8,128)(2,1)S(1)}, u32[]{:S(2)}, u32[]{:S(2)}) collective-permute-start(bf16[32,4096]{1,0:T(8,128)(2,1)S(1)} %slice.22), channel_id=1, source_target_pairs={{0,1},{1,2},{2,3},{3,4},{4,5},{5,6},{6,7},{7,8},{8,9},{9,10},{10,1... | collective-permute-start | bytes 786440 | tf_op jit(solution)/shard_map/ppermute | solution.py:263
  118.4 7.5 %collective-permute-start.19 = (bf16[32,4096]{1,0:T(8,128)(2,1)S(1)}, bf16[32,4096]{1,0:T(8,128)(2,1)S(1)}, u32[]{:S(2)}, u32[]{:S(2)}) collective-permute-start(bf16[32,4096]{1,0:T(8,128)(2,1)S(1)} %slice.23), channel_id=1, source_target_pairs={{0,1},{1,2},{2,3},{3,4},{4,5},{5,6},{6,7},{7,8},{8,9},{9,10},{10,1... | collective-permute-start | bytes 786440 | tf_op jit(solution)/shard_map/ppermute | solution.py:263
  125.9 3.1 %local_sums.1.sums = f32[64,128]{1,0:T(8,128)S(1)} custom-call(s32[5,64]{1,0:T(8,128)S(1)} %stack.23.idx, bf16[64,128,128]{2,1,0:T(8,128)(2,1)S(1)} %get-tuple-element.32.near_m, bf16[32,8192]{1,0:T(8,128)(2,1)S(1)} %get-tuple-element.46.own_a, bf16[32,8192]{1,0:T(8,128)(2,1)S(1)} %get-tuple-element.57.own_b, bf16[32,8192]{1,0:T(8,128)(2,1)S(1)} %get-tuple-element.58.rest_a, ...), custom_call_target="tpu_custom_call" | custom-call | tf_op jit(solution)/shard_map/local_sums/pallas_call | solution.py:27
  131.0 5.2 %collective-permute-start.20 = (f32[64,128]{1,0:T(8,128)S(1)}, f32[64,128]{1,0:T(8,128)S(1)}, u32[]{:S(2)}, u32[]{:S(2)}) collective-permute-start(f32[64,128]{1,0:T(8,128)S(1)} %crossing_sums.1), channel_id=1, source_target_pairs={{0,1},{1,0},{2,3},{3,2},{4,5},{5,4},{6,7},{7,6},{8,9},{9,8},{10,11... | collective-permute-start | bytes 98312 | tf_op jit(solution)/shard_map/ppermute | solution.py:318
  136.2 1.9 collective-permute-done.20
  138.1 8.4 %collective-permute-start.21 = (f32[64,128]{1,0:T(8,128)S(1)}, f32[64,128]{1,0:T(8,128)S(1)}, u32[]{:S(2)}, u32[]{:S(2)}) collective-permute-start(f32[64,128]{1,0:T(8,128)S(1)} %add.21), channel_id=1, source_target_pairs={{0,2},{1,3},{2,0},{3,1},{4,6},{5,7},{6,4},{7,5},{8,10},{9,11},{10,... | collective-permute-start | bytes 98312 | tf_op jit(solution)/shard_map/ppermute | solution.py:318
  146.4 1.9 collective-permute-done.21
  148.3 6.3 %collective-permute-start.22 = (f32[64,128]{1,0:T(8,128)S(1)}, f32[64,128]{1,0:T(8,128)S(1)}, u32[]{:S(2)}, u32[]{:S(2)}) collective-permute-start(f32[64,128]{1,0:T(8,128)S(1)} %add.22), channel_id=1, source_target_pairs={{0,4},{1,5},{2,6},{3,7},{4,0},{5,1},{6,2},{7,3},{8,12},{9,13},{10,... | collective-permute-start | bytes 98312 | tf_op jit(solution)/shard_map/ppermute | solution.py:318
  154.7 1.9 collective-permute-done.22
  156.6 5.4 %collective-permute-done.23 = f32[64,128]{1,0:T(8,128)S(1)} collective-permute-done((f32[64,128]{1,0:T(8,128)S(1)}, f32[64,128]{1,0:T(8,128)S(1)}, u32[]{:S(2)}, u32[]{:S(2)}) %collective-permute-start.23) | collective-permute-done | bytes 32800 | tf_op jit(solution)/shard_map/ppermute | solution.py:318
  163.2 11.6 %collective-permute-start.25 = (f32[64,128]{1,0:T(8,128)S(1)}, f32[64,128]{1,0:T(8,128)S(1)}, u32[]{:S(2)}, u32[]{:S(2)}) collective-permute-start(f32[64,128]{1,0:T(8,128)S(1)} %add.25), channel_id=1, source_target_pairs={{0,32},{1,33},{2,34},{3,35},{4,36},{5,37},{6,38},{7,39},{8,40},{9,... | collective-permute-start | bytes 98312 | tf_op jit(solution)/shard_map/ppermute | solution.py:318
  176.6 3.7 %collective-permute-start.26 = (f32[64,128]{1,0:T(8,128)S(1)}, f32[64,128]{1,0:T(8,128)S(1)}, u32[]{:S(2)}, u32[]{:S(2)}) collective-permute-start(f32[64,128]{1,0:T(8,128)S(1)} %add.26), channel_id=1, source_target_pairs={{0,64},{1,65},{2,66},{3,67},{4,68},{5,69},{6,70},{7,71},{8,72},{9,... | collective-permute-start | bytes 98312 | tf_op jit(solution)/shard_map/ppermute | solution.py:318
  182.2 8.0 %finish.1 = (f32[64,8192]{1,0:T(8,128)}, f32[64,64]{1,0:T(8,128)}) custom-call(s32[5,64]{1,0:T(8,128)S(1)} %stack.23.idx, f32[64,128]{1,0:T(8,128)S(1)} %add.27.sums, bf16[32,8192]{1,0:T(8,128)(2,1)S(1)} %get-tuple-element.46.own_a, bf16[32,8192]{1,0:T(8,128)(2,1)S(1)} %get-tuple-element.57.own_b, bf16[32,8192]{1,0:T(8,128)(2,1)S(1)} %get-tuple-element.58.rest_a, ...), custom_call_target="tpu_custom_call" | custom-call | tf_op jit(solution)/shard_map/finish/pallas_call | solution.py:27
  (64 shorter events, 24.6 us)
Async XLA Ops:
  0.6 4.2 %copy-start.3 = (s32[64]{0:T(128)S(1)}, s32[64]{0:T(128)}, u32[]{:S(2)}) copy-start(s32[64]{0:T(128)} %param.11) | copy-start | bytes 772
  0.6 4.2 %copy-start.4 = (s32[64]{0:T(128)S(1)}, s32[64]{0:T(128)}, u32[]{:S(2)}) copy-start(s32[64]{0:T(128)} %param.12) | copy-start | bytes 772
  0.7 4.1 %copy-start.5 = (s32[64]{0:T(128)S(1)}, s32[64]{0:T(128)}, u32[]{:S(2)}) copy-start(s32[64]{0:T(128)} %param.15) | copy-start | bytes 772
  0.7 4.2 %copy-start = (bf16[64,128,128]{2,1,0:T(8,128)(2,1)S(1)}, bf16[64,128,128]{2,1,0:T(8,128)(2,1)}, u32[]{:S(2)}) copy-start(bf16[64,128,128]{2,1,0:T(8,128)(2,1)} %cross.3) | copy-start | bytes 6291460
  2.1 21.9 %collective-permute-start = (bf16[32,8192]{1,0:T(8,128)(2,1)S(1)}, bf16[32,8192]{1,0:T(8,128)(2,1)}, u32[]{:S(2)}, u32[]{:S(2)}) collective-permute-start(bf16[32,8192]{1,0:T(8,128)(2,1)S(1)} %get-tuple-element.63.own.before), channel_id=1, source_target_pairs={{1,0},{2,1},{3,2},{4,3},{5,4},{6,5},{7,6},{8,7},{9,8},{10,9},{11,1... | collective-permute-start | bytes 1572872 | tf_op jit(solution)/shard_map/ppermute | solution.py:266
  6.1 12.2 %copy-start.2 = (bf16[64,128,128]{2,1,0:T(8,128)(2,1)S(1)}, bf16[64,128,128]{2,1,0:T(8,128)(2,1)}, u32[]{:S(2)}) copy-start(bf16[64,128,128]{2,1,0:T(8,128)(2,1)} %near.1) | copy-start | bytes 6291460
  7.8 16.2 %collective-permute-start.1 = (bf16[32,8192]{1,0:T(8,128)(2,1)S(1)}, bf16[32,8192]{1,0:T(8,128)(2,1)S(1)}, u32[]{:S(2)}, u32[]{:S(2)}) collective-permute-start(bf16[32,8192]{1,0:T(8,128)(2,1)S(1)} %get-tuple-element.36), channel_id=1, source_target_pairs={{0,1},{1,2},{2,3},{3,4},{4,5},{5,6},{6,7},{7,8},{8,9},{9,10},{10,1... | collective-permute-start | bytes 1572872 | tf_op jit(solution)/shard_map/ppermute | solution.py:263
  12.4 22.5 %collective-permute-start.8 = (bf16[32,8192]{1,0:T(8,128)(2,1)S(1)}, bf16[32,8192]{1,0:T(8,128)(2,1)S(1)}, u32[]{:S(2)}, u32[]{:S(2)}) collective-permute-start(bf16[32,8192]{1,0:T(8,128)(2,1)S(1)} %get-tuple-element.62.own.before), channel_id=1, source_target_pairs={{1,0},{2,1},{3,2},{4,3},{5,4},{6,5},{7,6},{8,7},{9,8},{10,9},{11,1... | collective-permute-start | bytes 1572872 | tf_op jit(solution)/shard_map/ppermute | solution.py:266
  13.7 21.2 %collective-permute-start.9 = (bf16[32,8192]{1,0:T(8,128)(2,1)S(1)}, bf16[32,8192]{1,0:T(8,128)(2,1)S(1)}, u32[]{:S(2)}, u32[]{:S(2)}) collective-permute-start(bf16[32,8192]{1,0:T(8,128)(2,1)S(1)} %get-tuple-element.47), channel_id=1, source_target_pairs={{0,1},{1,2},{2,3},{3,4},{4,5},{5,6},{6,7},{7,8},{8,9},{9,10},{10,1... | collective-permute-start | bytes 1572872 | tf_op jit(solution)/shard_map/ppermute | solution.py:263
  28.7 16.4 %collective-permute-start.2 = (bf16[32,8192]{1,0:T(8,128)(2,1)S(1)}, bf16[32,8192]{1,0:T(8,128)(2,1)S(1)}, u32[]{:S(2)}, u32[]{:S(2)}) collective-permute-start(bf16[32,8192]{1,0:T(8,128)(2,1)S(1)} %get-tuple-element.37.own), channel_id=1, source_target_pairs={{1,0},{2,1},{3,2},{4,3},{5,4},{6,5},{7,6},{8,7},{9,8},{10,9},{11,1... | collective-permute-start | bytes 1572872 | tf_op jit(solution)/shard_map/ppermute | solution.py:266
  30.0 15.1 %collective-permute-start.3 = (bf16[32,8192]{1,0:T(8,128)(2,1)S(1)}, bf16[32,8192]{1,0:T(8,128)(2,1)S(1)}, u32[]{:S(2)}, u32[]{:S(2)}) collective-permute-start(bf16[32,8192]{1,0:T(8,128)(2,1)S(1)} %get-tuple-element.38), channel_id=1, source_target_pairs={{0,1},{1,2},{2,3},{3,4},{4,5},{5,6},{6,7},{7,8},{8,9},{9,10},{10,1... | collective-permute-start | bytes 1572872 | tf_op jit(solution)/shard_map/ppermute | solution.py:263
  39.2 18.5 %collective-permute-start.10 = (bf16[32,8192]{1,0:T(8,128)(2,1)S(1)}, bf16[32,8192]{1,0:T(8,128)(2,1)S(1)}, u32[]{:S(2)}, u32[]{:S(2)}) collective-permute-start(bf16[32,8192]{1,0:T(8,128)(2,1)S(1)} %get-tuple-element.48.own), channel_id=1, source_target_pairs={{1,0},{2,1},{3,2},{4,3},{5,4},{6,5},{7,6},{8,7},{9,8},{10,9},{11,1... | collective-permute-start | bytes 1572872 | tf_op jit(solution)/shard_map/ppermute | solution.py:266
  40.5 17.2 %collective-permute-start.11 = (bf16[32,8192]{1,0:T(8,128)(2,1)S(1)}, bf16[32,8192]{1,0:T(8,128)(2,1)S(1)}, u32[]{:S(2)}, u32[]{:S(2)}) collective-permute-start(bf16[32,8192]{1,0:T(8,128)(2,1)S(1)} %get-tuple-element.49), channel_id=1, source_target_pairs={{0,1},{1,2},{2,3},{3,4},{4,5},{5,6},{6,7},{7,8},{8,9},{9,10},{10,1... | collective-permute-start | bytes 1572872 | tf_op jit(solution)/shard_map/ppermute | solution.py:263
  49.5 20.8 %collective-permute-start.4 = (bf16[32,8192]{1,0:T(8,128)(2,1)S(1)}, bf16[32,8192]{1,0:T(8,128)(2,1)S(1)}, u32[]{:S(2)}, u32[]{:S(2)}) collective-permute-start(bf16[32,8192]{1,0:T(8,128)(2,1)S(1)} %get-tuple-element.40.own), channel_id=1, source_target_pairs={{1,0},{2,1},{3,2},{4,3},{5,4},{6,5},{7,6},{8,7},{9,8},{10,9},{11,1... | collective-permute-start | bytes 1572872 | tf_op jit(solution)/shard_map/ppermute | solution.py:266
  50.8 19.5 %collective-permute-start.5 = (bf16[32,8192]{1,0:T(8,128)(2,1)S(1)}, bf16[32,8192]{1,0:T(8,128)(2,1)S(1)}, u32[]{:S(2)}, u32[]{:S(2)}) collective-permute-start(bf16[32,8192]{1,0:T(8,128)(2,1)S(1)} %get-tuple-element.41), channel_id=1, source_target_pairs={{0,1},{1,2},{2,3},{3,4},{4,5},{5,6},{6,7},{7,8},{8,9},{9,10},{10,1... | collective-permute-start | bytes 1572872 | tf_op jit(solution)/shard_map/ppermute | solution.py:263
  62.1 20.8 %collective-permute-start.12 = (bf16[32,8192]{1,0:T(8,128)(2,1)S(1)}, bf16[32,8192]{1,0:T(8,128)(2,1)S(1)}, u32[]{:S(2)}, u32[]{:S(2)}) collective-permute-start(bf16[32,8192]{1,0:T(8,128)(2,1)S(1)} %get-tuple-element.51.own), channel_id=1, source_target_pairs={{1,0},{2,1},{3,2},{4,3},{5,4},{6,5},{7,6},{8,7},{9,8},{10,9},{11,1... | collective-permute-start | bytes 1572872 | tf_op jit(solution)/shard_map/ppermute | solution.py:266
  63.4 19.5 %collective-permute-start.13 = (bf16[32,8192]{1,0:T(8,128)(2,1)S(1)}, bf16[32,8192]{1,0:T(8,128)(2,1)S(1)}, u32[]{:S(2)}, u32[]{:S(2)}) collective-permute-start(bf16[32,8192]{1,0:T(8,128)(2,1)S(1)} %get-tuple-element.52), channel_id=1, source_target_pairs={{0,1},{1,2},{2,3},{3,4},{4,5},{5,6},{6,7},{7,8},{8,9},{9,10},{10,1... | collective-permute-start | bytes 1572872 | tf_op jit(solution)/shard_map/ppermute | solution.py:263
  74.7 20.8 %collective-permute-start.6 = (bf16[32,8192]{1,0:T(8,128)(2,1)S(1)}, bf16[32,8192]{1,0:T(8,128)(2,1)S(1)}, u32[]{:S(2)}, u32[]{:S(2)}) collective-permute-start(bf16[32,8192]{1,0:T(8,128)(2,1)S(1)} %get-tuple-element.43.own), channel_id=1, source_target_pairs={{1,0},{2,1},{3,2},{4,3},{5,4},{6,5},{7,6},{8,7},{9,8},{10,9},{11,1... | collective-permute-start | bytes 1572872 | tf_op jit(solution)/shard_map/ppermute | solution.py:266
  76.0 19.5 %collective-permute-start.7 = (bf16[32,8192]{1,0:T(8,128)(2,1)S(1)}, bf16[32,8192]{1,0:T(8,128)(2,1)S(1)}, u32[]{:S(2)}, u32[]{:S(2)}) collective-permute-start(bf16[32,8192]{1,0:T(8,128)(2,1)S(1)} %get-tuple-element.44), channel_id=1, source_target_pairs={{0,1},{1,2},{2,3},{3,4},{4,5},{5,6},{6,7},{7,8},{8,9},{9,10},{10,1... | collective-permute-start | bytes 1572872 | tf_op jit(solution)/shard_map/ppermute | solution.py:263
  87.3 16.3 %collective-permute-start.14 = (bf16[32,8192]{1,0:T(8,128)(2,1)S(1)}, bf16[32,8192]{1,0:T(8,128)(2,1)S(1)}, u32[]{:S(2)}, u32[]{:S(2)}) collective-permute-start(bf16[32,8192]{1,0:T(8,128)(2,1)S(1)} %get-tuple-element.54.own), channel_id=1, source_target_pairs={{1,0},{2,1},{3,2},{4,3},{5,4},{6,5},{7,6},{8,7},{9,8},{10,9},{11,1... | collective-permute-start | bytes 1572872 | tf_op jit(solution)/shard_map/ppermute | solution.py:266
  88.6 18.9 %collective-permute-start.15 = (bf16[32,8192]{1,0:T(8,128)(2,1)S(1)}, bf16[32,8192]{1,0:T(8,128)(2,1)S(1)}, u32[]{:S(2)}, u32[]{:S(2)}) collective-permute-start(bf16[32,8192]{1,0:T(8,128)(2,1)S(1)} %get-tuple-element.55), channel_id=1, source_target_pairs={{0,1},{1,2},{2,3},{3,4},{4,5},{5,6},{6,7},{7,8},{8,9},{9,10},{10,1... | collective-permute-start | bytes 1572872 | tf_op jit(solution)/shard_map/ppermute | solution.py:263
  100.0 29.0 %collective-permute-start.16 = (bf16[32,4096]{1,0:T(8,128)(2,1)S(1)}, bf16[32,4096]{1,0:T(8,128)(2,1)S(1)}, u32[]{:S(2)}, u32[]{:S(2)}) collective-permute-start(bf16[32,4096]{1,0:T(8,128)(2,1)S(1)} %slice.20), channel_id=1, source_target_pairs={{1,0},{2,1},{3,2},{4,3},{5,4},{6,5},{7,6},{8,7},{9,8},{10,9},{11,1... | collective-permute-start | bytes 786440 | tf_op jit(solution)/shard_map/ppermute | solution.py:266
  112.0 17.1 %collective-permute-start.17 = (bf16[32,4096]{1,0:T(8,128)(2,1)S(1)}, bf16[32,4096]{1,0:T(8,128)(2,1)S(1)}, u32[]{:S(2)}, u32[]{:S(2)}) collective-permute-start(bf16[32,4096]{1,0:T(8,128)(2,1)S(1)} %slice.21), channel_id=1, source_target_pairs={{1,0},{2,1},{3,2},{4,3},{5,4},{6,5},{7,6},{8,7},{9,8},{10,9},{11,1... | collective-permute-start | bytes 786440 | tf_op jit(solution)/shard_map/ppermute | solution.py:266
  113.3 15.7 %collective-permute-start.18 = (bf16[32,4096]{1,0:T(8,128)(2,1)S(1)}, bf16[32,4096]{1,0:T(8,128)(2,1)S(1)}, u32[]{:S(2)}, u32[]{:S(2)}) collective-permute-start(bf16[32,4096]{1,0:T(8,128)(2,1)S(1)} %slice.22), channel_id=1, source_target_pairs={{0,1},{1,2},{2,3},{3,4},{4,5},{5,6},{6,7},{7,8},{8,9},{9,10},{10,1... | collective-permute-start | bytes 786440 | tf_op jit(solution)/shard_map/ppermute | solution.py:263
  118.4 11.4 %collective-permute-start.19 = (bf16[32,4096]{1,0:T(8,128)(2,1)S(1)}, bf16[32,4096]{1,0:T(8,128)(2,1)S(1)}, u32[]{:S(2)}, u32[]{:S(2)}) collective-permute-start(bf16[32,4096]{1,0:T(8,128)(2,1)S(1)} %slice.23), channel_id=1, source_target_pairs={{0,1},{1,2},{2,3},{3,4},{4,5},{5,6},{6,7},{7,8},{8,9},{9,10},{10,1... | collective-permute-start | bytes 786440 | tf_op jit(solution)/shard_map/ppermute | solution.py:263
  131.0 7.1 %collective-permute-start.20 = (f32[64,128]{1,0:T(8,128)S(1)}, f32[64,128]{1,0:T(8,128)S(1)}, u32[]{:S(2)}, u32[]{:S(2)}) collective-permute-start(f32[64,128]{1,0:T(8,128)S(1)} %crossing_sums.1), channel_id=1, source_target_pairs={{0,1},{1,0},{2,3},{3,2},{4,5},{5,4},{6,7},{7,6},{8,9},{9,8},{10,11... | collective-permute-start | bytes 98312 | tf_op jit(solution)/shard_map/ppermute | solution.py:318
  138.1 10.2 %collective-permute-start.21 = (f32[64,128]{1,0:T(8,128)S(1)}, f32[64,128]{1,0:T(8,128)S(1)}, u32[]{:S(2)}, u32[]{:S(2)}) collective-permute-start(f32[64,128]{1,0:T(8,128)S(1)} %add.21), channel_id=1, source_target_pairs={{0,2},{1,3},{2,0},{3,1},{4,6},{5,7},{6,4},{7,5},{8,10},{9,11},{10,... | collective-permute-start | bytes 98312 | tf_op jit(solution)/shard_map/ppermute | solution.py:318
  148.3 8.2 %collective-permute-start.22 = (f32[64,128]{1,0:T(8,128)S(1)}, f32[64,128]{1,0:T(8,128)S(1)}, u32[]{:S(2)}, u32[]{:S(2)}) collective-permute-start(f32[64,128]{1,0:T(8,128)S(1)} %add.22), channel_id=1, source_target_pairs={{0,4},{1,5},{2,6},{3,7},{4,0},{5,1},{6,2},{7,3},{8,12},{9,13},{10,... | collective-permute-start | bytes 98312 | tf_op jit(solution)/shard_map/ppermute | solution.py:318
  156.6 5.4 %collective-permute-start.23 = (f32[64,128]{1,0:T(8,128)S(1)}, f32[64,128]{1,0:T(8,128)S(1)}, u32[]{:S(2)}, u32[]{:S(2)}) collective-permute-start(f32[64,128]{1,0:T(8,128)S(1)} %add.23), channel_id=1, source_target_pairs={{0,8},{1,9},{2,10},{3,11},{4,12},{5,13},{6,14},{7,15},{8,0},{9,1},... | collective-permute-start | bytes 98312 | tf_op jit(solution)/shard_map/ppermute | solution.py:318
  162.0 1.2 collective-permute-start.24
  163.2 13.4 %collective-permute-start.25 = (f32[64,128]{1,0:T(8,128)S(1)}, f32[64,128]{1,0:T(8,128)S(1)}, u32[]{:S(2)}, u32[]{:S(2)}) collective-permute-start(f32[64,128]{1,0:T(8,128)S(1)} %add.25), channel_id=1, source_target_pairs={{0,32},{1,33},{2,34},{3,35},{4,36},{5,37},{6,38},{7,39},{8,40},{9,... | collective-permute-start | bytes 98312 | tf_op jit(solution)/shard_map/ppermute | solution.py:318
  176.6 5.6 %collective-permute-start.26 = (f32[64,128]{1,0:T(8,128)S(1)}, f32[64,128]{1,0:T(8,128)S(1)}, u32[]{:S(2)}, u32[]{:S(2)}) collective-permute-start(f32[64,128]{1,0:T(8,128)S(1)} %add.26), channel_id=1, source_target_pairs={{0,64},{1,65},{2,66},{3,67},{4,68},{5,69},{6,70},{7,71},{8,72},{9,... | collective-permute-start | bytes 98312 | tf_op jit(solution)/shard_map/ppermute | solution.py:318
  (2 other events, 5.4 us)

commit v2 on v1

v2 whole, which is shorter than its diff:
```python
import jax
import jax.numpy as jnp
from jax import lax
from jax.experimental import pallas as pl
from jax.experimental.pallas import tpu as pltpu
from jax.sharding import Mesh
from jax.sharding import PartitionSpec as P

EIGS = 64
TILE = 128
BR_DEV = 64
SLOTS = 64
HALF = 32
CHUNK = 32
PANEL = 1024
AXES = ("grp_0", "grp_1", "row_0", "row_1")
F32 = jnp.float32
BF16 = jnp.bfloat16
VM = pl.BlockSpec(memory_space=pltpu.VMEM)
SM = pl.BlockSpec(memory_space=pltpu.SMEM)
PARAMS = pltpu.CompilerParams(vmem_limit_bytes=16 * 1024 * 1024)
NEAR_ROW, NEAR_COL, CROSS_ROW, CROSS_COL, COUNTS = 0, 1, 2, 3, 4


def call(body, shapes, inputs, scratch=(), aliases=None, scalars=True):
    specs = [SM if scalars else VM] + [VM] * (len(inputs) - 1)
    return pl.pallas_call(
        body,
        out_shape=[jax.ShapeDtypeStruct(s, d) for s, d in shapes],
        in_specs=specs,
        out_specs=[VM] * len(shapes),
        scratch_shapes=[pltpu.VMEM(s, d) for s, d in scratch],
        input_output_aliases=aliases or {},
        compiler_params=PARAMS,
    )(*inputs)


def block(i):
    return pl.ds(pl.multiple_of(i * TILE, TILE), TILE)


def dot(a, b):
    return jnp.dot(a, b, preferred_element_type=F32)


def dot_t(a, b):
    return lax.dot_general(a, b, (((1,), (1,)), ((), ())), preferred_element_type=F32)


def over_slots(count, body):
    def chunk(i, carry):
        for u in range(0, CHUNK, 2):
            body(i * CHUNK + u, i * CHUNK + u + 1)
        return carry

    lax.fori_loop(0, (count + CHUNK - 1) // CHUNK, chunk, 0)


def over_panels(body):
    def panel(i, carry):
        body(pl.ds(pl.multiple_of(i * PANEL, PANEL), PANEL))
        return carry

    lax.fori_loop(0, BR_DEV * TILE // PANEL, panel, 0)


def add_pair(acc, to_1, to_2, left_1, left_2, tile_1, tile_2):
    rows = left_1.shape[0]
    both = dot(
        jnp.concatenate([left_1, left_2], axis=0), jnp.concatenate([tile_1, tile_2], axis=1)
    )
    acc[:, block(to_1)] += both[:rows, :TILE]
    acc[:, block(to_2)] += both[rows:, TILE:]


def add_products(idx, count, source, source_at, target, target_at, tiles):
    def pair(t, u):
        add_pair(
            target,
            idx[target_at, t],
            idx[target_at, u],
            source[:, block(idx[source_at, t])],
            source[:, block(idx[source_at, u])],
            tiles[t],
            tiles[u],
        )

    over_slots(count, pair)


def first_lent(idx, cross, source, out_a, out_b, acc):
    count = idx[COUNTS, 1]
    acc[...] = jnp.zeros_like(acc)

    def left(t):
        rows = source[:, block(idx[CROSS_ROW, t])]
        return jnp.where(t < count, rows, jnp.zeros_like(rows))

    def pair(t, u):
        add_pair(
            acc, idx[CROSS_COL, t], idx[CROSS_COL, u], left(t), left(u), cross[t], cross[u]
        )

    over_slots(count, pair)

    def close(s):
        out_a[:, s] = acc[:HALF, s].astype(BF16)
        out_b[:, s] = acc[HALF:, s].astype(BF16)

    over_panels(close)


def prepare(idx, near, cross, near_m, near_t, cross_m, cross_t):
    def one(t, carry):
        for which, src, plain, flipped in ((0, near, near_m, near_t), (1, cross, cross_m, cross_t)):
            tile = src[t]
            tile = jnp.where(t < idx[COUNTS, which], tile, jnp.zeros_like(tile))
            plain[t] = tile
            flipped[t] = tile.T
        return carry

    lax.fori_loop(0, SLOTS, one, 0)


def near_part(idx, near_m, near_t, own, to_row, to_col):
    to_row[...] = jnp.zeros_like(to_row)
    to_col[...] = jnp.zeros_like(to_col)

    def pair(t, u):
        for acc, source_at, target_at, tiles in (
            (to_row, NEAR_COL, NEAR_ROW, near_t),
            (to_col, NEAR_ROW, NEAR_COL, near_m),
        ):
            add_pair(
                acc,
                idx[target_at, t],
                idx[target_at, u],
                own[:, block(idx[source_at, t])],
                own[:, block(idx[source_at, u])],
                tiles[t],
                tiles[u],
            )

    over_slots(idx[COUNTS, 0], pair)

    def close(s):
        to_row[:, s] += to_col[:, s]

    over_panels(close)


def step_body(idx, cross_m, cross_t, ahead, behind, current, before, new, new_b, new_w, acc):
    count = idx[COUNTS, 1]
    add_products(idx, count, ahead, CROSS_COL, new, CROSS_ROW, cross_t)

    def update(s):
        image = new[:, s] + behind[:, s].astype(F32)
        following = -0.25 * current[:, s].astype(F32) - image
        if before is None:
            following = following * (1.0 / 0.75)
        else:
            following = following * (2.0 / 0.75) - before[:, s].astype(F32)
        new[:, s] = following
        new_b[:, s] = following.astype(BF16)
        acc[:, s] = jnp.zeros_like(following)

    over_panels(update)
    add_products(idx, count, new_b, CROSS_ROW, acc, CROSS_COL, cross_m)

    def close(s):
        new_w[:, s] = acc[:, s].astype(BF16)

    over_panels(close)


def first_step(idx, near_image, cross_m, cross_t, ahead, behind, current, new, new_b, new_w, acc):
    step_body(idx, cross_m, cross_t, ahead, behind, current, None, new, new_b, new_w, acc)


def next_step(
    idx, near_image, cross_m, cross_t, ahead, behind, current, before, new, new_b, new_w, acc
):
    step_body(idx, cross_m, cross_t, ahead, behind, current, before, new, new_b, new_w, acc)


def local_sums(idx, near_m, own_a, own_b, last_a, last_b, out, stack, acc):
    acc[...] = jnp.zeros_like(acc)

    def left(t):
        rows = block(idx[NEAR_ROW, t])
        return jnp.concatenate([own_a[:, rows], own_b[:, rows]], axis=0)

    def pair(t, u):
        add_pair(
            acc, idx[NEAR_COL, t], idx[NEAR_COL, u], left(t), left(u), near_m[t], near_m[u]
        )

    over_slots(idx[COUNTS, 0], pair)
    total = jnp.zeros((3 * EIGS, EIGS), F32)
    for k in range(0, BR_DEV * TILE, PANEL):
        s = slice(k, k + PANEL)
        own = jnp.concatenate([own_a[:, s], own_b[:, s]], axis=0)
        rest = jnp.concatenate([last_a[:, s], last_b[:, s]], axis=0) - own.astype(F32)
        both = jnp.concatenate([own, rest.astype(BF16)], axis=0)
        stack[:, s] = both
        total = total + dot_t(jnp.concatenate([both, acc[:, s].astype(BF16)], axis=0), own)
    half = 0.5 * total[:EIGS]
    out[:, :EIGS] = half + total[EIGS : 2 * EIGS]
    out[:, EIGS:] = half - total[2 * EIGS :]


def crossing_sums(
    sums, own_a, own_b, lent_a, lent_b, ahead_a, ahead_b, behind_a, behind_b, out
):
    middle = BR_DEV * TILE // 2
    total = jnp.zeros((EIGS, EIGS), F32)
    for k in range(0, middle, PANEL):
        s = slice(k, k + PANEL)
        left = jnp.concatenate([behind_a[:, s], behind_b[:, s]], axis=0)
        total = total + dot_t(left, jnp.concatenate([own_a[:, s], own_b[:, s]], axis=0))
        u = slice(middle + k, middle + k + PANEL)
        left = jnp.concatenate([lent_a[:, u], lent_b[:, u]], axis=0)
        total = total + dot_t(left, jnp.concatenate([ahead_a[:, s], ahead_b[:, s]], axis=0))
    gram = sums[:, :EIGS]
    inner = sums[:, EIGS:] - total
    out[:, :EIGS] = gram + gram.T
    out[:, EIGS:] = inner + inner.T


def split(x):
    high = x.astype(BF16)
    return high, (x - high.astype(F32)).astype(BF16)


def inverse_factor(gram):
    wide = 2 * EIGS
    rows = lax.broadcasted_iota(jnp.int32, (EIGS, wide), 0)
    lanes = lax.broadcasted_iota(jnp.int32, (EIGS, wide), 1)
    work = jnp.where(lanes < EIGS, gram, (lanes - EIGS == rows).astype(F32))
    work = [work[i : i + 8] for i in range(0, EIGS, 8)]
    below = lax.broadcasted_iota(jnp.int32, (8, wide), 0)
    done = []
    for p in range(EIGS // 8):
        columns = [
            [jnp.broadcast_to(w[:, 8 * p + k : 8 * p + k + 1], (8, wide)) for w in work]
            for k in range(8)
        ]
        for k in range(8):
            pivot = jnp.broadcast_to(columns[k][0][k : k + 1], (8, wide))
            row = jnp.broadcast_to(work[0][k : k + 1], (8, wide))
            scale = 1.0 / pivot
            factors = [c * scale for c in columns[k]]
            factors[0] = jnp.where(below > k, factors[0], 0.0)
            for later in range(k + 1, 8):
                top = jnp.broadcast_to(columns[later][0][k : k + 1], (8, wide))
                columns[later] = [c - f * top for c, f in zip(columns[later], factors)]
            work = [w - f * row for w, f in zip(work, factors)]
        done.append(work[0])
        work = work[1:]
    work = jnp.concatenate(done, axis=0)
    pivots = jnp.sum(jnp.where(lanes == rows, work, 0.0), axis=1, keepdims=True)
    return (work / jnp.sqrt(pivots))[:, EIGS:]


def finish(sums, stack, basis, rayleigh):
    count = 1.0 / float(128 * BR_DEV * TILE)
    inverse = inverse_factor(sums[...] * count)
    high, low = split(inverse)
    left = jnp.concatenate([high, high, low], axis=1)
    for k in range(0, BR_DEV * TILE, PANEL):
        s = slice(k, k + PANEL)
        both = stack[:, s]
        basis[:, s] = dot(left, jnp.concatenate([both, both[:EIGS]], axis=0))
    inner = sums[:, EIGS:] * count
    halfway = jnp.dot(
        inverse, inner, precision=lax.Precision.HIGHEST, preferred_element_type=F32
    )
    rayleigh[...] = lax.dot_general(
        inverse,
        halfway,
        (((1,), (1,)), ((), ())),
        precision=lax.Precision.HIGHEST,
        preferred_element_type=F32,
    )


def shards(
    iterate, near, near_rows, near_cols, near_count, cross, cross_rows, cross_cols, cross_count
):
    devices = lax.axis_size(AXES)
    width = BR_DEV * TILE
    onward = [(i, i + 1) for i in range(devices - 1)]
    back = [(b, a) for a, b in onward]

    def to_next(x):
        return lax.ppermute(x, AXES, onward)

    def to_last(x):
        return lax.ppermute(x, AXES, back)

    counts = jnp.concatenate([near_count, cross_count, jnp.zeros((SLOTS - 2,), jnp.int32)])
    idx = jnp.stack([near_rows, near_cols, cross_rows, cross_cols, counts])

    half = ((HALF, width), BF16)
    full = ((HALF, width), F32)
    tiles = ((SLOTS, TILE, TILE), BF16)
    middle = width // 2

    own = [iterate[:HALF], iterate[HALF:]]
    ahead, behind = [None, None], [None, None]
    ahead[0] = to_last(own[0])
    give = call(first_lent, [half, half], (idx, cross, iterate), [((EIGS, width), F32)])
    behind[0] = to_next(give[0])
    ahead[1] = to_last(own[1])
    behind[1] = to_next(give[1])
    near_m, near_t, cross_m, cross_t = call(prepare, [tiles] * 4, (idx, near, cross))

    def near_image(h):
        return call(near_part, [full], (idx, near_m, near_t, own[h]), [full])[0]

    images = [near_image(0), near_image(1)]
    before, current = [None, None], list(own)
    lend = [None, None]
    for step in range(4):
        for h in range(2):
            args = (idx, images[h], cross_m, cross_t, ahead[h], behind[h], current[h])
            if step == 0:
                new, new_b, new_w = call(first_step, [full, half, half], args, [full], {1: 0})
            else:
                new, new_b, new_w = call(
                    next_step, [full, half, half], args + (before[h],), [full], {1: 0}
                )
            before[h], current[h] = current[h], new
            own[h], lend[h] = new_b, new_w
            last = step == 3
            ahead[h] = to_last(new_b[:, middle:] if last else new_b)
            behind[h] = to_next(new_w[:, :middle] if last else new_w)
            if not last:
                images[h] = near_image(h)

    sums, stack = call(
        local_sums,
        [((EIGS, 2 * EIGS), F32), ((2 * EIGS, width), BF16)],
        (idx, near_m, *own, *current),
        [((EIGS, width), F32)],
    )
    sums = call(
        crossing_sums,
        [((EIGS, 2 * EIGS), F32)],
        (sums, *own, *lend, *ahead, *behind),
        scalars=False,
    )[0]
    reach = 1
    while reach < devices:
        sums = sums + lax.ppermute(sums, AXES, [(i, i ^ reach) for i in range(devices)])
        reach *= 2
    basis, rayleigh = call(
        finish, [((EIGS, width), F32), ((EIGS, EIGS), F32)], (sums, stack), scalars=False
    )
    return basis, rayleigh


def solution(mesh):
    finer = Mesh(mesh.devices.reshape(4, 2, 4, 4), AXES)
    in_specs = (
        P(None, AXES),
        P(AXES, None, None),
        P(AXES),
        P(AXES),
        P(AXES),
        P(AXES, None, None),
        P(AXES),
        P(AXES),
        P(AXES),
    )
    return jax.shard_map(
        shards, mesh=finer, in_specs=in_specs, out_specs=(P(None, AXES), P()), check_vma=False
    )
```

time: 193 us -> 186 us (0.964)
  waiting for transfers between devices: 23 us -> 15.9 us
  starting transfers between devices: 107 us -> 113 us
  Pallas kernels: 55.1 us -> 49.6 us
    ppermute x7, starting transfers between devices: 35.1 us -> 44.8 us  [shards(): lax.ppermute(sums, AXES, [(i, i ^ reach) for i in range(devices)])]
    pallas_call x13 -> x21, Pallas kernels: 55.1 us -> 49.6 us  [call(): pl.pallas_call(body, out_shape=[jax.ShapeDtypeStruct(s, d) for s, d in sh...]
    ppermute x10, starting transfers between devices: 58.8 us -> 54.9 us  [to_next(): return lax.ppermute(x, AXES, onward)]
    ppermute x7, waiting for transfers between devices: 16.1 us -> 12.2 us  [shards(): lax.ppermute(sums, AXES, [(i, i ^ reach) for i in range(devices)])]
    ppermute x10, waiting for transfers between devices: 4.71 us -> 1.58 us  [to_next(): return lax.ppermute(x, AXES, onward)]
  transfers between devices with their start and end apart: 27 -> 27, of which waited for: 10 -> 9; matrix products, arithmetic and copies ran while one was open for 0% -> 0% of each run, Pallas kernels for 24% -> 23%
where the time goes in v2:
time: 186 us; the launch traced here: 184 us
  starting transfers between devices  113 us (61%)
  Pallas kernels  49.6 us (27%)
  waiting for transfers between devices  15.9 us (9%)
  local copies, waits for them, and re-layouts  3.7 us (2%)
  between operations  2.46 us (1%)
    ppermute x10, starting transfers between devices, to_next(): return lax.ppermute(x, AXES, onward)  54.9 us
    pallas_call x21, Pallas kernels, call(): pl.pallas_call(body, out_shape=[jax.ShapeDtypeStruct(s, d) for s, d in sh...  49.6 us
    ppermute x7, starting transfers between devices, shards(): lax.ppermute(sums, AXES, [(i, i ^ reach) for i in range(devices)])  44.8 us
    ppermute x10, starting transfers between devices, to_last(): return lax.ppermute(x, AXES, back)  12.9 us
    ppermute x7, waiting for transfers between devices, shards(): lax.ppermute(sums, AXES, [(i, i ^ reach) for i in range(devices)])  12.2 us
  transfers between devices with their start and end apart: 27, of which 9 were waited for; matrix products, arithmetic and copies ran while one was open for 0% of the time, Pallas kernels for 23%

profile of v2, /device:TPU:0, one launch (start us, length us, event | category | flops | bytes accessed | tf_op | source)
XLA Modules:
  0.0 184.4 jit_solution(5328999269615240626)
XLA Ops:
  7.4 3.3 %collective-permute-start.9 = (bf16[32,8192]{1,0:T(8,128)(2,1)S(1)}, bf16[32,8192]{1,0:T(8,128)(2,1)S(1)}, u32[]{:S(2)}, u32[]{:S(2)}) collective-permute-start(bf16[32,8192]{1,0:T(8,128)(2,1)S(1)} %get-tuple-element.49), channel_id=1, source_target_pairs={{0,1},{1,2},{2,3},{3,4},{4,5},{5,6},{6,7},{7,8},{8,9},{9,10},{10,1... | collective-permute-start | bytes 1572872 | tf_op jit(solution)/shard_map/ppermute | solution.py:296
  12.1 4.6 %collective-permute-start.1 = (bf16[32,8192]{1,0:T(8,128)(2,1)S(1)}, bf16[32,8192]{1,0:T(8,128)(2,1)S(1)}, u32[]{:S(2)}, u32[]{:S(2)}) collective-permute-start(bf16[32,8192]{1,0:T(8,128)(2,1)S(1)} %get-tuple-element.38), channel_id=1, source_target_pairs={{0,1},{1,2},{2,3},{3,4},{4,5},{5,6},{6,7},{7,8},{8,9},{9,10},{10,1... | collective-permute-start | bytes 1572872 | tf_op jit(solution)/shard_map/ppermute | solution.py:296
  18.0 5.5 %shard_map.104 = (bf16[64,128,128]{2,1,0:T(8,128)(2,1)S(1)}, bf16[64,128,128]{2,1,0:T(8,128)(2,1)S(1)}, bf16[64,128,128]{2,1,0:T(8,128)(2,1)S(1)}, bf16[64,128,128]{2,1,0:T(8,128)(2,1)S(1)}) custom-call(s32[5,64]{1,0:T(8,128)S(1)} %stack.23.idx, bf16[64,128,128]{2,1,0:T(8,128)(2,1)S(1)} %copy-done.4, bf16[64,128,128]{2,1,0:T(8,128)(2,1)S(1)} %copy-done.1), custom_call_target="tpu_custom_call" | custom-call | tf_op jit(solution)/shard_map/pallas_call | solution.py:27
  25.4 2.0 %collective-permute-done.8.ahead = bf16[32,8192]{1,0:T(8,128)(2,1)S(1)} collective-permute-done((bf16[32,8192]{1,0:T(8,128)(2,1)S(1)}, bf16[32,8192]{1,0:T(8,128)(2,1)S(1)}, u32[]{:S(2)}, u32[]{:S(2)}) %collective-permute-start.8) | collective-permute-done | bytes 524320 | tf_op jit(solution)/shard_map/ppermute | solution.py:299
  27.4 2.4 %shard_map.115 = (f32[32,8192]{1,0:T(8,128)S(1)}, bf16[32,8192]{1,0:T(8,128)(2,1)S(1)}, bf16[32,8192]{1,0:T(8,128)(2,1)S(1)}) custom-call(s32[5,64]{1,0:T(8,128)S(1)} %stack.23.idx, f32[32,8192]{1,0:T(8,128)S(1)} %shard_map.114.near_image, bf16[64,128,128]{2,1,0:T(8,128)(2,1)S(1)} %get-tuple-element.36.cross_m, ...), custom_call_target="tpu_custom_call", output_to_operand_aliasing={{0}: (1, {})} | custom-call | tf_op jit(solution)/shard_map/pallas_call | solution.py:27
  31.2 4.6 %collective-permute-start.11 = (bf16[32,8192]{1,0:T(8,128)(2,1)S(1)}, bf16[32,8192]{1,0:T(8,128)(2,1)S(1)}, u32[]{:S(2)}, u32[]{:S(2)}) collective-permute-start(bf16[32,8192]{1,0:T(8,128)(2,1)S(1)} %get-tuple-element.51), channel_id=1, source_target_pairs={{0,1},{1,2},{2,3},{3,4},{4,5},{5,6},{6,7},{7,8},{8,9},{9,10},{10,1... | collective-permute-start | bytes 1572872 | tf_op jit(solution)/shard_map/ppermute | solution.py:296
  35.8 1.9 %shard_map.105.near_image = f32[32,8192]{1,0:T(8,128)S(1)} custom-call(s32[5,64]{1,0:T(8,128)S(1)} %stack.23.idx, bf16[64,128,128]{2,1,0:T(8,128)(2,1)S(1)} %get-tuple-element.34.near_m, bf16[64,128,128]{2,1,0:T(8,128)(2,1)S(1)} %get-tuple-element.35.near_t, bf16[32,8192]{1,0:T(8,128)(2,1)S(1)} %get-tuple-element.67.own.current.before), custom_call_target="tpu_custom_call" | custom-call | tf_op jit(solution)/shard_map/pallas_call | solution.py:27
  37.7 2.4 %shard_map.107 = (f32[32,8192]{1,0:T(8,128)S(1)}, bf16[32,8192]{1,0:T(8,128)(2,1)S(1)}, bf16[32,8192]{1,0:T(8,128)(2,1)S(1)}) custom-call(s32[5,64]{1,0:T(8,128)S(1)} %stack.23.idx, f32[32,8192]{1,0:T(8,128)S(1)} %shard_map.105.near_image, bf16[64,128,128]{2,1,0:T(8,128)(2,1)S(1)} %get-tuple-element.36.cross_m, ...), custom_call_target="tpu_custom_call", output_to_operand_aliasing={{0}: (1, {})} | custom-call | tf_op jit(solution)/shard_map/pallas_call | solution.py:27
  41.4 4.6 %collective-permute-start.3 = (bf16[32,8192]{1,0:T(8,128)(2,1)S(1)}, bf16[32,8192]{1,0:T(8,128)(2,1)S(1)}, u32[]{:S(2)}, u32[]{:S(2)}) collective-permute-start(bf16[32,8192]{1,0:T(8,128)(2,1)S(1)} %get-tuple-element.40), channel_id=1, source_target_pairs={{0,1},{1,2},{2,3},{3,4},{4,5},{5,6},{6,7},{7,8},{8,9},{9,10},{10,1... | collective-permute-start | bytes 1572872 | tf_op jit(solution)/shard_map/ppermute | solution.py:296
  46.0 1.9 %shard_map.116.near_image = f32[32,8192]{1,0:T(8,128)S(1)} custom-call(s32[5,64]{1,0:T(8,128)S(1)} %stack.23.idx, bf16[64,128,128]{2,1,0:T(8,128)(2,1)S(1)} %get-tuple-element.34.near_m, bf16[64,128,128]{2,1,0:T(8,128)(2,1)S(1)} %get-tuple-element.35.near_t, bf16[32,8192]{1,0:T(8,128)(2,1)S(1)} %get-tuple-element.50.own), custom_call_target="tpu_custom_call" | custom-call | tf_op jit(solution)/shard_map/pallas_call | solution.py:27
  47.9 2.5 %shard_map.117 = (f32[32,8192]{1,0:T(8,128)S(1)}, bf16[32,8192]{1,0:T(8,128)(2,1)S(1)}, bf16[32,8192]{1,0:T(8,128)(2,1)S(1)}) custom-call(s32[5,64]{1,0:T(8,128)S(1)} %stack.23.idx, f32[32,8192]{1,0:T(8,128)S(1)} %shard_map.116.near_image, bf16[64,128,128]{2,1,0:T(8,128)(2,1)S(1)} %get-tuple-element.36.cross_m, ...), custom_call_target="tpu_custom_call", output_to_operand_aliasing={{0}: (1, {})} | custom-call | tf_op jit(solution)/shard_map/pallas_call | solution.py:27
  51.7 4.6 %collective-permute-start.13 = (bf16[32,8192]{1,0:T(8,128)(2,1)S(1)}, bf16[32,8192]{1,0:T(8,128)(2,1)S(1)}, u32[]{:S(2)}, u32[]{:S(2)}) collective-permute-start(bf16[32,8192]{1,0:T(8,128)(2,1)S(1)} %get-tuple-element.54), channel_id=1, source_target_pairs={{0,1},{1,2},{2,3},{3,4},{4,5},{5,6},{6,7},{7,8},{8,9},{9,10},{10,1... | collective-permute-start | bytes 1572872 | tf_op jit(solution)/shard_map/ppermute | solution.py:296
  58.2 2.5 %shard_map.109 = (f32[32,8192]{1,0:T(8,128)S(1)}, bf16[32,8192]{1,0:T(8,128)(2,1)S(1)}, bf16[32,8192]{1,0:T(8,128)(2,1)S(1)}) custom-call(s32[5,64]{1,0:T(8,128)S(1)} %stack.23.idx, f32[32,8192]{1,0:T(8,128)S(1)} %shard_map.108.near_image, bf16[64,128,128]{2,1,0:T(8,128)(2,1)S(1)} %get-tuple-element.36.cross_m, ...), custom_call_target="tpu_custom_call", output_to_operand_aliasing={{0}: (1, {})} | custom-call | tf_op jit(solution)/shard_map/pallas_call | solution.py:27
  62.0 6.7 %collective-permute-start.5 = (bf16[32,8192]{1,0:T(8,128)(2,1)S(1)}, bf16[32,8192]{1,0:T(8,128)(2,1)S(1)}, u32[]{:S(2)}, u32[]{:S(2)}) collective-permute-start(bf16[32,8192]{1,0:T(8,128)(2,1)S(1)} %get-tuple-element.43), channel_id=1, source_target_pairs={{0,1},{1,2},{2,3},{3,4},{4,5},{5,6},{6,7},{7,8},{8,9},{9,10},{10,1... | collective-permute-start | bytes 1572872 | tf_op jit(solution)/shard_map/ppermute | solution.py:296
  70.6 2.4 %shard_map.119 = (f32[32,8192]{1,0:T(8,128)S(1)}, bf16[32,8192]{1,0:T(8,128)(2,1)S(1)}, bf16[32,8192]{1,0:T(8,128)(2,1)S(1)}) custom-call(s32[5,64]{1,0:T(8,128)S(1)} %stack.23.idx, f32[32,8192]{1,0:T(8,128)S(1)} %shard_map.118.near_image, bf16[64,128,128]{2,1,0:T(8,128)(2,1)S(1)} %get-tuple-element.36.cross_m, ...), custom_call_target="tpu_custom_call", output_to_operand_aliasing={{0}: (1, {})} | custom-call | tf_op jit(solution)/shard_map/pallas_call | solution.py:27
  74.4 6.7 %collective-permute-start.15 = (bf16[32,8192]{1,0:T(8,128)(2,1)S(1)}, bf16[32,8192]{1,0:T(8,128)(2,1)S(1)}, u32[]{:S(2)}, u32[]{:S(2)}) collective-permute-start(bf16[32,8192]{1,0:T(8,128)(2,1)S(1)} %get-tuple-element.57), channel_id=1, source_target_pairs={{0,1},{1,2},{2,3},{3,4},{4,5},{5,6},{6,7},{7,8},{8,9},{9,10},{10,1... | collective-permute-start | bytes 1572872 | tf_op jit(solution)/shard_map/ppermute | solution.py:296
  83.0 2.4 %shard_map.111 = (f32[32,8192]{1,0:T(8,128)S(1)}, bf16[32,8192]{1,0:T(8,128)(2,1)S(1)}, bf16[32,8192]{1,0:T(8,128)(2,1)S(1)}) custom-call(s32[5,64]{1,0:T(8,128)S(1)} %stack.23.idx, f32[32,8192]{1,0:T(8,128)S(1)} %shard_map.110.near_image, bf16[64,128,128]{2,1,0:T(8,128)(2,1)S(1)} %get-tuple-element.36.cross_m, ...), custom_call_target="tpu_custom_call", output_to_operand_aliasing={{0}: (1, {})} | custom-call | tf_op jit(solution)/shard_map/pallas_call | solution.py:27
  86.7 6.6 %collective-permute-start.7 = (bf16[32,8192]{1,0:T(8,128)(2,1)S(1)}, bf16[32,8192]{1,0:T(8,128)(2,1)S(1)}, u32[]{:S(2)}, u32[]{:S(2)}) collective-permute-start(bf16[32,8192]{1,0:T(8,128)(2,1)S(1)} %get-tuple-element.46), channel_id=1, source_target_pairs={{0,1},{1,2},{2,3},{3,4},{4,5},{5,6},{6,7},{7,8},{8,9},{9,10},{10,1... | collective-permute-start | bytes 1572872 | tf_op jit(solution)/shard_map/ppermute | solution.py:296
  95.3 2.1 %shard_map.112.near_image = f32[32,8192]{1,0:T(8,128)S(1)} custom-call(s32[5,64]{1,0:T(8,128)S(1)} %stack.23.idx, bf16[64,128,128]{2,1,0:T(8,128)(2,1)S(1)} %get-tuple-element.34.near_m, bf16[64,128,128]{2,1,0:T(8,128)(2,1)S(1)} %get-tuple-element.35.near_t, bf16[32,8192]{1,0:T(8,128)(2,1)S(1)} %get-tuple-element.45.own), custom_call_target="tpu_custom_call" | custom-call | tf_op jit(solution)/shard_map/pallas_call | solution.py:27
  97.4 2.4 %shard_map.121 = (f32[32,8192]{1,0:T(8,128)S(1)}, bf16[32,8192]{1,0:T(8,128)(2,1)S(1)}, bf16[32,8192]{1,0:T(8,128)(2,1)S(1)}) custom-call(s32[5,64]{1,0:T(8,128)S(1)} %stack.23.idx, f32[32,8192]{1,0:T(8,128)S(1)} %shard_map.120.near_image, bf16[64,128,128]{2,1,0:T(8,128)(2,1)S(1)} %get-tuple-element.36.cross_m, ...), custom_call_target="tpu_custom_call", output_to_operand_aliasing={{0}: (1, {})} | custom-call | tf_op jit(solution)/shard_map/pallas_call | solution.py:27
  101.2 6.7 %collective-permute-start.19 = (bf16[32,4096]{1,0:T(8,128)(2,1)S(1)}, bf16[32,4096]{1,0:T(8,128)(2,1)S(1)}, u32[]{:S(2)}, u32[]{:S(2)}) collective-permute-start(bf16[32,4096]{1,0:T(8,128)(2,1)S(1)} %slice.23), channel_id=1, source_target_pairs={{0,1},{1,2},{2,3},{3,4},{4,5},{5,6},{6,7},{7,8},{8,9},{9,10},{10,1... | collective-permute-start | bytes 786440 | tf_op jit(solution)/shard_map/ppermute | solution.py:296
  107.9 2.4 %shard_map.113 = (f32[32,8192]{1,0:T(8,128)S(1)}, bf16[32,8192]{1,0:T(8,128)(2,1)S(1)}, bf16[32,8192]{1,0:T(8,128)(2,1)S(1)}) custom-call(s32[5,64]{1,0:T(8,128)S(1)} %stack.23.idx, f32[32,8192]{1,0:T(8,128)S(1)} %shard_map.112.near_image, bf16[64,128,128]{2,1,0:T(8,128)(2,1)S(1)} %get-tuple-element.36.cross_m, ...), custom_call_target="tpu_custom_call", output_to_operand_aliasing={{0}: (1, {})} | custom-call | tf_op jit(solution)/shard_map/pallas_call | solution.py:27
  111.7 6.6 %collective-permute-start.18 = (bf16[32,4096]{1,0:T(8,128)(2,1)S(1)}, bf16[32,4096]{1,0:T(8,128)(2,1)S(1)}, u32[]{:S(2)}, u32[]{:S(2)}) collective-permute-start(bf16[32,4096]{1,0:T(8,128)(2,1)S(1)} %slice.22), channel_id=1, source_target_pairs={{0,1},{1,2},{2,3},{3,4},{4,5},{5,6},{6,7},{7,8},{8,9},{9,10},{10,1... | collective-permute-start | bytes 786440 | tf_op jit(solution)/shard_map/ppermute | solution.py:296
  118.3 2.7 %shard_map.122 = (f32[64,128]{1,0:T(8,128)S(1)}, bf16[128,8192]{1,0:T(8,128)(2,1)S(1)}) custom-call(s32[5,64]{1,0:T(8,128)S(1)} %stack.23.idx, bf16[64,128,128]{2,1,0:T(8,128)(2,1)S(1)} %get-tuple-element.34.near_m, bf16[32,8192]{1,0:T(8,128)(2,1)S(1)} %get-tuple-element.48.own_a, bf16[32,8192]{1,0:T(8,128)(2,1)S(1)} %get-tuple-element.59.own_b, ...), custom_call_target="tpu_custom_call" | custom-call | tf_op jit(solution)/shard_map/pallas_call | solution.py:27
  123.3 5.2 %collective-permute-start.20 = (f32[64,128]{1,0:T(8,128)S(1)}, f32[64,128]{1,0:T(8,128)S(1)}, u32[]{:S(2)}, u32[]{:S(2)}) collective-permute-start(f32[64,128]{1,0:T(8,128)S(1)} %shard_map.123), channel_id=1, source_target_pairs={{0,1},{1,0},{2,3},{3,2},{4,5},{5,4},{6,7},{7,6},{8,9},{9,8},{10,11... | collective-permute-start | bytes 98312 | tf_op jit(solution)/shard_map/ppermute | solution.py:355
  130.4 9.1 %collective-permute-start.21 = (f32[64,128]{1,0:T(8,128)S(1)}, f32[64,128]{1,0:T(8,128)S(1)}, u32[]{:S(2)}, u32[]{:S(2)}) collective-permute-start(f32[64,128]{1,0:T(8,128)S(1)} %add.21), channel_id=1, source_target_pairs={{0,2},{1,3},{2,0},{3,1},{4,6},{5,7},{6,4},{7,5},{8,10},{9,11},{10,... | collective-permute-start | bytes 98312 | tf_op jit(solution)/shard_map/ppermute | solution.py:355
  141.4 6.0 %collective-permute-start.22 = (f32[64,128]{1,0:T(8,128)S(1)}, f32[64,128]{1,0:T(8,128)S(1)}, u32[]{:S(2)}, u32[]{:S(2)}) collective-permute-start(f32[64,128]{1,0:T(8,128)S(1)} %add.22), channel_id=1, source_target_pairs={{0,4},{1,5},{2,6},{3,7},{4,0},{5,1},{6,2},{7,3},{8,12},{9,13},{10,... | collective-permute-start | bytes 98312 | tf_op jit(solution)/shard_map/ppermute | solution.py:355
  149.3 11.6 %collective-permute-start.23 = (f32[64,128]{1,0:T(8,128)S(1)}, f32[64,128]{1,0:T(8,128)S(1)}, u32[]{:S(2)}, u32[]{:S(2)}) collective-permute-start(f32[64,128]{1,0:T(8,128)S(1)} %add.23), channel_id=1, source_target_pairs={{0,8},{1,9},{2,10},{3,11},{4,12},{5,13},{6,14},{7,15},{8,0},{9,1},... | collective-permute-start | bytes 98312 | tf_op jit(solution)/shard_map/ppermute | solution.py:355
  162.7 1.9 %collective-permute-start.24 = (f32[64,128]{1,0:T(8,128)S(1)}, f32[64,128]{1,0:T(8,128)S(1)}, u32[]{:S(2)}, u32[]{:S(2)}) collective-permute-start(f32[64,128]{1,0:T(8,128)S(1)} %add.24), channel_id=1, source_target_pairs={{0,16},{1,17},{2,18},{3,19},{4,20},{5,21},{6,22},{7,23},{8,24},{9,... | collective-permute-start | bytes 98312 | tf_op jit(solution)/shard_map/ppermute | solution.py:355
  165.5 7.5 %collective-permute-start.25 = (f32[64,128]{1,0:T(8,128)S(1)}, f32[64,128]{1,0:T(8,128)S(1)}, u32[]{:S(2)}, u32[]{:S(2)}) collective-permute-start(f32[64,128]{1,0:T(8,128)S(1)} %add.25), channel_id=1, source_target_pairs={{0,32},{1,33},{2,34},{3,35},{4,36},{5,37},{6,38},{7,39},{8,40},{9,... | collective-permute-start | bytes 98312 | tf_op jit(solution)/shard_map/ppermute | solution.py:355
  174.9 3.6 %collective-permute-start.26 = (f32[64,128]{1,0:T(8,128)S(1)}, f32[64,128]{1,0:T(8,128)S(1)}, u32[]{:S(2)}, u32[]{:S(2)}) collective-permute-start(f32[64,128]{1,0:T(8,128)S(1)} %add.26), channel_id=1, source_target_pairs={{0,64},{1,65},{2,66},{3,67},{4,68},{5,69},{6,70},{7,71},{8,72},{9,... | collective-permute-start | bytes 98312 | tf_op jit(solution)/shard_map/ppermute | solution.py:355
  180.4 3.9 %shard_map.124 = (f32[64,8192]{1,0:T(8,128)}, f32[64,64]{1,0:T(8,128)}) custom-call(f32[64,128]{1,0:T(8,128)S(1)} %add.27.sums, bf16[128,8192]{1,0:T(8,128)(2,1)S(1)} %get-tuple-element.65.stack), custom_call_target="tpu_custom_call" | custom-call | tf_op jit(solution)/shard_map/pallas_call | solution.py:27
  (68 shorter events, 42.5 us)
Async XLA Ops:
  2.7 1.6 copy-start
  4.3 1.2 copy-start.2
  5.6 5.1 %copy-start.3 = (bf16[64,8192]{1,0:T(8,128)(2,1)S(1)}, bf16[64,8192]{1,0:T(8,128)(2,1)}, u32[]{:S(2)}) copy-start(bf16[64,8192]{1,0:T(8,128)(2,1)} %source.1) | copy-start | bytes 3145732
  5.6 12.4 %copy-start.1 = (bf16[64,128,128]{2,1,0:T(8,128)(2,1)S(1)}, bf16[64,128,128]{2,1,0:T(8,128)(2,1)}, u32[]{:S(2)}) copy-start(bf16[64,128,128]{2,1,0:T(8,128)(2,1)} %cross.3) | copy-start | bytes 6291460
  5.6 12.4 %copy-start.4 = (bf16[64,128,128]{2,1,0:T(8,128)(2,1)S(1)}, bf16[64,128,128]{2,1,0:T(8,128)(2,1)}, u32[]{:S(2)}) copy-start(bf16[64,128,128]{2,1,0:T(8,128)(2,1)} %near.1) | copy-start | bytes 6291460
  7.4 18.0 %collective-permute-start.9 = (bf16[32,8192]{1,0:T(8,128)(2,1)S(1)}, bf16[32,8192]{1,0:T(8,128)(2,1)S(1)}, u32[]{:S(2)}, u32[]{:S(2)}) collective-permute-start(bf16[32,8192]{1,0:T(8,128)(2,1)S(1)} %get-tuple-element.49), channel_id=1, source_target_pairs={{0,1},{1,2},{2,3},{3,4},{4,5},{5,6},{6,7},{7,8},{8,9},{9,10},{10,1... | collective-permute-start | bytes 1572872 | tf_op jit(solution)/shard_map/ppermute | solution.py:296
  10.8 16.7 %collective-permute-start.8 = (bf16[32,8192]{1,0:T(8,128)(2,1)S(1)}, bf16[32,8192]{1,0:T(8,128)(2,1)S(1)}, u32[]{:S(2)}, u32[]{:S(2)}) collective-permute-start(bf16[32,8192]{1,0:T(8,128)(2,1)S(1)} %get-tuple-element.66.own.current.before), channel_id=1, source_target_pairs={{1,0},{2,1},{3,2},{4,3},{5,4},{6,5},{7,6},{8,7},{9,8},{10,9},{11,1... | collective-permute-start | bytes 1572872 | tf_op jit(solution)/shard_map/ppermute | solution.py:299
  12.1 25.6 %collective-permute-start.1 = (bf16[32,8192]{1,0:T(8,128)(2,1)S(1)}, bf16[32,8192]{1,0:T(8,128)(2,1)S(1)}, u32[]{:S(2)}, u32[]{:S(2)}) collective-permute-start(bf16[32,8192]{1,0:T(8,128)(2,1)S(1)} %get-tuple-element.38), channel_id=1, source_target_pairs={{0,1},{1,2},{2,3},{3,4},{4,5},{5,6},{6,7},{7,8},{8,9},{9,10},{10,1... | collective-permute-start | bytes 1572872 | tf_op jit(solution)/shard_map/ppermute | solution.py:296
  16.6 21.0 %collective-permute-start = (bf16[32,8192]{1,0:T(8,128)(2,1)S(1)}, bf16[32,8192]{1,0:T(8,128)(2,1)S(1)}, u32[]{:S(2)}, u32[]{:S(2)}) collective-permute-start(bf16[32,8192]{1,0:T(8,128)(2,1)S(1)} %get-tuple-element.67.own.current.before), channel_id=1, source_target_pairs={{1,0},{2,1},{3,2},{4,3},{5,4},{6,5},{7,6},{8,7},{9,8},{10,9},{11,1... | collective-permute-start | bytes 1572872 | tf_op jit(solution)/shard_map/ppermute | solution.py:299
  29.9 18.0 %collective-permute-start.10 = (bf16[32,8192]{1,0:T(8,128)(2,1)S(1)}, bf16[32,8192]{1,0:T(8,128)(2,1)S(1)}, u32[]{:S(2)}, u32[]{:S(2)}) collective-permute-start(bf16[32,8192]{1,0:T(8,128)(2,1)S(1)} %get-tuple-element.50.own), channel_id=1, source_target_pairs={{1,0},{2,1},{3,2},{4,3},{5,4},{6,5},{7,6},{8,7},{9,8},{10,9},{11,1... | collective-permute-start | bytes 1572872 | tf_op jit(solution)/shard_map/ppermute | solution.py:299
  31.2 16.8 %collective-permute-start.11 = (bf16[32,8192]{1,0:T(8,128)(2,1)S(1)}, bf16[32,8192]{1,0:T(8,128)(2,1)S(1)}, u32[]{:S(2)}, u32[]{:S(2)}) collective-permute-start(bf16[32,8192]{1,0:T(8,128)(2,1)S(1)} %get-tuple-element.51), channel_id=1, source_target_pairs={{0,1},{1,2},{2,3},{3,4},{4,5},{5,6},{6,7},{7,8},{8,9},{9,10},{10,1... | collective-permute-start | bytes 1572872 | tf_op jit(solution)/shard_map/ppermute | solution.py:296
  40.1 18.1 %collective-permute-start.2 = (bf16[32,8192]{1,0:T(8,128)(2,1)S(1)}, bf16[32,8192]{1,0:T(8,128)(2,1)S(1)}, u32[]{:S(2)}, u32[]{:S(2)}) collective-permute-start(bf16[32,8192]{1,0:T(8,128)(2,1)S(1)} %get-tuple-element.39.own), channel_id=1, source_target_pairs={{1,0},{2,1},{3,2},{4,3},{5,4},{6,5},{7,6},{8,7},{9,8},{10,9},{11,1... | collective-permute-start | bytes 1572872 | tf_op jit(solution)/shard_map/ppermute | solution.py:299
  41.4 16.8 %collective-permute-start.3 = (bf16[32,8192]{1,0:T(8,128)(2,1)S(1)}, bf16[32,8192]{1,0:T(8,128)(2,1)S(1)}, u32[]{:S(2)}, u32[]{:S(2)}) collective-permute-start(bf16[32,8192]{1,0:T(8,128)(2,1)S(1)} %get-tuple-element.40), channel_id=1, source_target_pairs={{0,1},{1,2},{2,3},{3,4},{4,5},{5,6},{6,7},{7,8},{8,9},{9,10},{10,1... | collective-permute-start | bytes 1572872 | tf_op jit(solution)/shard_map/ppermute | solution.py:296
  50.4 20.2 %collective-permute-start.12 = (bf16[32,8192]{1,0:T(8,128)(2,1)S(1)}, bf16[32,8192]{1,0:T(8,128)(2,1)S(1)}, u32[]{:S(2)}, u32[]{:S(2)}) collective-permute-start(bf16[32,8192]{1,0:T(8,128)(2,1)S(1)} %get-tuple-element.53.own), channel_id=1, source_target_pairs={{1,0},{2,1},{3,2},{4,3},{5,4},{6,5},{7,6},{8,7},{9,8},{10,9},{11,1... | collective-permute-start | bytes 1572872 | tf_op jit(solution)/shard_map/ppermute | solution.py:299
  51.7 18.9 %collective-permute-start.13 = (bf16[32,8192]{1,0:T(8,128)(2,1)S(1)}, bf16[32,8192]{1,0:T(8,128)(2,1)S(1)}, u32[]{:S(2)}, u32[]{:S(2)}) collective-permute-start(bf16[32,8192]{1,0:T(8,128)(2,1)S(1)} %get-tuple-element.54), channel_id=1, source_target_pairs={{0,1},{1,2},{2,3},{3,4},{4,5},{5,6},{6,7},{7,8},{8,9},{9,10},{10,1... | collective-permute-start | bytes 1572872 | tf_op jit(solution)/shard_map/ppermute | solution.py:296
  60.7 22.2 %collective-permute-start.4 = (bf16[32,8192]{1,0:T(8,128)(2,1)S(1)}, bf16[32,8192]{1,0:T(8,128)(2,1)S(1)}, u32[]{:S(2)}, u32[]{:S(2)}) collective-permute-start(bf16[32,8192]{1,0:T(8,128)(2,1)S(1)} %get-tuple-element.42.own), channel_id=1, source_target_pairs={{1,0},{2,1},{3,2},{4,3},{5,4},{6,5},{7,6},{8,7},{9,8},{10,9},{11,1... | collective-permute-start | bytes 1572872 | tf_op jit(solution)/shard_map/ppermute | solution.py:299
  62.0 20.9 %collective-permute-start.5 = (bf16[32,8192]{1,0:T(8,128)(2,1)S(1)}, bf16[32,8192]{1,0:T(8,128)(2,1)S(1)}, u32[]{:S(2)}, u32[]{:S(2)}) collective-permute-start(bf16[32,8192]{1,0:T(8,128)(2,1)S(1)} %get-tuple-element.43), channel_id=1, source_target_pairs={{0,1},{1,2},{2,3},{3,4},{4,5},{5,6},{6,7},{7,8},{8,9},{9,10},{10,1... | collective-permute-start | bytes 1572872 | tf_op jit(solution)/shard_map/ppermute | solution.py:296
  73.1 24.3 %collective-permute-start.14 = (bf16[32,8192]{1,0:T(8,128)(2,1)S(1)}, bf16[32,8192]{1,0:T(8,128)(2,1)S(1)}, u32[]{:S(2)}, u32[]{:S(2)}) collective-permute-start(bf16[32,8192]{1,0:T(8,128)(2,1)S(1)} %get-tuple-element.56.own), channel_id=1, source_target_pairs={{1,0},{2,1},{3,2},{4,3},{5,4},{6,5},{7,6},{8,7},{9,8},{10,9},{11,1... | collective-permute-start | bytes 1572872 | tf_op jit(solution)/shard_map/ppermute | solution.py:299
  74.4 23.0 %collective-permute-start.15 = (bf16[32,8192]{1,0:T(8,128)(2,1)S(1)}, bf16[32,8192]{1,0:T(8,128)(2,1)S(1)}, u32[]{:S(2)}, u32[]{:S(2)}) collective-permute-start(bf16[32,8192]{1,0:T(8,128)(2,1)S(1)} %get-tuple-element.57), channel_id=1, source_target_pairs={{0,1},{1,2},{2,3},{3,4},{4,5},{5,6},{6,7},{7,8},{8,9},{9,10},{10,1... | collective-permute-start | bytes 1572872 | tf_op jit(solution)/shard_map/ppermute | solution.py:296
  85.4 22.4 %collective-permute-start.6 = (bf16[32,8192]{1,0:T(8,128)(2,1)S(1)}, bf16[32,8192]{1,0:T(8,128)(2,1)S(1)}, u32[]{:S(2)}, u32[]{:S(2)}) collective-permute-start(bf16[32,8192]{1,0:T(8,128)(2,1)S(1)} %get-tuple-element.45.own), channel_id=1, source_target_pairs={{1,0},{2,1},{3,2},{4,3},{5,4},{6,5},{7,6},{8,7},{9,8},{10,9},{11,1... | collective-permute-start | bytes 1572872 | tf_op jit(solution)/shard_map/ppermute | solution.py:299
  86.7 21.2 %collective-permute-start.7 = (bf16[32,8192]{1,0:T(8,128)(2,1)S(1)}, bf16[32,8192]{1,0:T(8,128)(2,1)S(1)}, u32[]{:S(2)}, u32[]{:S(2)}) collective-permute-start(bf16[32,8192]{1,0:T(8,128)(2,1)S(1)} %get-tuple-element.46), channel_id=1, source_target_pairs={{0,1},{1,2},{2,3},{3,4},{4,5},{5,6},{6,7},{7,8},{8,9},{9,10},{10,1... | collective-permute-start | bytes 1572872 | tf_op jit(solution)/shard_map/ppermute | solution.py:296
  99.9 21.2 %collective-permute-start.17 = (bf16[32,4096]{1,0:T(8,128)(2,1)S(1)}, bf16[32,4096]{1,0:T(8,128)(2,1)S(1)}, u32[]{:S(2)}, u32[]{:S(2)}) collective-permute-start(bf16[32,4096]{1,0:T(8,128)(2,1)S(1)} %slice.21), channel_id=1, source_target_pairs={{1,0},{2,1},{3,2},{4,3},{5,4},{6,5},{7,6},{8,7},{9,8},{10,9},{11,1... | collective-permute-start | bytes 786440 | tf_op jit(solution)/shard_map/ppermute | solution.py:299
  101.2 19.9 %collective-permute-start.19 = (bf16[32,4096]{1,0:T(8,128)(2,1)S(1)}, bf16[32,4096]{1,0:T(8,128)(2,1)S(1)}, u32[]{:S(2)}, u32[]{:S(2)}) collective-permute-start(bf16[32,4096]{1,0:T(8,128)(2,1)S(1)} %slice.23), channel_id=1, source_target_pairs={{0,1},{1,2},{2,3},{3,4},{4,5},{5,6},{6,7},{7,8},{8,9},{9,10},{10,1... | collective-permute-start | bytes 786440 | tf_op jit(solution)/shard_map/ppermute | solution.py:296
  110.4 10.7 %collective-permute-start.16 = (bf16[32,4096]{1,0:T(8,128)(2,1)S(1)}, bf16[32,4096]{1,0:T(8,128)(2,1)S(1)}, u32[]{:S(2)}, u32[]{:S(2)}) collective-permute-start(bf16[32,4096]{1,0:T(8,128)(2,1)S(1)} %slice.20), channel_id=1, source_target_pairs={{1,0},{2,1},{3,2},{4,3},{5,4},{6,5},{7,6},{8,7},{9,8},{10,9},{11,1... | collective-permute-start | bytes 786440 | tf_op jit(solution)/shard_map/ppermute | solution.py:299
  111.7 10.9 %collective-permute-start.18 = (bf16[32,4096]{1,0:T(8,128)(2,1)S(1)}, bf16[32,4096]{1,0:T(8,128)(2,1)S(1)}, u32[]{:S(2)}, u32[]{:S(2)}) collective-permute-start(bf16[32,4096]{1,0:T(8,128)(2,1)S(1)} %slice.22), channel_id=1, source_target_pairs={{0,1},{1,2},{2,3},{3,4},{4,5},{5,6},{6,7},{7,8},{8,9},{9,10},{10,1... | collective-permute-start | bytes 786440 | tf_op jit(solution)/shard_map/ppermute | solution.py:296
  123.3 7.1 %collective-permute-start.20 = (f32[64,128]{1,0:T(8,128)S(1)}, f32[64,128]{1,0:T(8,128)S(1)}, u32[]{:S(2)}, u32[]{:S(2)}) collective-permute-start(f32[64,128]{1,0:T(8,128)S(1)} %shard_map.123), channel_id=1, source_target_pairs={{0,1},{1,0},{2,3},{3,2},{4,5},{5,4},{6,7},{7,6},{8,9},{9,8},{10,11... | collective-permute-start | bytes 98312 | tf_op jit(solution)/shard_map/ppermute | solution.py:355
  130.4 10.9 %collective-permute-start.21 = (f32[64,128]{1,0:T(8,128)S(1)}, f32[64,128]{1,0:T(8,128)S(1)}, u32[]{:S(2)}, u32[]{:S(2)}) collective-permute-start(f32[64,128]{1,0:T(8,128)S(1)} %add.21), channel_id=1, source_target_pairs={{0,2},{1,3},{2,0},{3,1},{4,6},{5,7},{6,4},{7,5},{8,10},{9,11},{10,... | collective-permute-start | bytes 98312 | tf_op jit(solution)/shard_map/ppermute | solution.py:355
  141.4 7.9 %collective-permute-start.22 = (f32[64,128]{1,0:T(8,128)S(1)}, f32[64,128]{1,0:T(8,128)S(1)}, u32[]{:S(2)}, u32[]{:S(2)}) collective-permute-start(f32[64,128]{1,0:T(8,128)S(1)} %add.22), channel_id=1, source_target_pairs={{0,4},{1,5},{2,6},{3,7},{4,0},{5,1},{6,2},{7,3},{8,12},{9,13},{10,... | collective-permute-start | bytes 98312 | tf_op jit(solution)/shard_map/ppermute | solution.py:355
  149.3 13.5 %collective-permute-start.23 = (f32[64,128]{1,0:T(8,128)S(1)}, f32[64,128]{1,0:T(8,128)S(1)}, u32[]{:S(2)}, u32[]{:S(2)}) collective-permute-start(f32[64,128]{1,0:T(8,128)S(1)} %add.23), channel_id=1, source_target_pairs={{0,8},{1,9},{2,10},{3,11},{4,12},{5,13},{6,14},{7,15},{8,0},{9,1},... | collective-permute-start | bytes 98312 | tf_op jit(solution)/shard_map/ppermute | solution.py:355
  162.7 2.8 %collective-permute-start.24 = (f32[64,128]{1,0:T(8,128)S(1)}, f32[64,128]{1,0:T(8,128)S(1)}, u32[]{:S(2)}, u32[]{:S(2)}) collective-permute-start(f32[64,128]{1,0:T(8,128)S(1)} %add.24), channel_id=1, source_target_pairs={{0,16},{1,17},{2,18},{3,19},{4,20},{5,21},{6,22},{7,23},{8,24},{9,... | collective-permute-start | bytes 98312 | tf_op jit(solution)/shard_map/ppermute | solution.py:355
  165.5 9.4 %collective-permute-start.25 = (f32[64,128]{1,0:T(8,128)S(1)}, f32[64,128]{1,0:T(8,128)S(1)}, u32[]{:S(2)}, u32[]{:S(2)}) collective-permute-start(f32[64,128]{1,0:T(8,128)S(1)} %add.25), channel_id=1, source_target_pairs={{0,32},{1,33},{2,34},{3,35},{4,36},{5,37},{6,38},{7,39},{8,40},{9,... | collective-permute-start | bytes 98312 | tf_op jit(solution)/shard_map/ppermute | solution.py:355
  174.9 5.5 %collective-permute-start.26 = (f32[64,128]{1,0:T(8,128)S(1)}, f32[64,128]{1,0:T(8,128)S(1)}, u32[]{:S(2)}, u32[]{:S(2)}) collective-permute-start(f32[64,128]{1,0:T(8,128)S(1)} %add.26), channel_id=1, source_target_pairs={{0,64},{1,65},{2,66},{3,67},{4,68},{5,69},{6,70},{7,71},{8,72},{9,... | collective-permute-start | bytes 98312 | tf_op jit(solution)/shard_map/ppermute | solution.py:355

commit v3 on v2

--- a/solution.py
+++ b/solution.py
@@ -18,21 +18,34 @@
 BF16 = jnp.bfloat16
 VM = pl.BlockSpec(memory_space=pltpu.VMEM)
 SM = pl.BlockSpec(memory_space=pltpu.SMEM)
+ANY = pl.BlockSpec(memory_space=pl.ANY)
 PARAMS = pltpu.CompilerParams(vmem_limit_bytes=16 * 1024 * 1024)
 NEAR_ROW, NEAR_COL, CROSS_ROW, CROSS_COL, COUNTS = 0, 1, 2, 3, 4
-
-
-def call(body, shapes, inputs, scratch=(), aliases=None, scalars=True):
+ODD = 2
+MIDDLE = BR_DEV * TILE // 2
+
+
+def call(body, shapes, inputs, scratch=(), aliases=None, scalars=True, after=()):
     specs = [SM if scalars else VM] + [VM] * (len(inputs) - 1)
+    specs += [ANY] * (len(after))
+    inputs = tuple(inputs) + tuple(after)
     return pl.pallas_call(
-        body,
+        without(body, len(inputs) - len(after), len(after)),
         out_shape=[jax.ShapeDtypeStruct(s, d) for s, d in shapes],
         in_specs=specs,
         out_specs=[VM] * len(shapes),
         scratch_shapes=[pltpu.VMEM(s, d) for s, d in scratch],
         input_output_aliases=aliases or {},
         compiler_params=PARAMS,
+        name=body.__name__,
     )(*inputs)
+
+
+def without(body, at, count):
+    def run(*refs):
+        body(*refs[:at], *refs[at + count :])
+
+    return run if count else body
 
 
 def block(i):
@@ -88,8 +101,9 @@
     over_slots(count, pair)
 
 
-def first_lent(idx, cross, source, out_a, out_b, acc):
+def first_lent(idx, cross, source, even_a, odd_a, even_b, odd_b, acc):
     count = idx[COUNTS, 1]
+    is_odd = idx[COUNTS, ODD] == 1
     acc[...] = jnp.zeros_like(acc)
 
     def left(t):
@@ -104,22 +118,31 @@
     over_slots(count, pair)
 
     def close(s):
-        out_a[:, s] = acc[:HALF, s].astype(BF16)
-        out_b[:, s] = acc[HALF:, s].astype(BF16)
+        onward = acc[:, s].astype(BF16)
+        back = source[:, s]
+        even = jnp.where(is_odd, back, onward)
+        odd = jnp.where(is_odd, onward, back)
+        even_a[:, s], even_b[:, s] = even[:HALF], even[HALF:]
+        odd_a[:, s], odd_b[:, s] = odd[:HALF], odd[HALF:]
 
     over_panels(close)
 
 
 def prepare(idx, near, cross, near_m, near_t, cross_m, cross_t):
-    def one(t, carry):
-        for which, src, plain, flipped in ((0, near, near_m, near_t), (1, cross, cross_m, cross_t)):
-            tile = src[t]
-            tile = jnp.where(t < idx[COUNTS, which], tile, jnp.zeros_like(tile))
-            plain[t] = tile
-            flipped[t] = tile.T
+    def some(i, carry):
+        for u in range(4):
+            t = 4 * i + u
+            for which, src, plain, flipped in (
+                (0, near, near_m, near_t),
+                (1, cross, cross_m, cross_t),
+            ):
+                tile = src[t]
+                tile = jnp.where(t < idx[COUNTS, which], tile, jnp.zeros_like(tile))
+                plain[t] = tile
+                flipped[t] = tile.T
         return carry
 
-    lax.fori_loop(0, SLOTS, one, 0)
+    lax.fori_loop(0, SLOTS // 4, some, 0)
 
 
 def near_part(idx, near_m, near_t, own, to_row, to_col):
@@ -149,12 +172,21 @@
     over_panels(close)
 
 
-def step_body(idx, cross_m, cross_t, ahead, behind, current, before, new, new_b, new_w, acc):
+def step_body(
+    idx, cross_m, cross_t, from_even, from_odd, current, before, new, new_b, ahead, acc, close
+):
     count = idx[COUNTS, 1]
+    is_odd = idx[COUNTS, ODD] == 1
+
+    def choose(s):
+        ahead[:, s] = jnp.where(is_odd, from_odd[:, s], from_even[:, s])
+
+    over_panels(choose)
     add_products(idx, count, ahead, CROSS_COL, new, CROSS_ROW, cross_t)
 
     def update(s):
-        image = new[:, s] + behind[:, s].astype(F32)
+        behind = jnp.where(is_odd, from_even[:, s], from_odd[:, s])
+        image = new[:, s] + behind.astype(F32)
         following = -0.25 * current[:, s].astype(F32) - image
         if before is None:
             following = following * (1.0 / 0.75)
@@ -166,21 +198,58 @@
 
     over_panels(update)
     add_products(idx, count, new_b, CROSS_ROW, acc, CROSS_COL, cross_m)
-
-    def close(s):
-        new_w[:, s] = acc[:, s].astype(BF16)
-
-    over_panels(close)
-
-
-def first_step(idx, near_image, cross_m, cross_t, ahead, behind, current, new, new_b, new_w, acc):
-    step_body(idx, cross_m, cross_t, ahead, behind, current, None, new, new_b, new_w, acc)
+    close(is_odd)
+
+
+def close_full(new_b, acc, to_even, to_odd):
+    def close(is_odd):
+        def panel(s):
+            onward = acc[:, s].astype(BF16)
+            back = new_b[:, s]
+            to_even[:, s] = jnp.where(is_odd, back, onward)
+            to_odd[:, s] = jnp.where(is_odd, onward, back)
+
+        over_panels(panel)
+
+    return close
+
+
+def first_step(
+    idx, near_image, cross_m, cross_t, from_even, from_odd, current,
+    new, new_b, to_even, to_odd, ahead, acc,
+):
+    step_body(
+        idx, cross_m, cross_t, from_even, from_odd, current, None, new, new_b, ahead, acc,
+        close_full(new_b, acc, to_even, to_odd),
+    )
 
 
 def next_step(
-    idx, near_image, cross_m, cross_t, ahead, behind, current, before, new, new_b, new_w, acc
-):
-    step_body(idx, cross_m, cross_t, ahead, behind, current, before, new, new_b, new_w, acc)
+    idx, near_image, cross_m, cross_t, from_even, from_odd, current, before,
+    new, new_b, to_even, to_odd, ahead, acc,
+):
+    step_body(
+        idx, cross_m, cross_t, from_even, from_odd, current, before, new, new_b, ahead, acc,
+        close_full(new_b, acc, to_even, to_odd),
+    )
+
+
+def last_step(
+    idx, near_image, cross_m, cross_t, from_even, from_odd, current, before,
+    new, new_b, to_even, to_odd, kept, ahead, acc,
+):
+    def close(is_odd):
+        for k in range(0, MIDDLE, PANEL):
+            low, high = slice(k, k + PANEL), slice(MIDDLE + k, MIDDLE + k + PANEL)
+            onward = acc[:, low].astype(BF16)
+            back = new_b[:, high]
+            to_even[:, low] = jnp.where(is_odd, back, onward)
+            to_odd[:, low] = jnp.where(is_odd, onward, back)
+            kept[:, low] = acc[:, high].astype(BF16)
+
+    step_body(
+        idx, cross_m, cross_t, from_even, from_odd, current, before, new, new_b, ahead, acc, close
+    )
 
 
 def local_sums(idx, near_m, own_a, own_b, last_a, last_b, out, stack, acc):
@@ -210,17 +279,19 @@
 
 
 def crossing_sums(
-    sums, own_a, own_b, lent_a, lent_b, ahead_a, ahead_b, behind_a, behind_b, out
-):
-    middle = BR_DEV * TILE // 2
+    idx, sums, own_a, own_b, kept_a, kept_b, even_a, even_b, odd_a, odd_b, out
+):
+    is_odd = idx[COUNTS, ODD] == 1
     total = jnp.zeros((EIGS, EIGS), F32)
-    for k in range(0, middle, PANEL):
+    for k in range(0, MIDDLE, PANEL):
         s = slice(k, k + PANEL)
-        left = jnp.concatenate([behind_a[:, s], behind_b[:, s]], axis=0)
-        total = total + dot_t(left, jnp.concatenate([own_a[:, s], own_b[:, s]], axis=0))
-        u = slice(middle + k, middle + k + PANEL)
-        left = jnp.concatenate([lent_a[:, u], lent_b[:, u]], axis=0)
-        total = total + dot_t(left, jnp.concatenate([ahead_a[:, s], ahead_b[:, s]], axis=0))
+        even = jnp.concatenate([even_a[:, s], even_b[:, s]], axis=0)
+        odd = jnp.concatenate([odd_a[:, s], odd_b[:, s]], axis=0)
+        behind = jnp.where(is_odd, even, odd)
+        ahead = jnp.where(is_odd, odd, even)
+        own = jnp.concatenate([own_a[:, s], own_b[:, s]], axis=0)
+        kept = jnp.concatenate([kept_a[:, s], kept_b[:, s]], axis=0)
+        total = total + dot_t(behind, own) + dot_t(kept, ahead)
     gram = sums[:, :EIGS]
     inner = sums[:, EIGS:] - total
     out[:, :EIGS] = gram + gram.T
@@ -289,30 +360,27 @@
 ):
     devices = lax.axis_size(AXES)
     width = BR_DEV * TILE
-    onward = [(i, i + 1) for i in range(devices - 1)]
-    back = [(b, a) for a, b in onward]
-
-    def to_next(x):
-        return lax.ppermute(x, AXES, onward)
-
-    def to_last(x):
-        return lax.ppermute(x, AXES, back)
-
-    counts = jnp.concatenate([near_count, cross_count, jnp.zeros((SLOTS - 2,), jnp.int32)])
+
+    def swap(x, first):
+        pairs = [(i, i + 1) for i in range(first, devices - 1, 2)]
+        return lax.ppermute(x, AXES, pairs + [(b, a) for a, b in pairs])
+
+    odd = lax.axis_index("row_1") % 2
+    counts = jnp.concatenate(
+        [near_count, cross_count, odd[None].astype(jnp.int32), jnp.zeros((SLOTS - 3,), jnp.int32)]
+    )
     idx = jnp.stack([near_rows, near_cols, cross_rows, cross_cols, counts])
 
     half = ((HALF, width), BF16)
+    quarter = ((HALF, MIDDLE), BF16)
     full = ((HALF, width), F32)
     tiles = ((SLOTS, TILE, TILE), BF16)
-    middle = width // 2
 
     own = [iterate[:HALF], iterate[HALF:]]
-    ahead, behind = [None, None], [None, None]
-    ahead[0] = to_last(own[0])
-    give = call(first_lent, [half, half], (idx, cross, iterate), [((EIGS, width), F32)])
-    behind[0] = to_next(give[0])
-    ahead[1] = to_last(own[1])
-    behind[1] = to_next(give[1])
+    sent = call(first_lent, [half] * 4, (idx, cross, iterate), [((EIGS, width), F32)])
+    from_even, from_odd = [None, None], [None, None]
+    for h in range(2):
+        from_even[h], from_odd[h] = swap(sent[2 * h], 0), swap(sent[2 * h + 1], 1)
     near_m, near_t, cross_m, cross_t = call(prepare, [tiles] * 4, (idx, near, cross))
 
     def near_image(h):
@@ -320,22 +388,28 @@
 
     images = [near_image(0), near_image(1)]
     before, current = [None, None], list(own)
-    lend = [None, None]
+    kept = [None, None]
+    scratch = [half, full]
     for step in range(4):
         for h in range(2):
-            args = (idx, images[h], cross_m, cross_t, ahead[h], behind[h], current[h])
+            args = (idx, images[h], cross_m, cross_t, from_even[h], from_odd[h], current[h])
+            outs = [full, half, half, half]
+            after = (images[1 - h],) if step or h else ()
             if step == 0:
-                new, new_b, new_w = call(first_step, [full, half, half], args, [full], {1: 0})
+                new, own[h], even, odd = call(first_step, outs, args, scratch, {1: 0}, after=after)
+            elif step < 3:
+                args = args + (before[h],)
+                new, own[h], even, odd = call(next_step, outs, args, scratch, {1: 0}, after=after)
             else:
-                new, new_b, new_w = call(
-                    next_step, [full, half, half], args + (before[h],), [full], {1: 0}
+                args = args + (before[h],)
+                outs = [full, half, quarter, quarter, quarter]
+                after = after if h == 0 else ()
+                new, own[h], even, odd, kept[h] = call(
+                    last_step, outs, args, scratch, {1: 0}, after=after
                 )
             before[h], current[h] = current[h], new
-            own[h], lend[h] = new_b, new_w
-            last = step == 3
-            ahead[h] = to_last(new_b[:, middle:] if last else new_b)
-            behind[h] = to_next(new_w[:, :middle] if last else new_w)
-            if not last:
+            from_even[h], from_odd[h] = swap(even, 0), swap(odd, 1)
+            if step < 3:
                 images[h] = near_image(h)
 
     sums, stack = call(
@@ -347,8 +421,7 @@
     sums = call(
         crossing_sums,
         [((EIGS, 2 * EIGS), F32)],
-        (sums, *own, *lend, *ahead, *behind),
-        scalars=False,
+        (idx, sums, *own, *kept, *from_even, *from_odd),
     )[0]
     reach = 1
     while reach < devices:

time: 186 us -> 164 us (0.88)
  starting transfers between devices: 113 us -> 83.4 us
  waiting for transfers between devices: 15.9 us -> 23.9 us
    ppermute x20, starting transfers between devices: 67.8 us -> 50.7 us  [swap(): return lax.ppermute(x, AXES, pairs + [(b, a) for a, b in pairs])]
    ppermute x7, starting transfers between devices: 44.8 us -> 32.7 us  [shards(): lax.ppermute(sums, AXES, [(i, i ^ reach) for i in range(devices)])]
    ppermute x20, waiting for transfers between devices: 3.64 us -> 9.68 us  [swap(): return lax.ppermute(x, AXES, pairs + [(b, a) for a, b in pairs])]
    ppermute x7, waiting for transfers between devices: 12.2 us -> 14.2 us  [shards(): lax.ppermute(sums, AXES, [(i, i ^ reach) for i in range(devices)])]
  transfers between devices with their start and end apart: 27 -> 27, of which waited for: 9 -> 13; matrix products, arithmetic and copies ran while one was open for 0% -> 0% of each run, Pallas kernels for 23% -> 26%
where the time goes in v3:
time: 164 us; the launch traced here: 162 us
  starting transfers between devices  83.4 us (51%)
  Pallas kernels  48.9 us (30%)
  waiting for transfers between devices  23.9 us (15%)
  local copies, waits for them, and re-layouts  3.62 us (2%)
  between operations  2.26 us (1%)
    ppermute x20, starting transfers between devices, swap(): return lax.ppermute(x, AXES, pairs + [(b, a) for a, b in pairs])  50.7 us
    pallas_call x21, Pallas kernels, call(): pl.pallas_call(without(body, len(inputs) - len(after), len(after)), out_s...  48.9 us
    ppermute x7, starting transfers between devices, shards(): lax.ppermute(sums, AXES, [(i, i ^ reach) for i in range(devices)])  32.7 us
    ppermute x7, waiting for transfers between devices, shards(): lax.ppermute(sums, AXES, [(i, i ^ reach) for i in range(devices)])  14.2 us
    ppermute x20, waiting for transfers between devices, swap(): return lax.ppermute(x, AXES, pairs + [(b, a) for a, b in pairs])  9.68 us
  transfers between devices with their start and end apart: 27, of which 13 were waited for; matrix products, arithmetic and copies ran while one was open for 0% of the time, Pallas kernels for 26%

profile of v3, /device:TPU:0, one launch (start us, length us, event | category | flops | bytes accessed | tf_op | source)
XLA Modules:
  0.0 162.1 jit_solution(5449699709280476170)
XLA Ops:
  5.6 2.0 %first_lent.1 = (bf16[32,8192]{1,0:T(8,128)(2,1)S(1)}, bf16[32,8192]{1,0:T(8,128)(2,1)S(1)}, bf16[32,8192]{1,0:T(8,128)(2,1)S(1)}, bf16[32,8192]{1,0:T(8,128)(2,1)S(1)}) custom-call(s32[5,64]{1,0:T(8,128)S(1)} %stack.23.idx.refs_0_, bf16[64,128,128]{2,1,0:T(8,128)(2,1)S(1)} %copy-done, bf16[64,8192]{1,0:T(8,128)(2,1)S(1)} %copy-done.2), custom_call_target="tpu_custom_call" | custom-call | tf_op jit(solution)/shard_map/first_lent/pallas_call | solution.py:32
  10.1 4.2 %collective-permute-start.4 = (bf16[32,8192]{1,0:T(8,128)(2,1)S(1)}, bf16[32,8192]{1,0:T(8,128)(2,1)S(1)}, u32[]{:S(2)}, u32[]{:S(2)}) collective-permute-start(bf16[32,8192]{1,0:T(8,128)(2,1)S(1)} %get-tuple-element.56), channel_id=1, source_target_pairs={{0,1},{2,3},{4,5},{6,7},{8,9},{10,11},{12,13},{14,15},{16,17},{18,... | collective-permute-start | bytes 1572872 | tf_op jit(solution)/shard_map/ppermute | solution.py:366
  15.0 3.0 %prepare.1 = (bf16[64,128,128]{2,1,0:T(8,128)(2,1)S(1)}, bf16[64,128,128]{2,1,0:T(8,128)(2,1)S(1)}, bf16[64,128,128]{2,1,0:T(8,128)(2,1)S(1)}, bf16[64,128,128]{2,1,0:T(8,128)(2,1)S(1)}) custom-call(s32[5,64]{1,0:T(8,128)S(1)} %stack.23.idx.refs_0_, bf16[64,128,128]{2,1,0:T(8,128)(2,1)S(1)} %copy-done.3, bf16[64,128,128]{2,1,0:T(8,128)(2,1)S(1)} %copy-done.1), custom_call_target="tpu_custom_call" | custom-call | tf_op jit(solution)/shard_map/prepare/pallas_call | solution.py:32
  18.0 1.9 %near_part.8.near_image = f32[32,8192]{1,0:T(8,128)S(1)} custom-call(s32[5,64]{1,0:T(8,128)S(1)} %stack.23.idx.refs_0_, bf16[64,128,128]{2,1,0:T(8,128)(2,1)S(1)} %get-tuple-element.46.near_m, bf16[64,128,128]{2,1,0:T(8,128)(2,1)S(1)} %get-tuple-element.47.near_t, bf16[32,8192]{1,0:T(8,128)(2,1)S(1)} %get-tuple-element.91.own.current.refs_7_), custom_call_target="tpu_custom_call" | custom-call | tf_op jit(solution)/shard_map/near_part/pallas_call | solution.py:32
  19.9 2.6 %collective-permute-done.from_even = bf16[32,8192]{1,0:T(8,128)(2,1)S(1)} collective-permute-done((bf16[32,8192]{1,0:T(8,128)(2,1)S(1)}, bf16[32,8192]{1,0:T(8,128)(2,1)S(1)}, u32[]{:S(2)}, u32[]{:S(2)}) %collective-permute-start) | collective-permute-done | bytes 524320 | tf_op jit(solution)/shard_map/ppermute | solution.py:366
  22.5 2.6 %first_step.2 = (f32[32,8192]{1,0:T(8,128)S(1)}, bf16[32,8192]{1,0:T(8,128)(2,1)S(1)}, bf16[32,8192]{1,0:T(8,128)(2,1)S(1)}, bf16[32,8192]{1,0:T(8,128)(2,1)S(1)}) custom-call(s32[5,64]{1,0:T(8,128)S(1)} %stack.23.idx.refs_0_, f32[32,8192]{1,0:T(8,128)S(1)} %near_part.8.near_image, ...), custom_call_target="tpu_custom_call", output_to_operand_aliasing={{0}: (1, {})} | custom-call | tf_op jit(solution)/shard_map/first_step/pallas_call | solution.py:32
  25.1 4.5 %collective-permute-start.2 = (bf16[32,8192]{1,0:T(8,128)(2,1)S(1)}, bf16[32,8192]{1,0:T(8,128)(2,1)S(1)}, u32[]{:S(2)}, u32[]{:S(2)}) collective-permute-start(bf16[32,8192]{1,0:T(8,128)(2,1)S(1)} %get-tuple-element.53), channel_id=1, source_target_pairs={{0,1},{2,3},{4,5},{6,7},{8,9},{10,11},{12,13},{14,15},{16,17},{18,... | collective-permute-start | bytes 1572872 | tf_op jit(solution)/shard_map/ppermute | solution.py:366
  34.1 2.6 %first_step.3 = (f32[32,8192]{1,0:T(8,128)S(1)}, bf16[32,8192]{1,0:T(8,128)(2,1)S(1)}, bf16[32,8192]{1,0:T(8,128)(2,1)S(1)}, bf16[32,8192]{1,0:T(8,128)(2,1)S(1)}) custom-call(s32[5,64]{1,0:T(8,128)S(1)} %stack.23.idx.refs_0_, f32[32,8192]{1,0:T(8,128)S(1)} %near_part.10.refs_1_, ...), custom_call_target="tpu_custom_call", output_to_operand_aliasing={{0}: (1, {})} | custom-call | tf_op jit(solution)/shard_map/first_step/pallas_call | solution.py:32
  36.7 6.2 %collective-permute-start.8 = (bf16[32,8192]{1,0:T(8,128)(2,1)S(1)}, bf16[32,8192]{1,0:T(8,128)(2,1)S(1)}, u32[]{:S(2)}, u32[]{:S(2)}) collective-permute-start(bf16[32,8192]{1,0:T(8,128)(2,1)S(1)} %get-tuple-element.63), channel_id=1, source_target_pairs={{0,1},{2,3},{4,5},{6,7},{8,9},{10,11},{12,13},{14,15},{16,17},{18,... | collective-permute-start | bytes 1572872 | tf_op jit(solution)/shard_map/ppermute | solution.py:366
  45.5 2.6 %next_step.4 = (f32[32,8192]{1,0:T(8,128)S(1)}, bf16[32,8192]{1,0:T(8,128)(2,1)S(1)}, bf16[32,8192]{1,0:T(8,128)(2,1)S(1)}, bf16[32,8192]{1,0:T(8,128)(2,1)S(1)}) custom-call(s32[5,64]{1,0:T(8,128)S(1)} %stack.23.idx.refs_0_, f32[32,8192]{1,0:T(8,128)S(1)} %near_part.9.refs_7_.refs_1_, ...), custom_call_target="tpu_custom_call", output_to_operand_aliasing={{0}: (1, {})} | custom-call | tf_op jit(solution)/shard_map/next_step/pallas_call | solution.py:32
  48.1 4.1 %collective-permute-start.6 = (bf16[32,8192]{1,0:T(8,128)(2,1)S(1)}, bf16[32,8192]{1,0:T(8,128)(2,1)S(1)}, u32[]{:S(2)}, u32[]{:S(2)}) collective-permute-start(bf16[32,8192]{1,0:T(8,128)(2,1)S(1)} %get-tuple-element.60), channel_id=1, source_target_pairs={{0,1},{2,3},{4,5},{6,7},{8,9},{10,11},{12,13},{14,15},{16,17},{18,... | collective-permute-start | bytes 1572872 | tf_op jit(solution)/shard_map/ppermute | solution.py:366
  54.9 2.7 %next_step.5 = (f32[32,8192]{1,0:T(8,128)S(1)}, bf16[32,8192]{1,0:T(8,128)(2,1)S(1)}, bf16[32,8192]{1,0:T(8,128)(2,1)S(1)}, bf16[32,8192]{1,0:T(8,128)(2,1)S(1)}) custom-call(s32[5,64]{1,0:T(8,128)S(1)} %stack.23.idx.refs_0_, f32[32,8192]{1,0:T(8,128)S(1)} %near_part.11.refs_8_.refs_1_, ...), custom_call_target="tpu_custom_call", output_to_operand_aliasing={{0}: (1, {})} | custom-call | tf_op jit(solution)/shard_map/next_step/pallas_call | solution.py:32
  57.5 4.6 %collective-permute-start.12 = (bf16[32,8192]{1,0:T(8,128)(2,1)S(1)}, bf16[32,8192]{1,0:T(8,128)(2,1)S(1)}, u32[]{:S(2)}, u32[]{:S(2)}) collective-permute-start(bf16[32,8192]{1,0:T(8,128)(2,1)S(1)} %get-tuple-element.71), channel_id=1, source_target_pairs={{0,1},{2,3},{4,5},{6,7},{8,9},{10,11},{12,13},{14,15},{16,17},{18,... | collective-permute-start | bytes 1572872 | tf_op jit(solution)/shard_map/ppermute | solution.py:366
  64.9 2.6 %next_step.6 = (f32[32,8192]{1,0:T(8,128)S(1)}, bf16[32,8192]{1,0:T(8,128)(2,1)S(1)}, bf16[32,8192]{1,0:T(8,128)(2,1)S(1)}, bf16[32,8192]{1,0:T(8,128)(2,1)S(1)}) custom-call(s32[5,64]{1,0:T(8,128)S(1)} %stack.23.idx.refs_0_, f32[32,8192]{1,0:T(8,128)S(1)} %near_part.12.refs_8_.refs_1_, ...), custom_call_target="tpu_custom_call", output_to_operand_aliasing={{0}: (1, {})} | custom-call | tf_op jit(solution)/shard_map/next_step/pallas_call | solution.py:32
  69.4 5.4 %collective-permute-start.10 = (bf16[32,8192]{1,0:T(8,128)(2,1)S(1)}, bf16[32,8192]{1,0:T(8,128)(2,1)S(1)}, u32[]{:S(2)}, u32[]{:S(2)}) collective-permute-start(bf16[32,8192]{1,0:T(8,128)(2,1)S(1)} %get-tuple-element.68), channel_id=1, source_target_pairs={{0,1},{2,3},{4,5},{6,7},{8,9},{10,11},{12,13},{14,15},{16,17},{18,... | collective-permute-start | bytes 1572872 | tf_op jit(solution)/shard_map/ppermute | solution.py:366
  76.1 2.6 %next_step.7 = (f32[32,8192]{1,0:T(8,128)S(1)}, bf16[32,8192]{1,0:T(8,128)(2,1)S(1)}, bf16[32,8192]{1,0:T(8,128)(2,1)S(1)}, bf16[32,8192]{1,0:T(8,128)(2,1)S(1)}) custom-call(s32[5,64]{1,0:T(8,128)S(1)} %stack.23.idx.refs_0_, f32[32,8192]{1,0:T(8,128)S(1)} %near_part.13.refs_8_.refs_1_, ...), custom_call_target="tpu_custom_call", output_to_operand_aliasing={{0}: (1, {})} | custom-call | tf_op jit(solution)/shard_map/next_step/pallas_call | solution.py:32
  78.8 5.4 %collective-permute-start.14 = (bf16[32,8192]{1,0:T(8,128)(2,1)S(1)}, bf16[32,8192]{1,0:T(8,128)(2,1)S(1)}, u32[]{:S(2)}, u32[]{:S(2)}) collective-permute-start(bf16[32,8192]{1,0:T(8,128)(2,1)S(1)} %get-tuple-element.76), channel_id=1, source_target_pairs={{0,1},{2,3},{4,5},{6,7},{8,9},{10,11},{12,13},{14,15},{16,17},{18,... | collective-permute-start | bytes 1572872 | tf_op jit(solution)/shard_map/ppermute | solution.py:366
  87.5 2.5 %last_step.2 = (f32[32,8192]{1,0:T(8,128)S(1)}, bf16[32,8192]{1,0:T(8,128)(2,1)S(1)}, bf16[32,4096]{1,0:T(8,128)(2,1)S(1)}, bf16[32,4096]{1,0:T(8,128)(2,1)S(1)}, bf16[32,4096]{1,0:T(8,128)(2,1)S(1)}) custom-call(s32[5,64]{1,0:T(8,128)S(1)} %stack.23.idx.refs_0_, f32[32,8192]{1,0:T(8,128)S(1)} %near_part.14.refs_8_.refs_1_, ...), custom_call_target="tpu_custom_call", output_to_operand_aliasing={{0}: (1, {})} | custom-call | tf_op jit(solution)/shard_map/last_step/pallas_call | solution.py:32
  90.0 3.8 %collective-permute-start.16 = (bf16[32,4096]{1,0:T(8,128)(2,1)S(1)}, bf16[32,4096]{1,0:T(8,128)(2,1)S(1)}, u32[]{:S(2)}, u32[]{:S(2)}) collective-permute-start(bf16[32,4096]{1,0:T(8,128)(2,1)S(1)} %get-tuple-element.85), channel_id=1, source_target_pairs={{0,1},{2,3},{4,5},{6,7},{8,9},{10,11},{12,13},{14,15},{16,17},{18,... | collective-permute-start | bytes 786440 | tf_op jit(solution)/shard_map/ppermute | solution.py:366
  94.6 4.0 %collective-permute-done.14.from_even = bf16[32,8192]{1,0:T(8,128)(2,1)S(1)} collective-permute-done((bf16[32,8192]{1,0:T(8,128)(2,1)S(1)}, bf16[32,8192]{1,0:T(8,128)(2,1)S(1)}, u32[]{:S(2)}, u32[]{:S(2)}) %collective-permute-start.14) | collective-permute-done | bytes 524320 | tf_op jit(solution)/shard_map/ppermute | solution.py:366
  98.6 2.5 %last_step.3 = (f32[32,8192]{1,0:T(8,128)S(1)}, bf16[32,8192]{1,0:T(8,128)(2,1)S(1)}, bf16[32,4096]{1,0:T(8,128)(2,1)S(1)}, bf16[32,4096]{1,0:T(8,128)(2,1)S(1)}, bf16[32,4096]{1,0:T(8,128)(2,1)S(1)}) custom-call(s32[5,64]{1,0:T(8,128)S(1)} %stack.23.idx.refs_0_, f32[32,8192]{1,0:T(8,128)S(1)} %near_part.15.refs_8_.near_image, ...), custom_call_target="tpu_custom_call", output_to_operand_aliasing={{0}: (1, {})} | custom-call | tf_op jit(solution)/shard_map/last_step/pallas_call | solution.py:32
  101.1 3.8 %collective-permute-start.17 = (bf16[32,4096]{1,0:T(8,128)(2,1)S(1)}, bf16[32,4096]{1,0:T(8,128)(2,1)S(1)}, u32[]{:S(2)}, u32[]{:S(2)}) collective-permute-start(bf16[32,4096]{1,0:T(8,128)(2,1)S(1)} %get-tuple-element.86), channel_id=1, source_target_pairs={{0,1},{2,3},{4,5},{6,7},{8,9},{10,11},{12,13},{14,15},{16,17},{18,... | collective-permute-start | bytes 786440 | tf_op jit(solution)/shard_map/ppermute | solution.py:366
  105.6 2.7 %local_sums.1 = (f32[64,128]{1,0:T(8,128)S(1)}, bf16[128,8192]{1,0:T(8,128)(2,1)S(1)}) custom-call(s32[5,64]{1,0:T(8,128)S(1)} %stack.23.idx.refs_0_, bf16[64,128,128]{2,1,0:T(8,128)(2,1)S(1)} %get-tuple-element.46.near_m, bf16[32,8192]{1,0:T(8,128)(2,1)S(1)} %get-tuple-element.75.own_a, bf16[32,8192]{1,0:T(8,128)(2,1)S(1)} %get-tuple-element.79.own_b, ...), custom_call_target="tpu_custom_call" | custom-call | tf_op jit(solution)/shard_map/local_sums/pallas_call | solution.py:32
  111.3 5.4 %collective-permute-start.20 = (f32[64,128]{1,0:T(8,128)S(1)}, f32[64,128]{1,0:T(8,128)S(1)}, u32[]{:S(2)}, u32[]{:S(2)}) collective-permute-start(f32[64,128]{1,0:T(8,128)S(1)} %crossing_sums.1), channel_id=1, source_target_pairs={{0,1},{1,0},{2,3},{3,2},{4,5},{5,4},{6,7},{7,6},{8,9},{9,8},{10,11... | collective-permute-start | bytes 98312 | tf_op jit(solution)/shard_map/ppermute | solution.py:428
  116.7 1.9 %collective-permute-done.20 = f32[64,128]{1,0:T(8,128)S(1)} collective-permute-done((f32[64,128]{1,0:T(8,128)S(1)}, f32[64,128]{1,0:T(8,128)S(1)}, u32[]{:S(2)}, u32[]{:S(2)}) %collective-permute-start.20) | collective-permute-done | bytes 32800 | tf_op jit(solution)/shard_map/ppermute | solution.py:428
  118.6 7.6 %collective-permute-start.21 = (f32[64,128]{1,0:T(8,128)S(1)}, f32[64,128]{1,0:T(8,128)S(1)}, u32[]{:S(2)}, u32[]{:S(2)}) collective-permute-start(f32[64,128]{1,0:T(8,128)S(1)} %add.26), channel_id=1, source_target_pairs={{0,2},{1,3},{2,0},{3,1},{4,6},{5,7},{6,4},{7,5},{8,10},{9,11},{10,... | collective-permute-start | bytes 98312 | tf_op jit(solution)/shard_map/ppermute | solution.py:428
  128.0 6.3 %collective-permute-start.22 = (f32[64,128]{1,0:T(8,128)S(1)}, f32[64,128]{1,0:T(8,128)S(1)}, u32[]{:S(2)}, u32[]{:S(2)}) collective-permute-start(f32[64,128]{1,0:T(8,128)S(1)} %add.27), channel_id=1, source_target_pairs={{0,4},{1,5},{2,6},{3,7},{4,0},{5,1},{6,2},{7,3},{8,12},{9,13},{10,... | collective-permute-start | bytes 98312 | tf_op jit(solution)/shard_map/ppermute | solution.py:428
  136.2 9.6 %collective-permute-start.23 = (f32[64,128]{1,0:T(8,128)S(1)}, f32[64,128]{1,0:T(8,128)S(1)}, u32[]{:S(2)}, u32[]{:S(2)}) collective-permute-start(f32[64,128]{1,0:T(8,128)S(1)} %add.28), channel_id=1, source_target_pairs={{0,8},{1,9},{2,10},{3,11},{4,12},{5,13},{6,14},{7,15},{8,0},{9,1},... | collective-permute-start | bytes 98312 | tf_op jit(solution)/shard_map/ppermute | solution.py:428
  150.0 2.8 %collective-permute-done.25 = f32[64,128]{1,0:T(8,128)S(1)} collective-permute-done((f32[64,128]{1,0:T(8,128)S(1)}, f32[64,128]{1,0:T(8,128)S(1)}, u32[]{:S(2)}, u32[]{:S(2)}) %collective-permute-start.25) | collective-permute-done | bytes 32800 | tf_op jit(solution)/shard_map/ppermute | solution.py:428
  152.8 2.7 %collective-permute-start.26 = (f32[64,128]{1,0:T(8,128)S(1)}, f32[64,128]{1,0:T(8,128)S(1)}, u32[]{:S(2)}, u32[]{:S(2)}) collective-permute-start(f32[64,128]{1,0:T(8,128)S(1)} %add.31), channel_id=1, source_target_pairs={{0,64},{1,65},{2,66},{3,67},{4,68},{5,69},{6,70},{7,71},{8,72},{9,... | collective-permute-start | bytes 98312 | tf_op jit(solution)/shard_map/ppermute | solution.py:428
  155.5 2.7 %collective-permute-done.26 = f32[64,128]{1,0:T(8,128)S(1)} collective-permute-done((f32[64,128]{1,0:T(8,128)S(1)}, f32[64,128]{1,0:T(8,128)S(1)}, u32[]{:S(2)}, u32[]{:S(2)}) %collective-permute-start.26) | collective-permute-done | bytes 32800 | tf_op jit(solution)/shard_map/ppermute | solution.py:428
  158.2 3.9 %finish.1 = (f32[64,8192]{1,0:T(8,128)}, f32[64,64]{1,0:T(8,128)}) custom-call(f32[64,128]{1,0:T(8,128)S(1)} %add.32.sums, bf16[128,8192]{1,0:T(8,128)(2,1)S(1)} %get-tuple-element.89.stack), custom_call_target="tpu_custom_call" | custom-call | tf_op jit(solution)/shard_map/finish/pallas_call | solution.py:32
  (62 shorter events, 38.2 us)
Async XLA Ops:
  2.7 1.6 copy-start
  4.3 1.2 copy-start.2
  5.6 9.4 %copy-start.1 = (bf16[64,128,128]{2,1,0:T(8,128)(2,1)S(1)}, bf16[64,128,128]{2,1,0:T(8,128)(2,1)}, u32[]{:S(2)}) copy-start(bf16[64,128,128]{2,1,0:T(8,128)(2,1)} %cross.3) | copy-start | bytes 6291460
  5.6 9.4 %copy-start.3 = (bf16[64,128,128]{2,1,0:T(8,128)(2,1)S(1)}, bf16[64,128,128]{2,1,0:T(8,128)(2,1)}, u32[]{:S(2)}) copy-start(bf16[64,128,128]{2,1,0:T(8,128)(2,1)} %near.1) | copy-start | bytes 6291460
  7.6 14.9 %collective-permute-start = (bf16[32,8192]{1,0:T(8,128)(2,1)S(1)}, bf16[32,8192]{1,0:T(8,128)(2,1)S(1)}, u32[]{:S(2)}, u32[]{:S(2)}) collective-permute-start(bf16[32,8192]{1,0:T(8,128)(2,1)S(1)} %get-tuple-element.50), channel_id=1, source_target_pairs={{0,1},{2,3},{4,5},{6,7},{8,9},{10,11},{12,13},{14,15},{16,17},{18,... | collective-permute-start | bytes 1572872 | tf_op jit(solution)/shard_map/ppermute | solution.py:366
  9.4 13.1 %collective-permute-start.1 = (bf16[32,8192]{1,0:T(8,128)(2,1)S(1)}, bf16[32,8192]{1,0:T(8,128)(2,1)S(1)}, u32[]{:S(2)}, u32[]{:S(2)}) collective-permute-start(bf16[32,8192]{1,0:T(8,128)(2,1)S(1)} %get-tuple-element.51), channel_id=1, source_target_pairs={{1,2},{3,4},{5,6},{7,8},{9,10},{11,12},{13,14},{15,16},{17,18},{19... | collective-permute-start | bytes 1572872 | tf_op jit(solution)/shard_map/ppermute | solution.py:366
  10.1 24.0 %collective-permute-start.4 = (bf16[32,8192]{1,0:T(8,128)(2,1)S(1)}, bf16[32,8192]{1,0:T(8,128)(2,1)S(1)}, u32[]{:S(2)}, u32[]{:S(2)}) collective-permute-start(bf16[32,8192]{1,0:T(8,128)(2,1)S(1)} %get-tuple-element.56), channel_id=1, source_target_pairs={{0,1},{2,3},{4,5},{6,7},{8,9},{10,11},{12,13},{14,15},{16,17},{18,... | collective-permute-start | bytes 1572872 | tf_op jit(solution)/shard_map/ppermute | solution.py:366
  14.2 19.9 %collective-permute-start.5 = (bf16[32,8192]{1,0:T(8,128)(2,1)S(1)}, bf16[32,8192]{1,0:T(8,128)(2,1)S(1)}, u32[]{:S(2)}, u32[]{:S(2)}) collective-permute-start(bf16[32,8192]{1,0:T(8,128)(2,1)S(1)} %get-tuple-element.57), channel_id=1, source_target_pairs={{1,2},{3,4},{5,6},{7,8},{9,10},{11,12},{13,14},{15,16},{17,18},{19... | collective-permute-start | bytes 1572872 | tf_op jit(solution)/shard_map/ppermute | solution.py:366
  25.1 20.4 %collective-permute-start.2 = (bf16[32,8192]{1,0:T(8,128)(2,1)S(1)}, bf16[32,8192]{1,0:T(8,128)(2,1)S(1)}, u32[]{:S(2)}, u32[]{:S(2)}) collective-permute-start(bf16[32,8192]{1,0:T(8,128)(2,1)S(1)} %get-tuple-element.53), channel_id=1, source_target_pairs={{0,1},{2,3},{4,5},{6,7},{8,9},{10,11},{12,13},{14,15},{16,17},{18,... | collective-permute-start | bytes 1572872 | tf_op jit(solution)/shard_map/ppermute | solution.py:366
  29.6 15.9 %collective-permute-start.3 = (bf16[32,8192]{1,0:T(8,128)(2,1)S(1)}, bf16[32,8192]{1,0:T(8,128)(2,1)S(1)}, u32[]{:S(2)}, u32[]{:S(2)}) collective-permute-start(bf16[32,8192]{1,0:T(8,128)(2,1)S(1)} %get-tuple-element.54), channel_id=1, source_target_pairs={{1,2},{3,4},{5,6},{7,8},{9,10},{11,12},{13,14},{15,16},{17,18},{19... | collective-permute-start | bytes 1572872 | tf_op jit(solution)/shard_map/ppermute | solution.py:366
  36.7 18.1 %collective-permute-start.8 = (bf16[32,8192]{1,0:T(8,128)(2,1)S(1)}, bf16[32,8192]{1,0:T(8,128)(2,1)S(1)}, u32[]{:S(2)}, u32[]{:S(2)}) collective-permute-start(bf16[32,8192]{1,0:T(8,128)(2,1)S(1)} %get-tuple-element.63), channel_id=1, source_target_pairs={{0,1},{2,3},{4,5},{6,7},{8,9},{10,11},{12,13},{14,15},{16,17},{18,... | collective-permute-start | bytes 1572872 | tf_op jit(solution)/shard_map/ppermute | solution.py:366
  42.9 12.0 %collective-permute-start.9 = (bf16[32,8192]{1,0:T(8,128)(2,1)S(1)}, bf16[32,8192]{1,0:T(8,128)(2,1)S(1)}, u32[]{:S(2)}, u32[]{:S(2)}) collective-permute-start(bf16[32,8192]{1,0:T(8,128)(2,1)S(1)} %get-tuple-element.64), channel_id=1, source_target_pairs={{1,2},{3,4},{5,6},{7,8},{9,10},{11,12},{13,14},{15,16},{17,18},{19... | collective-permute-start | bytes 1572872 | tf_op jit(solution)/shard_map/ppermute | solution.py:366
  48.1 16.8 %collective-permute-start.6 = (bf16[32,8192]{1,0:T(8,128)(2,1)S(1)}, bf16[32,8192]{1,0:T(8,128)(2,1)S(1)}, u32[]{:S(2)}, u32[]{:S(2)}) collective-permute-start(bf16[32,8192]{1,0:T(8,128)(2,1)S(1)} %get-tuple-element.60), channel_id=1, source_target_pairs={{0,1},{2,3},{4,5},{6,7},{8,9},{10,11},{12,13},{14,15},{16,17},{18,... | collective-permute-start | bytes 1572872 | tf_op jit(solution)/shard_map/ppermute | solution.py:366
  52.2 12.7 %collective-permute-start.7 = (bf16[32,8192]{1,0:T(8,128)(2,1)S(1)}, bf16[32,8192]{1,0:T(8,128)(2,1)S(1)}, u32[]{:S(2)}, u32[]{:S(2)}) collective-permute-start(bf16[32,8192]{1,0:T(8,128)(2,1)S(1)} %get-tuple-element.61), channel_id=1, source_target_pairs={{1,2},{3,4},{5,6},{7,8},{9,10},{11,12},{13,14},{15,16},{17,18},{19... | collective-permute-start | bytes 1572872 | tf_op jit(solution)/shard_map/ppermute | solution.py:366
  57.5 18.6 %collective-permute-start.12 = (bf16[32,8192]{1,0:T(8,128)(2,1)S(1)}, bf16[32,8192]{1,0:T(8,128)(2,1)S(1)}, u32[]{:S(2)}, u32[]{:S(2)}) collective-permute-start(bf16[32,8192]{1,0:T(8,128)(2,1)S(1)} %get-tuple-element.71), channel_id=1, source_target_pairs={{0,1},{2,3},{4,5},{6,7},{8,9},{10,11},{12,13},{14,15},{16,17},{18,... | collective-permute-start | bytes 1572872 | tf_op jit(solution)/shard_map/ppermute | solution.py:366
  62.1 14.0 %collective-permute-start.13 = (bf16[32,8192]{1,0:T(8,128)(2,1)S(1)}, bf16[32,8192]{1,0:T(8,128)(2,1)S(1)}, u32[]{:S(2)}, u32[]{:S(2)}) collective-permute-start(bf16[32,8192]{1,0:T(8,128)(2,1)S(1)} %get-tuple-element.72), channel_id=1, source_target_pairs={{1,2},{3,4},{5,6},{7,8},{9,10},{11,12},{13,14},{15,16},{17,18},{19... | collective-permute-start | bytes 1572872 | tf_op jit(solution)/shard_map/ppermute | solution.py:366
  69.4 18.1 %collective-permute-start.10 = (bf16[32,8192]{1,0:T(8,128)(2,1)S(1)}, bf16[32,8192]{1,0:T(8,128)(2,1)S(1)}, u32[]{:S(2)}, u32[]{:S(2)}) collective-permute-start(bf16[32,8192]{1,0:T(8,128)(2,1)S(1)} %get-tuple-element.68), channel_id=1, source_target_pairs={{0,1},{2,3},{4,5},{6,7},{8,9},{10,11},{12,13},{14,15},{16,17},{18,... | collective-permute-start | bytes 1572872 | tf_op jit(solution)/shard_map/ppermute | solution.py:366
  74.8 12.7 %collective-permute-start.11 = (bf16[32,8192]{1,0:T(8,128)(2,1)S(1)}, bf16[32,8192]{1,0:T(8,128)(2,1)S(1)}, u32[]{:S(2)}, u32[]{:S(2)}) collective-permute-start(bf16[32,8192]{1,0:T(8,128)(2,1)S(1)} %get-tuple-element.69), channel_id=1, source_target_pairs={{1,2},{3,4},{5,6},{7,8},{9,10},{11,12},{13,14},{15,16},{17,18},{19... | collective-permute-start | bytes 1572872 | tf_op jit(solution)/shard_map/ppermute | solution.py:366
  78.8 19.8 %collective-permute-start.14 = (bf16[32,8192]{1,0:T(8,128)(2,1)S(1)}, bf16[32,8192]{1,0:T(8,128)(2,1)S(1)}, u32[]{:S(2)}, u32[]{:S(2)}) collective-permute-start(bf16[32,8192]{1,0:T(8,128)(2,1)S(1)} %get-tuple-element.76), channel_id=1, source_target_pairs={{0,1},{2,3},{4,5},{6,7},{8,9},{10,11},{12,13},{14,15},{16,17},{18,... | collective-permute-start | bytes 1572872 | tf_op jit(solution)/shard_map/ppermute | solution.py:366
  84.1 14.4 %collective-permute-start.15 = (bf16[32,8192]{1,0:T(8,128)(2,1)S(1)}, bf16[32,8192]{1,0:T(8,128)(2,1)S(1)}, u32[]{:S(2)}, u32[]{:S(2)}) collective-permute-start(bf16[32,8192]{1,0:T(8,128)(2,1)S(1)} %get-tuple-element.77), channel_id=1, source_target_pairs={{1,2},{3,4},{5,6},{7,8},{9,10},{11,12},{13,14},{15,16},{17,18},{19... | collective-permute-start | bytes 1572872 | tf_op jit(solution)/shard_map/ppermute | solution.py:366
  90.0 18.3 %collective-permute-start.16 = (bf16[32,4096]{1,0:T(8,128)(2,1)S(1)}, bf16[32,4096]{1,0:T(8,128)(2,1)S(1)}, u32[]{:S(2)}, u32[]{:S(2)}) collective-permute-start(bf16[32,4096]{1,0:T(8,128)(2,1)S(1)} %get-tuple-element.85), channel_id=1, source_target_pairs={{0,1},{2,3},{4,5},{6,7},{8,9},{10,11},{12,13},{14,15},{16,17},{18,... | collective-permute-start | bytes 786440 | tf_op jit(solution)/shard_map/ppermute | solution.py:366
  93.9 14.4 %collective-permute-start.18 = (bf16[32,4096]{1,0:T(8,128)(2,1)S(1)}, bf16[32,4096]{1,0:T(8,128)(2,1)S(1)}, u32[]{:S(2)}, u32[]{:S(2)}) collective-permute-start(bf16[32,4096]{1,0:T(8,128)(2,1)S(1)} %get-tuple-element.87), channel_id=1, source_target_pairs={{1,2},{3,4},{5,6},{7,8},{9,10},{11,12},{13,14},{15,16},{17,18},{19... | collective-permute-start | bytes 786440 | tf_op jit(solution)/shard_map/ppermute | solution.py:366
  101.1 8.9 %collective-permute-start.17 = (bf16[32,4096]{1,0:T(8,128)(2,1)S(1)}, bf16[32,4096]{1,0:T(8,128)(2,1)S(1)}, u32[]{:S(2)}, u32[]{:S(2)}) collective-permute-start(bf16[32,4096]{1,0:T(8,128)(2,1)S(1)} %get-tuple-element.86), channel_id=1, source_target_pairs={{0,1},{2,3},{4,5},{6,7},{8,9},{10,11},{12,13},{14,15},{16,17},{18,... | collective-permute-start | bytes 786440 | tf_op jit(solution)/shard_map/ppermute | solution.py:366
  104.9 5.1 %collective-permute-start.19 = (bf16[32,4096]{1,0:T(8,128)(2,1)S(1)}, bf16[32,4096]{1,0:T(8,128)(2,1)S(1)}, u32[]{:S(2)}, u32[]{:S(2)}) collective-permute-start(bf16[32,4096]{1,0:T(8,128)(2,1)S(1)} %get-tuple-element.88), channel_id=1, source_target_pairs={{1,2},{3,4},{5,6},{7,8},{9,10},{11,12},{13,14},{15,16},{17,18},{19... | collective-permute-start | bytes 786440 | tf_op jit(solution)/shard_map/ppermute | solution.py:366
  111.3 7.3 %collective-permute-start.20 = (f32[64,128]{1,0:T(8,128)S(1)}, f32[64,128]{1,0:T(8,128)S(1)}, u32[]{:S(2)}, u32[]{:S(2)}) collective-permute-start(f32[64,128]{1,0:T(8,128)S(1)} %crossing_sums.1), channel_id=1, source_target_pairs={{0,1},{1,0},{2,3},{3,2},{4,5},{5,4},{6,7},{7,6},{8,9},{9,8},{10,11... | collective-permute-start | bytes 98312 | tf_op jit(solution)/shard_map/ppermute | solution.py:428
  118.6 9.5 %collective-permute-start.21 = (f32[64,128]{1,0:T(8,128)S(1)}, f32[64,128]{1,0:T(8,128)S(1)}, u32[]{:S(2)}, u32[]{:S(2)}) collective-permute-start(f32[64,128]{1,0:T(8,128)S(1)} %add.26), channel_id=1, source_target_pairs={{0,2},{1,3},{2,0},{3,1},{4,6},{5,7},{6,4},{7,5},{8,10},{9,11},{10,... | collective-permute-start | bytes 98312 | tf_op jit(solution)/shard_map/ppermute | solution.py:428
  128.0 8.2 %collective-permute-start.22 = (f32[64,128]{1,0:T(8,128)S(1)}, f32[64,128]{1,0:T(8,128)S(1)}, u32[]{:S(2)}, u32[]{:S(2)}) collective-permute-start(f32[64,128]{1,0:T(8,128)S(1)} %add.27), channel_id=1, source_target_pairs={{0,4},{1,5},{2,6},{3,7},{4,0},{5,1},{6,2},{7,3},{8,12},{9,13},{10,... | collective-permute-start | bytes 98312 | tf_op jit(solution)/shard_map/ppermute | solution.py:428
  136.2 11.5 %collective-permute-start.23 = (f32[64,128]{1,0:T(8,128)S(1)}, f32[64,128]{1,0:T(8,128)S(1)}, u32[]{:S(2)}, u32[]{:S(2)}) collective-permute-start(f32[64,128]{1,0:T(8,128)S(1)} %add.28), channel_id=1, source_target_pairs={{0,8},{1,9},{2,10},{3,11},{4,12},{5,13},{6,14},{7,15},{8,0},{9,1},... | collective-permute-start | bytes 98312 | tf_op jit(solution)/shard_map/ppermute | solution.py:428
  147.7 1.2 collective-permute-start.24
  148.9 3.9 %collective-permute-start.25 = (f32[64,128]{1,0:T(8,128)S(1)}, f32[64,128]{1,0:T(8,128)S(1)}, u32[]{:S(2)}, u32[]{:S(2)}) collective-permute-start(f32[64,128]{1,0:T(8,128)S(1)} %add.30), channel_id=1, source_target_pairs={{0,32},{1,33},{2,34},{3,35},{4,36},{5,37},{6,38},{7,39},{8,40},{9,... | collective-permute-start | bytes 98312 | tf_op jit(solution)/shard_map/ppermute | solution.py:428
  152.8 5.4 %collective-permute-start.26 = (f32[64,128]{1,0:T(8,128)S(1)}, f32[64,128]{1,0:T(8,128)S(1)}, u32[]{:S(2)}, u32[]{:S(2)}) collective-permute-start(f32[64,128]{1,0:T(8,128)S(1)} %add.31), channel_id=1, source_target_pairs={{0,64},{1,65},{2,66},{3,67},{4,68},{5,69},{6,70},{7,71},{8,72},{9,... | collective-permute-start | bytes 98312 | tf_op jit(solution)/shard_map/ppermute | solution.py:428
